TPU v7x, 32 devices: a whole 2x2x4 slice. The times are simulated.
32 devices in a mesh: dp: 2 (over core), zero: 16 (over z, y, x).
Axes of the slice: x: 2, y: 2, z: 4, core: 2. Of those that a mesh axis runs over, the one named last changes fastest.
Arguments:
- tokens: bfloat16 [32768, 768], P(('dp', 'zero')), may hold values from -6 to 6
- out_grad: bfloat16 [32768, 768], P(('dp', 'zero')), may hold values from -6 to 6
- mask_pos: int32 [256, 32], P(('dp', 'zero')), may hold values from -1 to 127, as said below
- repl_id: int32 [256, 32], P(('dp', 'zero')), may hold values from 0 to 4095
- replace_embed: bfloat16 [4096, 768], replicated, may hold values from -6 to 6
- masters: float32 [16, 768, 768], P(None, 'zero'), as said below
- norm_params: float32 [4, 768], P(None, 'zero'), as said below
- first_moment: float32 [16, 768, 768], P(None, 'zero')
- second_moment: float32 [16, 768, 768], P(None, 'zero'), as said below
- left_basis: float32 [16, 768, 768], P(None, 'zero'), as said below
- right_basis: float32 [16, 768, 768], P(None, 'zero'), as said below
- norm_first: float32 [4, 768], P(None, 'zero')
- norm_second: float32 [4, 768], P(None, 'zero'), as said below
- step: int32 [1], replicated, may hold values from 1 to 20
Outputs:
- layer_out: bfloat16 [32768, 768], P(('dp', 'zero'))
- in_grad: float32 [32768, 768], P(('dp', 'zero'))
- new_first: float32 [16, 768, 768], P(None, 'zero')
- new_second: float32 [16, 768, 768], P(None, 'zero')
- new_master: float32 [16, 768, 768], P(None, 'zero')
- new_copy: bfloat16 [16, 768, 768], P(None, 'zero')
- new_norm_first: float32 [4, 768], P(None, 'zero')
- new_norm_second: float32 [4, 768], P(None, 'zero')
- new_norms: float32 [4, 768], P(None, 'zero')
Inputs may be any that keep to these rules, and one draw needn't show every extreme that they name: `mask_pos`: in each sequence the entries other than -1 are distinct positions and stand in the first slots; a sequence has 1 to 32 of them. `masters`: tiles 0 to 2, the gate and up tiles, tile 3 and the down tiles have entries of deviation about 768^-0.5, (4/768)^0.5, and (2/3072)^0.5. `norm_params`: rows 0 and 2 are gains within 0.7 to 1.3; rows 1 and 3 are shifts. `second_moment`: every entry is positive. `left_basis`: each tile's basis is orthogonal. `right_basis`: each tile's basis is orthogonal. `norm_second`: every entry is positive.
All inputs are finite; a program needn't handle non-finite values.
Results may differ from a plain program's by a relative error of at most 0.0075.
The roundings to bfloat16 on the way count: a program that leaves them out, or rounds other values in their place, can miss the bound.
Values may be sent and summed in bfloat16 or wider, within the bound.
A program may use at most 256 MiB of HBM per device.

v0:
```python
import math

import jax
import jax.numpy as jnp
import numpy as np
from jax import lax
from jax.sharding import PartitionSpec as P

HEADS = 12
CAP = 1


highest = lax.Precision.HIGHEST
norm_eps = 1e-12
beta_one = 0.9
beta_two = 0.95
adam_eps = 1e-08
peak_rate = 0.1
warm_steps = 5.0
total_steps = 60.0
decay_rate = 0.01


def alibi_slopes(head_count):

    def power_slopes(power_count):
        first_slope = 2.0 ** (-8.0 / power_count)
        return [first_slope ** (position + 1) for position in range(power_count)]

    nearest = 2 ** int(math.floor(math.log2(head_count)))
    slope_list = power_slopes(nearest)
    slope_list = slope_list + power_slopes(2 * nearest)[0::2][: head_count - nearest]
    return np.array(slope_list, np.float32)


def layer_norm(values, gain_row, shift_row):
    row_mean = jnp.mean(values, axis=-1, keepdims=True)
    centered = values - row_mean
    spread = jnp.mean(centered * centered, axis=-1, keepdims=True)
    return centered * lax.rsqrt(spread + norm_eps) * gain_row + shift_row


def gated(gate_val, up_value):
    return jax.nn.gelu(gate_val, approximate=False) * up_value


def shards(
    tokens,
    out_grad,
    mask_pos,
    repl_id,
    replace_embed,
    masters,
    norm_params,
    first_moment,
    second_moment,
    left_basis,
    right_basis,
    norm_first,
    norm_second,
    step,
):
    seq_count = mask_pos.shape[0]
    tok_rows, model_width = tokens.shape
    length = tok_rows // seq_count
    head_count = HEADS
    head_size = model_width // head_count
    score_scale = float(head_size) ** (-0.5)
    tile_count = masters.shape[0]
    ff_parts = (tile_count - 4) // 3
    shard_rows = masters.shape[1]
    positions = jnp.arange(length, dtype=jnp.int32)
    mask_hits = mask_pos[:, :, None] == positions[None, None, :]
    masked = jnp.any(mask_hits, axis=1).reshape(-1, 1)
    row_ids = jnp.sum(jnp.where(mask_hits, repl_id[:, :, None], 0), axis=1).reshape(-1)
    inputs = jnp.where(masked, jnp.take(replace_embed, row_ids, axis=0), tokens)
    shard_low = masters.astype(jnp.bfloat16)
    whole_tiles, norm_whole = (
        lax.all_gather(shard_low, "zero", axis=1, tiled=True),
        lax.all_gather(norm_params.astype(jnp.bfloat16), "zero", axis=1, tiled=True),
    )
    norm_gains = norm_whole.astype(jnp.float32)
    slopes = jnp.asarray(alibi_slopes(head_count))
    distance = jnp.abs(positions[:, None] - positions[None, :]).astype(jnp.float32)
    alibi_bias = -slopes[:, None, None] * distance[None]
    head_shape = (seq_count, length, head_count, head_size)
    qkv_low = jnp.einsum(
        "td,kde->kte", inputs, whole_tiles[0:3], preferred_element_type=jnp.float32
    ).astype(jnp.bfloat16)
    queries = qkv_low[0].reshape(head_shape)
    key_rows = qkv_low[1].reshape(head_shape)
    values = qkv_low[2].reshape(head_shape)

    def score_block():
        raw_scores = jnp.einsum(
            "bqhd,bkhd->bhqk", queries, key_rows, preferred_element_type=jnp.float32
        )
        return raw_scores * score_scale + alibi_bias[None]

    scores = score_block()
    row_max = jnp.max(scores, axis=-1, keepdims=True)
    log_total = row_max + jnp.log(jnp.sum(jnp.exp(scores - row_max), axis=-1, keepdims=True))
    soft_low = jnp.exp(scores - log_total).astype(jnp.bfloat16)
    mixed_low = jnp.einsum("bhqk,bkhd->bqhd", soft_low, values, preferred_element_type=jnp.float32)
    mixed_low = mixed_low.reshape(tok_rows, model_width).astype(jnp.bfloat16)
    attended = jnp.dot(mixed_low, whole_tiles[3], preferred_element_type=jnp.float32)
    first_sum = inputs.astype(jnp.float32) + attended
    hidden, first_back = jax.vjp(layer_norm, first_sum, norm_gains[0], norm_gains[1])
    hidden_low = hidden.astype(jnp.bfloat16)
    gate_up = jnp.einsum(
        "td,fde->tfe",
        hidden_low,
        whole_tiles[4 : 4 + 2 * ff_parts],
        preferred_element_type=jnp.float32,
    )
    gate_val = gate_up[:, :ff_parts].reshape(tok_rows, ff_parts * model_width)
    up_value = gate_up[:, ff_parts:].reshape(tok_rows, ff_parts * model_width)
    inner_act, inner_back = jax.vjp(gated, gate_val, up_value)
    inner_low = inner_act.astype(jnp.bfloat16).reshape(tok_rows, ff_parts, model_width)
    branch = jnp.einsum(
        "tfe,fed->td",
        inner_low,
        whole_tiles[4 + 2 * ff_parts :],
        preferred_element_type=jnp.float32,
    )
    layer_out, second_back = jax.vjp(layer_norm, hidden + branch, norm_gains[2], norm_gains[3])
    back_tiles = lax.all_gather(shard_low, "zero", axis=1, tiled=True)
    d_second, d_gain_two, d_shift_two = second_back(out_grad.astype(jnp.float32))
    d_branch = d_second.astype(jnp.bfloat16)
    grad_down = jnp.einsum("tfe,td->fed", inner_low, d_branch, preferred_element_type=jnp.float32)
    d_inner = jnp.einsum(
        "td,fed->tfe", d_branch, back_tiles[4 + 2 * ff_parts :], preferred_element_type=jnp.float32
    )
    d_gate, d_up = inner_back(d_inner.reshape(tok_rows, ff_parts * model_width))
    d_gate_up = jnp.concatenate(
        [
            d_gate.reshape(tok_rows, ff_parts, model_width),
            d_up.reshape(tok_rows, ff_parts, model_width),
        ],
        axis=1,
    ).astype(jnp.bfloat16)
    grad_gate_up = jnp.einsum(
        "td,tfe->fde", hidden_low, d_gate_up, preferred_element_type=jnp.float32
    )
    d_hidden = d_second + jnp.einsum(
        "tfe,fde->td",
        d_gate_up,
        back_tiles[4 : 4 + 2 * ff_parts],
        preferred_element_type=jnp.float32,
    )
    d_first, d_gain_one, d_shift_one = first_back(d_hidden)
    d_attended = d_first.astype(jnp.bfloat16)
    grad_out = jnp.einsum("td,te->de", mixed_low, d_attended, preferred_element_type=jnp.float32)
    d_mixed = jnp.einsum("te,de->td", d_attended, back_tiles[3], preferred_element_type=jnp.float32)
    d_mixed = d_mixed.astype(jnp.bfloat16).reshape(head_shape)
    again_probs = jnp.exp(score_block() - log_total)
    again_low = again_probs.astype(jnp.bfloat16)
    d_probs = jnp.einsum("bqhd,bkhd->bhqk", d_mixed, values, preferred_element_type=jnp.float32)
    row_delta = jnp.sum(again_probs * d_probs, axis=-1, keepdims=True)
    d_scores = (again_probs * (d_probs - row_delta)).astype(jnp.bfloat16)
    d_query = (
        jnp.einsum("bhqk,bkhd->bqhd", d_scores, key_rows, preferred_element_type=jnp.float32)
        * score_scale
    )
    d_keys = (
        jnp.einsum("bhqk,bqhd->bkhd", d_scores, queries, preferred_element_type=jnp.float32)
        * score_scale
    )
    d_values = jnp.einsum("bhqk,bqhd->bkhd", again_low, d_mixed, preferred_element_type=jnp.float32)
    d_qkv = (
        jnp.stack([d_query, d_keys, d_values])
        .reshape(3, tok_rows, model_width)
        .astype(jnp.bfloat16)
    )
    grad_qkv = jnp.einsum("td,kte->kde", inputs, d_qkv, preferred_element_type=jnp.float32)
    d_inputs = d_first + jnp.einsum(
        "kte,kde->td", d_qkv, back_tiles[0:3], preferred_element_type=jnp.float32
    )
    in_grad = jnp.where(masked, 0.0, d_inputs)
    tile_grads = jnp.concatenate([grad_qkv, grad_out[None], grad_gate_up, grad_down], axis=0)
    norm_grads = jnp.stack([d_gain_one, d_shift_one, d_gain_two, d_shift_two])
    step_value = step[0].astype(jnp.float32)
    step_rate = peak_rate * jnp.minimum(
        step_value / warm_steps, (total_steps - step_value) / (total_steps - warm_steps)
    )
    fix_one = 1.0 - jnp.power(beta_one, step_value)
    fix_two = 1.0 - jnp.power(beta_two, step_value)
    devices = lax.axis_size("zero")
    capacity = CAP
    target = jnp.arange(tile_count, dtype=jnp.int32)
    slot_index = jnp.arange(devices * capacity, dtype=jnp.int32)
    source = jnp.where(slot_index < tile_count, slot_index, 0)

    def outgoing(source_array):
        return jnp.take(source_array, source, axis=0).reshape(
            devices, capacity, shard_rows, model_width
        )

    tile_sum, norm_sum = (
        lax.psum_scatter(tile_grads, "zero", scatter_dimension=1, tiled=True),
        lax.psum_scatter(norm_grads, "zero", scatter_dimension=1, tiled=True),
    )
    tile_sum, norm_sum = lax.psum((tile_sum, norm_sum), "dp")
    left_whole = lax.all_to_all(
        outgoing(left_basis), "zero", split_axis=0, concat_axis=2, tiled=True
    )
    right_whole = lax.all_to_all(
        outgoing(right_basis), "zero", split_axis=0, concat_axis=2, tiled=True
    )
    rotated = jnp.einsum(
        "akji,akjl->akil",
        left_whole,
        lax.all_to_all(outgoing(tile_sum), "zero", split_axis=0, concat_axis=2, tiled=True),
        precision=highest,
    )
    rotated = jnp.einsum("akil,aklm->akim", rotated, right_whole, precision=highest)
    moment_one = (
        beta_one
        * lax.all_to_all(outgoing(first_moment), "zero", split_axis=0, concat_axis=2, tiled=True)
        + (1.0 - beta_one) * rotated
    )
    moment_two = (
        beta_two
        * lax.all_to_all(outgoing(second_moment), "zero", split_axis=0, concat_axis=2, tiled=True)
        + (1.0 - beta_two) * rotated * rotated
    )
    direction = moment_one / fix_one / (jnp.sqrt(moment_two / fix_two) + adam_eps)
    update = jnp.einsum("akij,akjl->akil", left_whole, direction, precision=highest)
    update = jnp.einsum("akil,akml->akim", update, right_whole, precision=highest)
    results = jnp.stack([moment_one, moment_two, update], axis=2)
    returned = lax.all_to_all(results, "zero", split_axis=3, concat_axis=0, tiled=True)
    returned = returned.reshape(devices * capacity, 3, shard_rows, model_width)
    owned_back = jnp.take(returned, target, axis=0)
    new_master = masters - step_rate * (owned_back[:, 2] + decay_rate * masters)
    new_norm_first = beta_one * norm_first + (1.0 - beta_one) * norm_sum
    new_norm_second = beta_two * norm_second + (1.0 - beta_two) * norm_sum * norm_sum
    new_norms = norm_params - step_rate * (new_norm_first / fix_one) / (
        jnp.sqrt(new_norm_second / fix_two) + adam_eps
    )
    return (
        layer_out.astype(jnp.bfloat16),
        in_grad,
        owned_back[:, 0],
        owned_back[:, 1],
        new_master,
        new_master.astype(jnp.bfloat16),
        new_norm_first,
        new_norm_second,
        new_norms,
    )


def solution(mesh):
    in_specs = (
        P(("dp", "zero"), None),
        P(("dp", "zero"), None),
        P(("dp", "zero"), None),
        P(("dp", "zero"), None),
        P(),
        P(None, "zero", None),
        P(None, "zero"),
        P(None, "zero", None),
        P(None, "zero", None),
        P(None, "zero", None),
        P(None, "zero", None),
        P(None, "zero"),
        P(None, "zero"),
        P(),
    )
    out_specs = (
        P(("dp", "zero"), None),
        P(("dp", "zero"), None),
        P(None, "zero", None),
        P(None, "zero", None),
        P(None, "zero", None),
        P(None, "zero", None),
        P(None, "zero"),
        P(None, "zero"),
        P(None, "zero"),
    )
    return jax.shard_map(shards, mesh=mesh, in_specs=in_specs, out_specs=out_specs, check_vma=False)
```

profile of v0, /device:TPU:0, one launch (start us, length us, event | category | flops | bytes accessed | tf_op | source)
XLA Modules:
  0.0 1709.2 jit_solution(17990816463985661530)
XLA Ops:
  15.6 9.2 gather_fusion
  27.4 43.7 %all-gather = bf16[16,48,4]{1,2,0:T(4,128)(2,1)S(1)} all-gather(bf16[1,48,4]{1,2,0:T(4,128)(2,1)S(1)} %convert_bitcast_fusion.1), channel_id=1, replica_groups=mesh['dp'=2,'zero'=16] {'zero'}, dimensions={0}, use_global_device_ids=true | all-gather | bytes 6528 | tf_op jit(solution)/shard_map/all_gather | solution.py:80
  74.8 150.4 %all-gather.3.cloned.1.call-done = bf16[16,768,768]{2,1,0:T(8,128)(2,1)} async-done(((bf16[16,48,768]{2,1,0:T(8,128)(2,1)}), bf16[16,768,768]{2,1,0:T(8,128)(2,1)}) %all-gather.3.cloned.1.call-update) | async-done | bytes 18874384 | tf_op jit(solution)/shard_map/all_gather | solution.py:79
  260.6 19.5 %fusion.9 = f32[1024,8,768]{2,0,1:T(8,128)} fusion(bf16[16,768,768]{2,1,0:T(8,128)(2,1)} %all-gather.3.cloned.1.call-done, f32[1024,768]{0,1:T(8,128)S(1)} %get-tuple-element.114, f32[768]{0:T(1024)S(1)} %get-tuple-element.83, f32[768]{0:T(1024)S(1)} %get-tuple-element.84, f32[1024]{0:T(1024)S(1)} %fusion.81, f32[1024]{0:T(1024)S(1)} %broadcast_multiply_fusion.4), kind=kOutput, calls=%fused_computation.31 | convolution fusion | flops 9667608576 | bytes 37763072 | tf_op jit(solution)/shard_map/td,fde->tfe/dot_general | solution.py:110
  280.1 29.9 %multiply_convert_fusion.1 = (bf16[1024,4,768]{2,0,1:T(8,128)(2,1)S(1)}, f32[1024,4,768]{2,0,1:T(8,128)}) fusion(f32[1024,8,768]{2,0,1:T(8,128)} %fusion.9), kind=kLoop, calls=%fused_computation.13 | loop fusion | flops 207618048 | bytes 44040192 | tf_op jit(solution)/shard_map/convert_element_type | solution.py:119
  310.1 9.3 fusion.101
  323.9 24.6 %add_convert_fusion = (bf16[1024,4,768]{2,0,1:T(8,128)(2,1)}, bf16[1024,4,768]{2,0,1:T(8,128)(2,1)}) fusion(f32[1024,4,768]{2,0,1:T(8,128)} %get-tuple-element.93, f32[1024,8,768]{2,0,1:T(8,128)} %fusion.9, bf16[16,768,768]{2,1,0:T(8,128)(2,1)} %all-gather.3.cloned.1.call-done, f32[1024]{0:T(1024)S(1)} %negate_multiply_fusion.2, ...), kind=kOutput, calls=%fused_computation.12 | convolution fusion | flops 4895539200 | bytes 59788288 | tf_op jit(solution)/shard_map/td,fed->tfe/dot_general | solution.py:131
  348.5 24.5 %multiply_reduce_fusion.1 = (f32[768]{0:T(1024)}, f32[1024]{0:T(1024)S(1)}, f32[768]{0:T(1024)}, f32[1024,768]{0,1:T(8,128)}) fusion(f32[1024,768]{0,1:T(8,128)} %copy-done.12, f32[1024]{0:T(1024)S(1)} %fusion.81, f32[1024]{0:T(1024)S(1)} %broadcast_multiply_fusion.4, f32[768]{0:T(1024)S(1)} %get-tuple-element.84, ...), kind=kOutput, calls=%fused_computation.65 | convolution fusion | flops 9683334144 | bytes 33071104 | tf_op jit(solution)/shard_map/tfe,fde->td/dot_general | solution.py:145
  405.4 8.2 fusion.77
  413.6 18.5 %fusion.12 = f32[8,768,768]{1,2,0:T(8,128)} fusion(bf16[1024,4,768]{2,0,1:T(8,128)(2,1)} %get-tuple-element.95, bf16[1024,4,768]{2,0,1:T(8,128)(2,1)} %get-tuple-element.94, f32[1024,768]{0,1:T(8,128)} %copy-done.12, f32[768]{0:T(1024)S(1)} %get-tuple-element.83, f32[768]{0:T(1024)S(1)} %get-tuple-element.84, f32[1024]{0:T(1024)S(1)} %fusion.81, ...), kind=kOutput, calls=%fused_computation.34 | convolution fusion | flops 9673900032 | bytes 34617344 | tf_op jit(solution)/shard_map/td,tfe->fde/dot_general | solution.py:142
  466.5 9.7 convolution_bitcast_fusion
  476.2 26.0 %pad_maximum_fusion = f32[16,768,768]{1,2,0:T(8,128)} fusion(f32[4,768,768]{1,2,0:T(8,128)} %fusion.77, f32[8,768,768]{1,2,0:T(8,128)} %fusion.12, f32[1,768,768]{1,2,0:T(8,128)} %convolution_bitcast_fusion.2, f32[3,768,768]{1,2,0:T(8,128)} %convolution_bitcast_fusion), kind=kLoop, calls=%fused_computation.7 | loop fusion | flops 28311552 | bytes 75497472 | tf_op jit(solution)/shard_map/concatenate | solution.py:180
  502.1 37.9 %copy.333 = f32[16,768,768]{2,0,1:T(8,128)} copy(f32[16,768,768]{1,2,0:T(8,128)} %pad_maximum_fusion) | data formatting | bytes 75497472 | tf_op jit(solution)/shard_map/concatenate | solution.py:180
  540.1 539.0 %reduce-scatter.5.cloned.1.call-done = f32[16,48,768]{2,0,1:T(8,128)} async-done(((f32[16,768,768]{2,0,1:T(8,128)}), f32[16,48,768]{2,0,1:T(8,128)}) %reduce-scatter.5.cloned.1.call-update) | async-done | bytes 2359312 | tf_op jit(solution)/shard_map/reduce_scatter | solution.py:200
  1116.3 62.3 %all_to_all.60 = f32[16,1,48,768]{3,2,1,0:T(8,128)} all-to-all(f32[16,1,48,768]{3,2,1,0:T(8,128)} %get-tuple-element.107), channel_id=1, replica_groups=mesh['dp'=2,'zero'=16] {'zero'}, dimensions={0} | all-to-all | bytes 4718592 | tf_op jit(solution)/shard_map/all_to_all | solution.py:204
  1178.7 57.7 %all_to_all.61 = f32[16,1,48,768]{3,2,1,0:T(8,128)} all-to-all(f32[16,1,48,768]{3,2,1,0:T(8,128)S(1)} %get-tuple-element.106), channel_id=1, replica_groups=mesh['dp'=2,'zero'=16] {'zero'}, dimensions={0} | all-to-all | bytes 4718592 | tf_op jit(solution)/shard_map/all_to_all | solution.py:224
  1236.4 57.8 %all_to_all.62 = f32[16,1,48,768]{3,2,1,0:T(8,128)} all-to-all(f32[16,1,48,768]{3,2,1,0:T(8,128)S(1)} %get-tuple-element.110), channel_id=1, replica_groups=mesh['dp'=2,'zero'=16] {'zero'}, dimensions={0} | all-to-all | bytes 4718592 | tf_op jit(solution)/shard_map/all_to_all | solution.py:219
  1294.2 57.8 %all_to_all.63 = f32[16,1,48,768]{3,2,1,0:T(8,128)} all-to-all(f32[16,1,48,768]{3,2,1,0:T(8,128)S(1)} %get-tuple-element.108), channel_id=1, replica_groups=mesh['dp'=2,'zero'=16] {'zero'}, dimensions={0} | all-to-all | bytes 4718592 | tf_op jit(solution)/shard_map/all_to_all | solution.py:213
  1371.7 31.2 %all-to-all-done.3 = f32[16,1,48,768]{3,2,1,0:T(8,128)} async-done(((f32[16,1,48,768]{3,2,1,0:T(8,128)}), f32[16,1,48,768]{3,2,1,0:T(8,128)}, u32[]{:S(2)}, u32[]{:S(2)}) %all-to-all-start.3) | async-done | bytes 2359328 | tf_op jit(solution)/shard_map/all_to_all | solution.py:207
  1402.8 10.3 fusion.31
  1428.1 10.4 copy.336
  1438.4 10.9 all-to-all-start.5
  1450.5 10.0 fusion.23
  1466.7 209.3 %reduce-scatter.7.cloned.1.call-done = f32[48,4]{1,0:T(8,128)} async-done(((f32[768,4]{1,0:T(8,128)}), f32[48,4]{1,0:T(8,128)}) %reduce-scatter.7.cloned.1.call-update) | async-done | bytes 784
  (186 shorter events, 225.3 us)
Async XLA Ops:
  7.2 1076.4 %copy-start = (f32[16,48,768]{2,1,0:T(8,128)S(1)}, f32[16,48,768]{2,1,0:T(8,128)}, u32[]{:S(2)}) copy-start(f32[16,48,768]{2,1,0:T(8,128)} %param.25) | copy-start | bytes 7077892
  7.2 218.0 %all-gather.3.cloned.1.call-start = ((), (), s32[]{:S(2)}) async-start(), calls=%async_computation.8 | async-start | bytes 20054016 | tf_op jit(solution)/shard_map/all_gather | solution.py:79
  10.2 1068.9 %reduce-scatter.5.cloned.1.call-start = ((), (), s32[]{:S(2)}) async-start(), calls=%async_computation.9 | async-start | bytes 40108032 | tf_op jit(solution)/shard_map/reduce_scatter | solution.py:200
  24.8 46.6 %copy-start.34 = (f32[12]{0:T(128)S(1)}, f32[12]{0:T(128)}, u32[]{:S(2)}) copy-start(f32[12]{0:T(128)} %constant.173) | copy-start | bytes 148
  71.3 160.2 %copy-start.30 = (pred[8,128]{1,0:T(8,128)(4,1)}, pred[8,128]{1,0:T(8,128)(4,1)S(1)}, u32[]{:S(2)}) copy-start(pred[8,128]{1,0:T(8,128)(4,1)S(1)} %fusion.80) | copy-start | bytes 3076
  260.2 49.8 %copy-start.12 = (f32[1024,768]{0,1:T(8,128)}, f32[1024,768]{0,1:T(8,128)S(1)}, u32[]{:S(2)}) copy-start(f32[1024,768]{0,1:T(8,128)S(1)} %get-tuple-element.114) | copy-start | bytes 9437188
  310.1 9.4 copy-start.15
  310.1 9.4 copy-start.6
  386.9 9.8 slice-start
  392.1 12.5 slice-start.2
  396.7 7.9 slice-start.3
  540.1 564.6 %all-reduce.2.cloned.1.call-start = ((), (), s32[]{:S(2)}) async-start(), calls=%async_computation.10 | async-start | bytes 4718592 | tf_op jit(solution)/shard_map/psum | solution.py:203
  1352.0 50.9 %all-to-all-start.3 = ((f32[16,1,48,768]{3,2,1,0:T(8,128)}), f32[16,1,48,768]{3,2,1,0:T(8,128)}, u32[]{:S(2)}, u32[]{:S(2)}) async-start(f32[16,1,48,768]{3,2,1,0:T(8,128)} %get-tuple-element.109), calls=%async_computation.4 | async-start | bytes 4718592 | tf_op jit(solution)/shard_map/all_to_all | solution.py:207
  1402.8 10.3 copy-start.18
  1438.4 11.0 copy-start.23
  1438.4 11.0 copy-start.22
  1438.4 11.0 copy-start.29
  1438.4 11.1 copy-start.28
  1438.4 12.1 copy-start.31
  1438.4 241.4 %all-to-all-start.5 = ((f32[1,1,3,768,768]{4,1,2,0,3:T(1,128)}), f32[1,1,3,768,768]{4,1,2,0,3:T(1,128)}, u32[]{:S(2)}, u32[]{:S(2)}) async-start(f32[1,1,3,768,768]{4,1,2,0,3:T(1,128)} %copy.336), calls=%async_computation.6 | async-start | bytes 14155776 | tf_op jit(solution)/shard_map/all_to_all | solution.py:231
  1449.3 226.7 %reduce-scatter.7.cloned.1.call-start = ((), (), s32[]{:S(2)}) async-start(), calls=%async_computation.11 | async-start | bytes 417792
  1463.1 216.2 %copy-start.26 = (f32[4,48]{1,0:T(4,128)S(1)}, f32[4,48]{1,0:T(4,128)}, u32[]{:S(2)}) copy-start(f32[4,48]{1,0:T(4,128)} %param.23) | copy-start | bytes 2308
  1463.1 216.2 %copy-start.32 = (f32[4,48]{1,0:T(4,128)S(1)}, f32[4,48]{1,0:T(4,128)}, u32[]{:S(2)}) copy-start(f32[4,48]{1,0:T(4,128)} %param.29) | copy-start | bytes 2308
  1463.1 216.2 %copy-start.33 = (f32[4,48]{1,0:T(4,128)S(1)}, f32[4,48]{1,0:T(4,128)}, u32[]{:S(2)}) copy-start(f32[4,48]{1,0:T(4,128)} %param.28) | copy-start | bytes 2308
  (21 other events, 66.0 us)
Sparse Core Ops, SparseCore 0:
  11.3 213.8 all-gather.2
  540.2 538.8 reduce-scatter.4
  1083.7 20.9 all-reduce.1
  1455.1 220.8 reduce-scatter.6
where the time goes:
time: 1720 us; the launch traced here: 1710 us
  waiting for transfers between devices  937 us (54%)
  blocking collectives  282 us (16%)
  matrix products  194 us (11%)
  local copies, waits for them, and re-layouts  170 us (10%)
  other arithmetic  94.5 us (5%)
    reduce_scatter x1, waiting for transfers between devices, shards(): lax.psum_scatter(tile_grads, 'zero', scatter_dimension=1, tiled=True)  539 us
    unnamed x5, waiting for transfers between devices  209 us
    all_gather x1, waiting for transfers between devices, shards(): lax.all_gather(shard_low, 'zero', axis=1, tiled=True)  150 us
    all_to_all x1, blocking collectives, shards(): lax.all_to_all(outgoing(left_basis), 'zero', split_axis=0, concat_axis=2,...  62.3 us
    all_to_all x1, blocking collectives, shards(): lax.all_to_all(outgoing(first_moment), 'zero', split_axis=0, concat_axis=...  57.8 us
    all_to_all x1, blocking collectives, shards(): lax.all_to_all(outgoing(tile_sum), 'zero', split_axis=0, concat_axis=2, t...  57.8 us
    all_to_all x1, blocking collectives, shards(): lax.all_to_all(outgoing(second_moment), 'zero', split_axis=0, concat_axis...  57.7 us
    all_gather x1, blocking collectives, shards(): lax.all_gather(norm_params.astype(jnp.bfloat16), 'zero', axis=1, tiled=True)  43.7 us
  transfers between devices with their start and end apart: 6, of which 5 were waited for; matrix products, arithmetic and copies ran while one was open for 4% of the time, Pallas kernels for 0%

commit v1 on v0

v1 whole, which is shorter than its diff:
```python
import math

import jax
import jax.numpy as jnp
import numpy as np
from jax import lax
from jax.sharding import PartitionSpec as P

HEADS = 12

norm_eps = 1e-12
beta_one = 0.9
beta_two = 0.95
adam_eps = 1e-08
peak_rate = 0.1
warm_steps = 5.0
total_steps = 60.0
decay_rate = 0.01
low_type = jnp.bfloat16
full_type = jnp.float32


def alibi_slopes(head_count):

    def power_slopes(power_count):
        first_slope = 2.0 ** (-8.0 / power_count)
        return [first_slope ** (position + 1) for position in range(power_count)]

    nearest = 2 ** int(math.floor(math.log2(head_count)))
    slope_list = power_slopes(nearest)
    slope_list = slope_list + power_slopes(2 * nearest)[0::2][: head_count - nearest]
    return np.array(slope_list, np.float32)


def norm_stats(values):
    row_mean = jnp.mean(values, axis=-1, keepdims=True)
    centered = values - row_mean
    rstd = lax.rsqrt(jnp.mean(centered * centered, axis=-1, keepdims=True) + norm_eps)
    return centered * rstd, rstd


def norm_back(grad, unit, rstd, gain_row):
    scaled = grad * gain_row
    mean_grad = jnp.mean(scaled, axis=-1, keepdims=True)
    mean_prod = jnp.mean(scaled * unit, axis=-1, keepdims=True)
    gain_grad = jnp.sum(grad * unit, axis=0)
    shift_grad = jnp.sum(grad, axis=0)
    return rstd * (scaled - mean_grad - unit * mean_prod), gain_grad, shift_grad


def dot32(spec, left, right):
    return jnp.einsum(spec, left, right, preferred_element_type=full_type)


def two_parts(values):
    high = lax.reduce_precision(values, 8, 7)
    return high.astype(low_type), (values - high).astype(low_type)


def shards(
    tokens,
    out_grad,
    mask_pos,
    repl_id,
    replace_embed,
    masters,
    norm_params,
    first_moment,
    second_moment,
    left_basis,
    right_basis,
    norm_first,
    norm_second,
    step,
):
    seq_count = mask_pos.shape[0]
    tok_rows, width = tokens.shape
    length = tok_rows // seq_count
    heads = HEADS
    head_size = width // heads
    scale = float(head_size) ** (-0.5)
    tiles = masters.shape[0]
    ff = (tiles - 4) // 3
    rows = masters.shape[1]
    replicas = lax.axis_size("dp")
    owners = lax.axis_size("zero")
    my_copy = lax.axis_index("dp")
    my_rows = lax.axis_index("zero")

    part = rows // replicas
    shard_low = masters.astype(low_type)
    sent = lax.dynamic_slice_in_dim(shard_low, my_copy * part, part, 1)
    whole = lax.all_gather(sent, ("zero", "dp"), axis=1, tiled=True)
    norm_whole = lax.all_gather(norm_params.astype(low_type), "zero", axis=1, tiled=True)

    def outgoing(values):
        spare = owners - tiles
        return jnp.pad(values, ((0, spare),) + ((0, 0),) * (values.ndim - 1)) if spare else values

    packed = jnp.stack([left_basis, right_basis, first_moment, second_moment], axis=1)
    packed = lax.all_to_all(
        outgoing(packed.astype(low_type)), "zero", split_axis=0, concat_axis=0, tiled=True
    )
    packed = packed.transpose(1, 0, 2, 3).reshape(4, width, width)

    positions = jnp.arange(length, dtype=jnp.int32)
    mask_hits = mask_pos[:, :, None] == positions[None, None, :]
    masked = jnp.any(mask_hits, axis=1).reshape(-1, 1)
    row_ids = jnp.sum(jnp.where(mask_hits, repl_id[:, :, None], 0), axis=1).reshape(-1)
    inputs = jnp.where(masked, jnp.take(replace_embed, row_ids, axis=0), tokens)
    whole, packed, inputs = lax.optimization_barrier((whole, packed, inputs))
    left_low, right_low, moment_one_low, moment_two_low = packed
    gains = norm_whole.astype(full_type)

    slopes = jnp.asarray(alibi_slopes(heads))
    distance = jnp.abs(positions[:, None] - positions[None, :]).astype(full_type)
    alibi_bias = -slopes[:, None, None] * distance[None]
    head_shape = (seq_count, length, heads, head_size)

    qkv = [dot32("td,de->te", inputs, whole[k]).astype(low_type) for k in range(3)]
    queries, key_rows, values = [part_k.reshape(head_shape) for part_k in qkv]
    scores = dot32("bqhd,bkhd->bhqk", queries, key_rows) * scale + alibi_bias[None]
    row_max = jnp.max(scores, axis=-1, keepdims=True)
    log_total = row_max + jnp.log(jnp.sum(jnp.exp(scores - row_max), axis=-1, keepdims=True))
    probs = jnp.exp(scores - log_total)
    soft_low = probs.astype(low_type)
    mixed = dot32("bhqk,bkhd->bqhd", soft_low, values).reshape(tok_rows, width).astype(low_type)
    attended = dot32("td,de->te", mixed, whole[3])
    unit_one, rstd_one = norm_stats(inputs.astype(full_type) + attended)
    hidden = unit_one * gains[0] + gains[1]
    hidden_low = hidden.astype(low_type)

    gate = dot32("td,fde->tfe", hidden_low, whole[4 : 4 + ff])
    up = dot32("td,fde->tfe", hidden_low, whole[4 + ff : 4 + 2 * ff])
    half_erf = 0.5 + 0.5 * lax.erf(gate * math.sqrt(0.5))
    act = gate * half_erf
    slope = half_erf + gate * (jnp.exp(-0.5 * gate * gate) * (1.0 / math.sqrt(2.0 * math.pi)))
    inner_low = (act * up).astype(low_type)
    inner_low, act, up_slope = lax.optimization_barrier((inner_low, act, up * slope))
    branch = dot32("tfe,fed->td", inner_low, whole[4 + 2 * ff :])
    unit_two, rstd_two = norm_stats(hidden + branch)
    layer_out = (unit_two * gains[2] + gains[3]).astype(low_type)

    d_second, d_gain_two, d_shift_two = norm_back(
        out_grad.astype(full_type), unit_two, rstd_two, gains[2]
    )
    d_branch = d_second.astype(low_type)
    grad_down = dot32("tfe,td->fed", inner_low, d_branch).astype(low_type)
    d_inner = dot32("td,fed->tfe", d_branch, whole[4 + 2 * ff :])
    d_gate = (d_inner * up_slope).astype(low_type)
    d_up = (d_inner * act).astype(low_type)
    grad_gate = dot32("td,tfe->fde", hidden_low, d_gate).astype(low_type)
    grad_up = dot32("td,tfe->fde", hidden_low, d_up).astype(low_type)
    d_hidden = (
        d_second
        + dot32("tfe,fde->td", d_gate, whole[4 : 4 + ff])
        + dot32("tfe,fde->td", d_up, whole[4 + ff : 4 + 2 * ff])
    )
    d_first, d_gain_one, d_shift_one = norm_back(d_hidden, unit_one, rstd_one, gains[0])
    d_attended = d_first.astype(low_type)
    grad_out = dot32("td,te->de", mixed, d_attended).astype(low_type)
    d_mixed = dot32("te,de->td", d_attended, whole[3]).astype(low_type).reshape(head_shape)
    d_probs = dot32("bqhd,bkhd->bhqk", d_mixed, values)
    row_delta = jnp.sum(probs * d_probs, axis=-1, keepdims=True)
    d_scores = (probs * (d_probs - row_delta)).astype(low_type)
    d_query = dot32("bhqk,bkhd->bqhd", d_scores, key_rows) * scale
    d_keys = dot32("bhqk,bqhd->bkhd", d_scores, queries) * scale
    d_values = dot32("bhqk,bqhd->bkhd", soft_low, d_mixed)
    d_qkv = [
        grad.astype(low_type).reshape(tok_rows, width) for grad in (d_query, d_keys, d_values)
    ]
    grad_qkv = [dot32("td,te->de", inputs, grad).astype(low_type)[None] for grad in d_qkv]
    d_inputs = d_first
    for k in range(3):
        d_inputs = d_inputs + dot32("te,de->td", d_qkv[k], whole[k])
    in_grad = jnp.where(masked, 0.0, d_inputs)

    tile_grads = jnp.concatenate(
        grad_qkv + [grad_out[None], grad_gate, grad_up, grad_down], axis=0
    )
    norm_grads = jnp.stack([d_gain_one, d_shift_one, d_gain_two, d_shift_two])
    norm_sum = lax.psum(norm_grads, ("dp", "zero"))
    norm_sum = lax.dynamic_slice_in_dim(norm_sum, my_rows * norm_params.shape[1], norm_params.shape[1], 1)
    flat_grads = outgoing(tile_grads).reshape(owners * width, width)
    tile_part = lax.psum_scatter(flat_grads, ("zero", "dp"), scatter_dimension=0, tiled=True)
    tile_part, in_grad, norm_sum = lax.optimization_barrier((tile_part, in_grad, norm_sum))
    tile_sum = lax.all_gather(tile_part, "dp", axis=0, tiled=True)

    step_value = step[0].astype(full_type)
    step_rate = peak_rate * jnp.minimum(
        step_value / warm_steps, (total_steps - step_value) / (total_steps - warm_steps)
    )
    fix_one = 1.0 - jnp.power(beta_one, step_value)
    fix_two = 1.0 - jnp.power(beta_two, step_value)
    turned = dot32("ji,jl->il", left_low, tile_sum)
    high, rest = two_parts(turned)
    rotated = dot32("il,lm->im", high, right_low) + dot32("il,lm->im", rest, right_low)
    mean_one = beta_one * moment_one_low.astype(full_type) + (1.0 - beta_one) * rotated
    mean_two = beta_two * moment_two_low.astype(full_type) + (1.0 - beta_two) * rotated * rotated
    direction = mean_one / fix_one / (jnp.sqrt(mean_two / fix_two) + adam_eps)
    high, rest = two_parts(direction)
    turned = dot32("ij,jl->il", left_low, high) + dot32("ij,jl->il", left_low, rest)
    high, rest = two_parts(turned)
    update = dot32("il,ml->im", high, right_low) + dot32("il,ml->im", rest, right_low)
    results = jnp.stack(
        [rotated.astype(low_type).reshape(owners, rows, width),
         update.astype(low_type).reshape(owners, rows, width)], axis=1
    )
    returned = lax.all_to_all(results, "zero", split_axis=0, concat_axis=0, tiled=True)[:tiles]
    returned = returned.astype(full_type)
    turned_rows = returned[:, 0]
    new_first = beta_one * first_moment + (1.0 - beta_one) * turned_rows
    new_second = beta_two * second_moment + (1.0 - beta_two) * turned_rows * turned_rows
    new_master = masters - step_rate * (returned[:, 1] + decay_rate * masters)
    new_norm_first = beta_one * norm_first + (1.0 - beta_one) * norm_sum
    new_norm_second = beta_two * norm_second + (1.0 - beta_two) * norm_sum * norm_sum
    new_norms = norm_params - step_rate * (new_norm_first / fix_one) / (
        jnp.sqrt(new_norm_second / fix_two) + adam_eps
    )
    return (
        layer_out,
        in_grad,
        new_first,
        new_second,
        new_master,
        new_master.astype(low_type),
        new_norm_first,
        new_norm_second,
        new_norms,
    )


def solution(mesh):
    in_specs = (
        P(("dp", "zero"), None),
        P(("dp", "zero"), None),
        P(("dp", "zero"), None),
        P(("dp", "zero"), None),
        P(),
        P(None, "zero", None),
        P(None, "zero"),
        P(None, "zero", None),
        P(None, "zero", None),
        P(None, "zero", None),
        P(None, "zero", None),
        P(None, "zero"),
        P(None, "zero"),
        P(),
    )
    out_specs = (
        P(("dp", "zero"), None),
        P(("dp", "zero"), None),
        P(None, "zero", None),
        P(None, "zero", None),
        P(None, "zero", None),
        P(None, "zero", None),
        P(None, "zero"),
        P(None, "zero"),
        P(None, "zero"),
    )
    return jax.shard_map(shards, mesh=mesh, in_specs=in_specs, out_specs=out_specs, check_vma=False)
```

time: 1720 us -> 748 us (0.43)
  waiting for transfers between devices: 937 us -> 234 us
  local copies, waits for them, and re-layouts: 170 us -> 65.2 us
  other arithmetic: 94.5 us -> 27.3 us
  blocking collectives: 282 us -> 217 us
  matrix products: 194 us -> 159 us
    reduce_scatter x1, waiting for transfers between devices: 539 us -> 158 us  [shards(): lax.psum_scatter(flat_grads, ('zero', 'dp'), scatter_dimension=0, tiled=T...]
    all_to_all x4 -> x0, blocking collectives: 236 us -> none  [the longest x1 62.3 us: shards(): lax.all_to_all(outgoing(left_basis), 'zero', split_axis=0, concat_axis=2,...]
    unnamed x5 -> x3, waiting for transfers between devices: 209 us -> 0.05 us
    all_gather x1 -> x2, waiting for transfers between devices: 150 us -> 33.9 us  [the longest x1 24.7 us: shards(): whole = lax.all_gather(sent, ('zero', 'dp'), axis=1, tiled=True)]
    all_gather x1, blocking collectives: 43.7 us -> 148 us  [shards(): lax.all_gather(norm_params.astype(low_type), 'zero', axis=1, tiled=True)]
    psum x1, blocking collectives: 2.45 us -> 69.3 us  [shards(): norm_sum = lax.psum(norm_grads, ('dp', 'zero'))]
    concatenate x1 -> x0, local copies, waits for them, and re-layouts: 37.9 us -> none  [shards(): jnp.concatenate([grad_qkv, grad_out[None], grad_gate_up, grad_down], axis=0)]
    dot_general x22 -> x34, matrix products: 194 us -> 159 us  [dot32(): return jnp.einsum(spec, left, right, preferred_element_type=full_type)]
  transfers between devices with their start and end apart: 6 -> 5, of which waited for: 5 -> 4; matrix products, arithmetic and copies ran while one was open for 4% -> 6% of each run, Pallas kernels for 0% -> 0%
where the time goes in v1:
time: 748 us; the launch traced here: 734 us
  waiting for transfers between devices  234 us (31%)
  blocking collectives  217 us (29%)
  matrix products  159 us (21%)
  local copies, waits for them, and re-layouts  65.2 us (9%)
  other arithmetic  27.3 us (4%)
  starting transfers between devices  15.7 us (2%)
  between operations  15.7 us (2%)
    dot_general x34, matrix products, dot32(): return jnp.einsum(spec, left, right, preferred_element_type=full_type)  159 us
    reduce_scatter x1, waiting for transfers between devices, shards(): lax.psum_scatter(flat_grads, ('zero', 'dp'), scatter_dimension=0, tiled=T...  158 us
    all_gather x1, blocking collectives, shards(): lax.all_gather(norm_params.astype(low_type), 'zero', axis=1, tiled=True)  148 us
    psum x1, blocking collectives, shards(): norm_sum = lax.psum(norm_grads, ('dp', 'zero'))  69.3 us
    all_to_all x1, waiting for transfers between devices, shards(): lax.all_to_all(results, 'zero', split_axis=0, concat_axis=0, tiled=True)  42.1 us
    unnamed x112, local copies, waits for them, and re-layouts  32.5 us
    all_gather x1, waiting for transfers between devices, shards(): whole = lax.all_gather(sent, ('zero', 'dp'), axis=1, tiled=True)  24.7 us
  transfers between devices with their start and end apart: 5, of which 4 were waited for; matrix products, arithmetic and copies ran while one was open for 6% of the time, Pallas kernels for 0%

profile of v1, /device:TPU:0, one launch (start us, length us, event | category | flops | bytes accessed | tf_op | source)
XLA Modules:
  0.0 734.0 jit_solution(10944323217176093074)
XLA Ops:
  16.0 8.5 %all-to-all-start = ((bf16[16,4,48,768]{3,2,1,0:T(8,128)(2,1)}), bf16[16,4,48,768]{3,2,1,0:T(8,128)(2,1)}, u32[]{:S(2)}, u32[]{:S(2)}) async-start(bf16[16,4,48,768]{3,2,1,0:T(8,128)(2,1)} %pad_maximum_fusion), calls=%async_computation | async-start | bytes 9437184 | tf_op jit(solution)/shard_map/all_to_all | solution.py:101
  24.6 147.8 %all-gather = bf16[16,48,4]{1,2,0:T(4,128)(2,1)S(1)} all-gather(bf16[1,48,4]{1,2,0:T(4,128)(2,1)S(1)} %convert_bitcast_fusion.4), channel_id=1, replica_groups=mesh['dp'=2,'zero'=16] {'zero'}, dimensions={0}, use_global_device_ids=true | all-gather | bytes 6528 | tf_op jit(solution)/shard_map/all_gather | solution.py:94
  172.7 8.1 %gather_fusion = bf16[1024,768]{1,0:T(8,128)(2,1)S(1)} fusion(bf16[4096,768]{1,0:T(8,128)(2,1)} %param.19, s32[1024]{0:T(1024)S(1)} %broadcast_clamp_fusion), kind=kCustom, calls=%fused_computation | custom fusion | bytes 3149824 | tf_op jit(solution)/shard_map/jit(_take)/gather | solution.py:110
  189.9 5.0 copy.169
  194.9 24.7 %all-gather.4.cloned.1.call-done = bf16[16,768,768]{2,1,0:T(8,128)(2,1)} async-done(((bf16[16,24,768]{2,1,0:T(8,128)(2,1)}), bf16[16,768,768]{2,1,0:T(8,128)(2,1)}) %all-gather.4.cloned.1.call-update) | async-done | bytes 18874384 | tf_op jit(solution)/shard_map/all_gather | solution.py:93
  219.6 4.4 convolution_convert_fusion.3
  259.3 11.1 %fusion.19 = f32[1024,4,768]{2,0,1:T(8,128)} fusion(bf16[1024,768,1]{0,1,2:T(8,128)(2,1)S(1)} %fusion.44, bf16[16,768,768]{2,1,0:T(8,128)(2,1)} %all-gather.4.cloned.1.call-done), kind=kOutput, calls=%fused_computation.37 | convolution fusion | flops 4831838208 | bytes 18874368 | tf_op jit(solution)/shard_map/td,fde->tfe/dot_general | solution.py:52
  270.4 20.2 %multiply_convert_fusion.2 = (bf16[1024,4,768]{2,0,1:T(8,128)(2,1)S(1)}, f32[1024,4,768]{2,0,1:T(8,128)}, f32[1024,4,768]{2,0,1:T(8,128)}) fusion(f32[1024,4,768]{2,0,1:T(8,128)} %fusion.19, bf16[1024,768,1]{0,1,2:T(8,128)(2,1)S(1)} %fusion.44, bf16[16,768,768]{2,1,0:T(8,128)(2,1)} %all-gather.4.cloned.1.call-done), kind=kOutput, calls=%fused_computation.9 | convolution fusion | flops 4869586944 | bytes 50331648 | tf_op jit(solution)/shard_map/td,fde->tfe/dot_general | solution.py:52
  290.6 9.2 %fusion.174 = (f32[1024]{0:T(1024)S(1)}, f32[1024,768]{0,1:T(8,128)S(1)}) fusion(bf16[1024,4,768]{2,0,1:T(8,128)(2,1)S(1)} %get-tuple-element.20, bf16[16,768,768]{2,1,0:T(8,128)(2,1)} %all-gather.4.cloned.1.call-done, f32[768]{0:T(1024)S(1)} %get-tuple-element.82, f32[768]{0:T(1024)S(1)} %get-tuple-element.83, f32[1024]{0:T(1024)S(1)} %add_rsqrt_fusion.1, ...), kind=kOutput, calls=%fused_computation.225 | convolution fusion | flops 4836555776 | bytes 17319936 | tf_op jit(solution)/shard_map/tfe,fed->td/dot_general | solution.py:52
  304.3 16.8 %multiply_convert_fusion.1 = (bf16[1024,4,768]{2,0,1:T(8,128)(2,1)}, bf16[1024,4,768]{2,0,1:T(8,128)(2,1)}) fusion(f32[1024,4,768]{2,0,1:T(8,128)} %get-tuple-element.21, f32[1024,4,768]{2,0,1:T(8,128)} %get-tuple-element.22, bf16[16,768,768]{2,1,0:T(8,128)(2,1)} %all-gather.4.cloned.1.call-done, f32[1024]{0:T(1024)S(1)} %broadcast_multiply_fusion.3, ...), kind=kOutput, calls=%fused_computation.8 | convolution fusion | flops 4851499008 | bytes 47205376 | tf_op jit(solution)/shard_map/td,fed->tfe/dot_general | solution.py:52
  321.1 8.7 %fusion.13 = f32[1024,768,1]{0,1,2:T(8,128)S(1)} fusion(bf16[1024,4,768]{2,0,1:T(8,128)(2,1)} %get-tuple-element.93, bf16[16,768,768]{2,1,0:T(8,128)(2,1)} %all-gather.4.cloned.1.call-done), kind=kOutput, calls=%fused_computation.31 | convolution fusion | flops 4831838208 | bytes 14155776 | tf_op jit(solution)/shard_map/tfe,fde->td/dot_general | solution.py:52
  329.9 9.0 %multiply_reduce_fusion.1 = (f32[768]{0:T(1024)S(1)}, f32[1024]{0:T(1024)S(1)}, f32[1024]{0:T(1024)S(1)}, f32[768]{0:T(1024)S(1)}, f32[1024,768]{0,1:T(8,128)S(1)}) fusion(f32[1024,768]{0,1:T(8,128)S(1)} %copy-done.5, f32[1024]{0:T(1024)S(1)} %add_rsqrt_fusion.1, f32[1024]{0:T(1024)S(1)} %broadcast_multiply_fusion.6, f32[768]{0:T(1024)S(1)} %get-tuple-element.83, ...), kind=kOutput, calls=%fused_computation.55 | convolution fusion | flops 4846776320 | bytes 25210880 | tf_op jit(solution)/shard_map/tfe,fde->td/dot_general | solution.py:52
  341.4 3.9 convolution_convert_fusion.1
  349.9 5.2 fusion.74
  374.2 5.8 bitcast_dynamic-update-slice_fusion.1
  380.1 7.5 %bitcast_dynamic-update-slice_fusion = bf16[16,768,768]{2,1,0:T(8,128)(2,1)S(1)} fusion(bf16[16,768,768]{2,1,0:T(8,128)(2,1)S(1)} %bitcast_dynamic-update-slice_fusion.1, bf16[1024,768,1]{0,1,2:T(8,128)(2,1)} %copy-done.32, bf16[1024,4,768]{2,0,1:T(8,128)(2,1)S(1)} %bitcast.283), kind=kOutput, calls=%fused_computation.21 | convolution fusion | flops 4834197504 | bytes 12582912 | tf_op jit(solution)/shard_map/td,tfe->fde/dot_general | solution.py:52
  387.6 9.1 %convert_dynamic-update-slice_fusion = bf16[16,768,768]{2,1,0:T(8,128)(2,1)S(1)} fusion(bf16[16,768,768]{2,1,0:T(8,128)(2,1)S(1)} %bitcast_dynamic-update-slice_fusion, bf16[1024,4,768]{2,0,1:T(8,128)(2,1)} %copy-done.43, bf16[1024,768]{0,1:T(8,128)(2,1)S(1)} %copy-done.8, f32[1024,768]{0,1:T(8,128)S(1)} %copy-done.3, ...), kind=kOutput, calls=%fused_computation.23 | convolution fusion | flops 4841275392 | bytes 15749120 | tf_op jit(solution)/shard_map/tfe,td->fed/dot_general | solution.py:52
  396.7 6.5 copy-done.6
  403.3 69.3 %psum.7 = f32[4,768]{1,0:T(4,128)S(1)} all-reduce(f32[4,768]{1,0:T(4,128)S(1)} %pad_maximum_fusion.2), channel_id=1, replica_groups=mesh['dp'=2,'zero'=16] {'dp','zero'}, use_global_device_ids=true, to_apply=%region_18.19 | all-reduce | flops 3072 | bytes 24576 | tf_op jit(solution)/shard_map/psum | solution.py:182
  481.6 157.7 %reduce-scatter.2.cloned.1.call-done = bf16[384,768]{1,0:T(8,128)(2,1)} async-done(((bf16[12288,768]{1,0:T(8,128)(2,1)}), bf16[384,768]{1,0:T(8,128)(2,1)}) %reduce-scatter.2.cloned.1.call-update) | async-done | bytes 589840 | tf_op jit(solution)/shard_map/reduce_scatter | solution.py:185
  640.1 9.2 %all-gather.6.cloned.1.call-done = bf16[768,768]{1,0:T(8,128)(2,1)} async-done(((bf16[384,768]{1,0:T(8,128)(2,1)}), bf16[768,768]{1,0:T(8,128)(2,1)}) %all-gather.6.cloned.1.call-update) | async-done | bytes 1179664 | tf_op jit(solution)/shard_map/all_gather | solution.py:187
  665.3 7.1 all-to-all-start.1
  678.0 42.1 %all-to-all-done.1 = bf16[16,2,48,768]{3,2,1,0:T(8,128)(2,1)} async-done(((bf16[16,2,48,768]{3,2,1,0:T(8,128)(2,1)}), bf16[16,2,48,768]{3,2,1,0:T(8,128)(2,1)}, u32[]{:S(2)}, u32[]{:S(2)}) %all-to-all-start.1) | async-done | bytes 2359328 | tf_op jit(solution)/shard_map/all_to_all | solution.py:209
  723.2 4.1 fusion.170
  (194 shorter events, 117.3 us)
Async XLA Ops:
  7.2 212.4 %all-gather.4.cloned.1.call-start = ((), (), s32[]{:S(2)}) async-start(), calls=%async_computation.3 | async-start | bytes 19464192 | tf_op jit(solution)/shard_map/all_gather | solution.py:93
  16.0 8.6 %copy-start.37 = (f32[4,48]{1,0:T(4,128)S(1)}, f32[4,48]{1,0:T(4,128)}, u32[]{:S(2)}) copy-start(f32[4,48]{1,0:T(4,128)} %param.21) | copy-start | bytes 2308
  16.0 156.5 %copy-start.34 = (s32[8,32]{1,0:T(8,128)S(1)}, s32[8,32]{1,0:T(8,128)}, u32[]{:S(2)}) copy-start(s32[8,32]{1,0:T(8,128)} %param.17) | copy-start | bytes 3076
  16.0 156.5 %copy-start.39 = (s32[8,32]{1,0:T(8,128)S(1)}, s32[8,32]{1,0:T(8,128)}, u32[]{:S(2)}) copy-start(s32[8,32]{1,0:T(8,128)} %param.18) | copy-start | bytes 3076
  16.0 173.9 %all-to-all-start = ((bf16[16,4,48,768]{3,2,1,0:T(8,128)(2,1)}), bf16[16,4,48,768]{3,2,1,0:T(8,128)(2,1)}, u32[]{:S(2)}, u32[]{:S(2)}) async-start(bf16[16,4,48,768]{3,2,1,0:T(8,128)(2,1)} %pad_maximum_fusion), calls=%async_computation | async-start | bytes 9437184 | tf_op jit(solution)/shard_map/all_to_all | solution.py:101
  24.5 614.8 %reduce-scatter.2.cloned.1.call-start = ((), (), s32[]{:S(2)}) async-start(), calls=%async_computation.4 | async-start | bytes 19464192 | tf_op jit(solution)/shard_map/reduce_scatter | solution.py:185
  183.1 146.7 %copy-start.7 = (bf16[1024,768]{0,1:T(8,128)(2,1)}, bf16[1024,768]{0,1:T(8,128)(2,1)S(1)}, u32[]{:S(2)}) copy-start(bf16[1024,768]{0,1:T(8,128)(2,1)S(1)} %copy.184) | copy-start | bytes 4718596
  186.4 8.4 %copy-start.35 = (pred[8,128]{1,0:T(8,128)(4,1)}, pred[8,128]{1,0:T(8,128)(4,1)S(1)}, u32[]{:S(2)}) copy-start(pred[8,128]{1,0:T(8,128)(4,1)S(1)} %fusion.160) | copy-start | bytes 3076
  258.4 32.2 %copy-start.4 = (f32[1024,768]{0,1:T(8,128)}, f32[1024,768]{0,1:T(8,128)S(1)}, u32[]{:S(2)}) copy-start(f32[1024,768]{0,1:T(8,128)S(1)} %get-tuple-element.100) | copy-start | bytes 9437188
  259.3 11.1 %copy-start.32 = (bf16[1024,768,1]{0,1,2:T(8,128)(2,1)}, bf16[1024,768,1]{0,1,2:T(8,128)(2,1)S(1)}, u32[]{:S(2)}) copy-start(bf16[1024,768,1]{0,1,2:T(8,128)(2,1)S(1)} %fusion.44) | copy-start | bytes 4718596
  290.6 9.2 %copy-start.43 = (bf16[1024,4,768]{2,0,1:T(8,128)(2,1)}, bf16[1024,4,768]{2,0,1:T(8,128)(2,1)S(1)}, u32[]{:S(2)}) copy-start(bf16[1024,4,768]{2,0,1:T(8,128)(2,1)S(1)} %get-tuple-element.20) | copy-start | bytes 18874372
  321.1 8.8 %copy-start.2 = (f32[1024,768]{0,1:T(8,128)S(1)}, f32[1024,768]{0,1:T(8,128)}, u32[]{:S(2)}) copy-start(f32[1024,768]{0,1:T(8,128)} %copy-done.1) | copy-start | bytes 9437188
  321.1 8.8 %copy-start.5 = (f32[1024,768]{0,1:T(8,128)S(1)}, f32[1024,768]{0,1:T(8,128)}, u32[]{:S(2)}) copy-start(f32[1024,768]{0,1:T(8,128)} %copy-done.4) | copy-start | bytes 9437188
  321.1 8.8 %copy-start.24 = (bf16[1024,4,768]{2,0,1:T(8,128)(2,1)S(1)}, bf16[1024,4,768]{2,0,1:T(8,128)(2,1)}, u32[]{:S(2)}) copy-start(bf16[1024,4,768]{2,0,1:T(8,128)(2,1)} %get-tuple-element.92) | copy-start | bytes 18874372
  345.3 9.8 %slice-start = ((s8[6291456]{0:T(1024)(128)(4,1)}), s8[2097152]{0:T(1024)(128)(4,1)S(1)}, s32[]{:S(2)}) async-start(s8[6291456]{0:T(1024)(128)(4,1)} %bitcast.256), calls=%async_computation.6 | async-start | bytes 4194304
  364.9 5.4 copy-start.22
  372.7 7.3 slice-start.4
  374.2 5.8 slice-start.5
  380.0 7.5 %copy-start.3 = (f32[1024,768]{0,1:T(8,128)S(1)}, f32[1024,768]{0,1:T(8,128)}, u32[]{:S(2)}) copy-start(f32[1024,768]{0,1:T(8,128)} %copy-done.1) | copy-start | bytes 9437188
  380.0 7.5 %copy-start.8 = (bf16[1024,768]{0,1:T(8,128)(2,1)S(1)}, bf16[1024,768]{0,1:T(8,128)(2,1)}, u32[]{:S(2)}) copy-start(bf16[1024,768]{0,1:T(8,128)(2,1)} %copy-done.7) | copy-start | bytes 4718596
  396.7 6.5 copy-start.6
  403.2 246.1 %all-gather.6.cloned.1.call-start = ((), (), s32[]{:S(2)}) async-start(), calls=%async_computation.5 | async-start | bytes 1769472 | tf_op jit(solution)/shard_map/all_gather | solution.py:187
  665.3 54.7 %all-to-all-start.1 = ((bf16[16,2,48,768]{3,2,1,0:T(8,128)(2,1)}), bf16[16,2,48,768]{3,2,1,0:T(8,128)(2,1)}, u32[]{:S(2)}, u32[]{:S(2)}) async-start(bf16[16,2,48,768]{3,2,1,0:T(8,128)(2,1)} %pad_maximum_fusion.1), calls=%async_computation.2 | async-start | bytes 4718592 | tf_op jit(solution)/shard_map/all_to_all | solution.py:209
  678.0 44.5 %copy-start.19 = (f32[16,48,768]{2,1,0:T(8,128)S(1)}, f32[16,48,768]{2,1,0:T(8,128)}, u32[]{:S(2)}) copy-start(f32[16,48,768]{2,1,0:T(8,128)} %param.23) | copy-start | bytes 7077892
  (33 other events, 98.1 us)
Sparse Core Ops, SparseCore 0:
  11.5 208.0 all-gather.3
  403.3 235.9 reduce-scatter.1
  640.8 8.3 all-gather.5

commit v2 on v1

--- a/solution.py
+++ b/solution.py
@@ -93,23 +93,97 @@
     whole = lax.all_gather(sent, ("zero", "dp"), axis=1, tiled=True)
     norm_whole = lax.all_gather(norm_params.astype(low_type), "zero", axis=1, tiled=True)
 
+    group = ff
+    lines = owners // group
+    my_line, my_spot = my_rows // group, my_rows % group
+
+    def pick(values, index, axis):
+        return lax.dynamic_index_in_dim(values, index, axis, keepdims=False)
+
+    def from_copies(values, shift):
+        pairs = [(i, (i + shift) % replicas) for i in range(replicas)]
+        return lax.ppermute(values, "dp", pairs)
+
+    def from_spots(values, shift):
+        pairs = [(i, i - i % group + (i + shift) % group) for i in range(owners)]
+        return lax.ppermute(values, "zero", pairs)
+
+    def from_lines(values, shift, targets):
+        pairs = [(i, (i + shift * group) % owners) for i in range(owners)]
+        return lax.ppermute(values, "zero", [(i, k) for i, k in pairs if k // group in targets])
+
+    def join_copies(values):
+        pieces = [values] + [from_copies(values, shift) for shift in range(1, replicas)]
+        if replicas == 2:
+            first = my_copy == 0
+            return jnp.stack(
+                [jnp.where(first, pieces[0], pieces[1]), jnp.where(first, pieces[1], pieces[0])]
+            )
+        joined = jnp.zeros((replicas,) + values.shape, values.dtype)
+        for shift, piece in enumerate(pieces):
+            joined = lax.dynamic_update_index_in_dim(
+                joined, piece, (my_copy + replicas - shift) % replicas, 0
+            )
+        return joined
+
+    def sum_everywhere(values):
+        total = values
+        for shift in range(1, replicas):
+            total = total + from_copies(values, shift)
+        values = total
+        for shift in range(1, group):
+            total = total + from_spots(values, shift)
+        values = total
+        for shift in range(1, lines):
+            total = total + from_lines(values, shift, range(lines))
+        return total
+
+    def sum_copies(tile_list):
+        parts = [tile.reshape(tile.shape[:-2] + (replicas, -1, width)) for tile in tile_list]
+        merge = jnp.stack if parts[0].ndim == 3 else jnp.concatenate
+
+        def part_of(index):
+            return merge([pick(tile, index, tile.ndim - 3) for tile in parts])
+
+        total = part_of(my_copy).astype(full_type)
+        for shift in range(1, replicas):
+            total = total + from_copies(part_of((my_copy + shift) % replicas), shift).astype(full_type)
+        return total.astype(low_type)
+
+    def sum_spots(low):
+        total = pick(low, my_spot, 0).astype(full_type)
+        for shift in range(1, group):
+            sent_tile = pick(low, (my_spot + shift) % group, 0)
+            total = total + from_spots(sent_tile, shift).astype(full_type)
+        return total.astype(low_type)
+
+    def sum_lines(group_sums, first_line):
+        last = len(group_sums) - 1
+        stacked = jnp.stack(group_sums)
+        targets = range(first_line, first_line + last + 1)
+
+        def sum_for(line):
+            return pick(stacked, jnp.clip(line - first_line, 0, last), 0)
+
+        total = sum_for(my_line).astype(full_type)
+        for shift in range(1, lines):
+            moved = from_lines(sum_for((my_line + shift) % lines), shift, targets)
+            total = total + moved.astype(full_type)
+        return total
+
     def outgoing(values):
         spare = owners - tiles
         return jnp.pad(values, ((0, spare),) + ((0, 0),) * (values.ndim - 1)) if spare else values
-
-    packed = jnp.stack([left_basis, right_basis, first_moment, second_moment], axis=1)
-    packed = lax.all_to_all(
-        outgoing(packed.astype(low_type)), "zero", split_axis=0, concat_axis=0, tiled=True
-    )
-    packed = packed.transpose(1, 0, 2, 3).reshape(4, width, width)
 
     positions = jnp.arange(length, dtype=jnp.int32)
     mask_hits = mask_pos[:, :, None] == positions[None, None, :]
     masked = jnp.any(mask_hits, axis=1).reshape(-1, 1)
     row_ids = jnp.sum(jnp.where(mask_hits, repl_id[:, :, None], 0), axis=1).reshape(-1)
     inputs = jnp.where(masked, jnp.take(replace_embed, row_ids, axis=0), tokens)
-    whole, packed, inputs = lax.optimization_barrier((whole, packed, inputs))
-    left_low, right_low, moment_one_low, moment_two_low = packed
+    packed = jnp.stack([left_basis, right_basis, first_moment, second_moment], axis=1)
+    packed = lax.dynamic_slice_in_dim(packed, my_copy * part, part, 2).astype(low_type)
+    whole, inputs, packed = lax.optimization_barrier((whole, inputs, outgoing(packed)))
+    packed = lax.all_to_all(packed, "zero", split_axis=0, concat_axis=0, tiled=True)
     gains = norm_whole.astype(full_type)
 
     slopes = jnp.asarray(alibi_slopes(heads))
@@ -138,6 +212,7 @@
     inner_low = (act * up).astype(low_type)
     inner_low, act, up_slope = lax.optimization_barrier((inner_low, act, up * slope))
     branch = dot32("tfe,fed->td", inner_low, whole[4 + 2 * ff :])
+    branch, packed = lax.optimization_barrier((branch, packed))
     unit_two, rstd_two = norm_stats(hidden + branch)
     layer_out = (unit_two * gains[2] + gains[3]).astype(low_type)
 
@@ -146,16 +221,29 @@
     )
     d_branch = d_second.astype(low_type)
     grad_down = dot32("tfe,td->fed", inner_low, d_branch).astype(low_type)
+    d_branch, grad_down = lax.optimization_barrier((d_branch, grad_down))
+    down_low = sum_copies([grad_down])
+    packed = join_copies(packed)
     d_inner = dot32("td,fed->tfe", d_branch, whole[4 + 2 * ff :])
     d_gate = (d_inner * up_slope).astype(low_type)
     d_up = (d_inner * act).astype(low_type)
+    d_gate, d_up, down_low, packed = lax.optimization_barrier((d_gate, d_up, down_low, packed))
+    down_sum = sum_spots(down_low)
     grad_gate = dot32("td,tfe->fde", hidden_low, d_gate).astype(low_type)
     grad_up = dot32("td,tfe->fde", hidden_low, d_up).astype(low_type)
+    d_gate, d_up, grad_gate, grad_up, down_sum = lax.optimization_barrier(
+        (d_gate, d_up, grad_gate, grad_up, down_sum)
+    )
+    gate_low = sum_copies([grad_gate])
+    up_low = sum_copies([grad_up])
     d_hidden = (
         d_second
         + dot32("tfe,fde->td", d_gate, whole[4 : 4 + ff])
         + dot32("tfe,fde->td", d_up, whole[4 + ff : 4 + 2 * ff])
     )
+    d_hidden, gate_low, up_low = lax.optimization_barrier((d_hidden, gate_low, up_low))
+    gate_sum = sum_spots(gate_low)
+    up_sum = sum_spots(up_low)
     d_first, d_gain_one, d_shift_one = norm_back(d_hidden, unit_one, rstd_one, gains[0])
     d_attended = d_first.astype(low_type)
     grad_out = dot32("td,te->de", mixed, d_attended).astype(low_type)
@@ -163,28 +251,31 @@
     d_probs = dot32("bqhd,bkhd->bhqk", d_mixed, values)
     row_delta = jnp.sum(probs * d_probs, axis=-1, keepdims=True)
     d_scores = (probs * (d_probs - row_delta)).astype(low_type)
+    d_scores, gate_sum, up_sum = lax.optimization_barrier((d_scores, gate_sum, up_sum))
+    ff_total = sum_lines([gate_sum, up_sum, down_sum], 1)
+    norm_sum = sum_everywhere(jnp.stack([d_gain_one, d_shift_one, d_gain_two, d_shift_two]))
     d_query = dot32("bhqk,bkhd->bqhd", d_scores, key_rows) * scale
     d_keys = dot32("bhqk,bqhd->bkhd", d_scores, queries) * scale
     d_values = dot32("bhqk,bqhd->bkhd", soft_low, d_mixed)
     d_qkv = [
         grad.astype(low_type).reshape(tok_rows, width) for grad in (d_query, d_keys, d_values)
     ]
-    grad_qkv = [dot32("td,te->de", inputs, grad).astype(low_type)[None] for grad in d_qkv]
+    *d_qkv, norm_sum = lax.optimization_barrier((*d_qkv, norm_sum))
+    grad_qkv = [dot32("td,te->de", inputs, grad).astype(low_type) for grad in d_qkv]
     d_inputs = d_first
     for k in range(3):
         d_inputs = d_inputs + dot32("te,de->td", d_qkv[k], whole[k])
     in_grad = jnp.where(masked, 0.0, d_inputs)
 
-    tile_grads = jnp.concatenate(
-        grad_qkv + [grad_out[None], grad_gate, grad_up, grad_down], axis=0
-    )
-    norm_grads = jnp.stack([d_gain_one, d_shift_one, d_gain_two, d_shift_two])
-    norm_sum = lax.psum(norm_grads, ("dp", "zero"))
-    norm_sum = lax.dynamic_slice_in_dim(norm_sum, my_rows * norm_params.shape[1], norm_params.shape[1], 1)
-    flat_grads = outgoing(tile_grads).reshape(owners * width, width)
-    tile_part = lax.psum_scatter(flat_grads, ("zero", "dp"), scatter_dimension=0, tiled=True)
-    tile_part, in_grad, norm_sum = lax.optimization_barrier((tile_part, in_grad, norm_sum))
-    tile_sum = lax.all_gather(tile_part, "dp", axis=0, tiled=True)
+    columns = norm_params.shape[1]
+    norm_sum = lax.dynamic_slice_in_dim(norm_sum, my_rows * columns, columns, 1)
+    *grad_qkv, ff_total = lax.optimization_barrier((*grad_qkv, ff_total))
+    attention_low = sum_copies(grad_qkv + [grad_out])
+    attention_total = sum_lines([sum_spots(attention_low)], 0)
+    mine = jnp.where(my_line == 0, attention_total, ff_total).astype(low_type)
+    tile_sum = join_copies(mine).reshape(width, width)
+    packed = packed.transpose(2, 1, 0, 3, 4).reshape(4, width, width)
+    left_low, right_low, moment_one_low, moment_two_low = packed
 
     step_value = step[0].astype(full_type)
     step_rate = peak_rate * jnp.minimum(
@@ -202,12 +293,11 @@
     turned = dot32("ij,jl->il", left_low, high) + dot32("ij,jl->il", left_low, rest)
     high, rest = two_parts(turned)
     update = dot32("il,ml->im", high, right_low) + dot32("il,ml->im", rest, right_low)
-    results = jnp.stack(
-        [rotated.astype(low_type).reshape(owners, rows, width),
-         update.astype(low_type).reshape(owners, rows, width)], axis=1
-    )
+    results = jnp.stack([rotated, update]).reshape(2, owners, replicas, part, width)
+    results = pick(results, my_copy, 2).astype(low_type).transpose(1, 0, 2, 3)
     returned = lax.all_to_all(results, "zero", split_axis=0, concat_axis=0, tiled=True)[:tiles]
-    returned = returned.astype(full_type)
+    returned = join_copies(returned).transpose(1, 2, 0, 3, 4)
+    returned = returned.reshape(tiles, 2, rows, width).astype(full_type)
     turned_rows = returned[:, 0]
     new_first = beta_one * first_moment + (1.0 - beta_one) * turned_rows
     new_second = beta_two * second_moment + (1.0 - beta_two) * turned_rows * turned_rows

time: 748 us -> 750 us (level)
  blocking collectives: 217 us -> 43.3 us
  local copies, waits for them, and re-layouts: 65.2 us -> 163 us
  starting transfers between devices: 15.7 us -> 57.6 us
  other arithmetic: 27.3 us -> 60.6 us
  waiting for transfers between devices: 234 us -> 253 us
  matrix products: 159 us -> 147 us
    reduce_scatter x1 -> x0, waiting for transfers between devices: 158 us -> none  [shards(): lax.psum_scatter(flat_grads, ('zero', 'dp'), scatter_dimension=0, tiled=T...]
    ppermute x0 -> x32, waiting for transfers between devices: none -> 155 us  [the longest x15 80 us: from_spots(): return lax.ppermute(values, 'zero', pairs)]
    all_gather x1, blocking collectives: 148 us -> 43.3 us  [shards(): lax.all_gather(norm_params.astype(low_type), 'zero', axis=1, tiled=True)]
    psum x1 -> x0, blocking collectives: 69.3 us -> none  [shards(): norm_sum = lax.psum(norm_grads, ('dp', 'zero'))]
    dynamic_slice x1 -> x8, local copies, waits for them, and re-layouts: 0.07 us -> 50.1 us  [pick(): return lax.dynamic_index_in_dim(values, index, axis, keepdims=False)]
    ppermute x0 -> x32, starting transfers between devices: none -> 48.3 us  [the longest x9 26 us: from_lines(): lax.ppermute(values, 'zero', [(i, k) for i, k in pairs if k // group in t...]
    all_gather x1, waiting for transfers between devices: 24.7 us -> 64.1 us  [shards(): whole = lax.all_gather(sent, ('zero', 'dp'), axis=1, tiled=True)]
    all_to_all x1, waiting for transfers between devices: 42.1 us -> 21.1 us  [shards(): lax.all_to_all(results, 'zero', split_axis=0, concat_axis=0, tiled=True)]
  transfers between devices with their start and end apart: 5 -> 35, of which waited for: 4 -> 16; matrix products, arithmetic and copies ran while one was open for 6% -> 25% of each run, Pallas kernels for 0% -> 0%
where the time goes in v2:
time: 750 us; the launch traced here: 740 us
  waiting for transfers between devices  253 us (34%)
  local copies, waits for them, and re-layouts  163 us (22%)
  matrix products  147 us (20%)
  other arithmetic  60.6 us (8%)
  starting transfers between devices  57.6 us (8%)
  blocking collectives  43.3 us (6%)
  between operations  16.5 us (2%)
    dot_general x34, matrix products, dot32(): return jnp.einsum(spec, left, right, preferred_element_type=full_type)  147 us
    ppermute x15, waiting for transfers between devices, from_spots(): return lax.ppermute(values, 'zero', pairs)  80 us
    ppermute x9, waiting for transfers between devices, from_lines(): lax.ppermute(values, 'zero', [(i, k) for i, k in pairs if k // group in t...  70.3 us
    all_gather x1, waiting for transfers between devices, shards(): whole = lax.all_gather(sent, ('zero', 'dp'), axis=1, tiled=True)  64.1 us
    unnamed x139, local copies, waits for them, and re-layouts  51.3 us
    dynamic_slice x8, local copies, waits for them, and re-layouts, pick(): return lax.dynamic_index_in_dim(values, index, axis, keepdims=False)  50.1 us
    all_gather x1, blocking collectives, shards(): lax.all_gather(norm_params.astype(low_type), 'zero', axis=1, tiled=True)  43.3 us
    ppermute x9, starting transfers between devices, from_lines(): lax.ppermute(values, 'zero', [(i, k) for i, k in pairs if k // group in t...  26 us
  transfers between devices with their start and end apart: 35, of which 16 were waited for; matrix products, arithmetic and copies ran while one was open for 25% of the time, Pallas kernels for 0%

profile of v2, /device:TPU:0, one launch (start us, length us, event | category | flops | bytes accessed | tf_op | source)
XLA Modules:
  0.0 740.2 jit_solution(15061356343327602651)
XLA Ops:
  25.1 43.3 %all-gather = bf16[16,48,4]{1,2,0:T(4,128)(2,1)S(1)} all-gather(bf16[1,48,4]{1,2,0:T(4,128)(2,1)S(1)} %convert_bitcast_fusion.2), channel_id=1, replica_groups=mesh['dp'=2,'zero'=16] {'zero'}, dimensions={0}, use_global_device_ids=true | all-gather | bytes 6528 | tf_op jit(solution)/shard_map/all_gather | solution.py:94
  74.4 64.1 %all-gather.3.cloned.1.call-done = bf16[16,768,768]{2,1,0:T(8,128)(2,1)} async-done(((bf16[16,24,768]{2,1,0:T(8,128)(2,1)}), bf16[16,768,768]{2,1,0:T(8,128)(2,1)}) %all-gather.3.cloned.1.call-update) | async-done | bytes 18874384 | tf_op jit(solution)/shard_map/all_gather | solution.py:93
  189.3 15.4 %multiply_convert_fusion.2 = (bf16[1024,4,768]{2,0,1:T(8,128)(2,1)}, f32[1024,4,768]{2,0,1:T(8,128)}, f32[1024,4,768]{2,0,1:T(8,128)}) fusion(f32[1024,4,768]{2,0,1:T(8,128)S(1)} %fusion.28, bf16[1024,768,1]{0,1,2:T(8,128)(2,1)S(1)} %fusion.61, bf16[16,768,768]{2,1,0:T(8,128)(2,1)} %all-gather.3.cloned.1.call-done), kind=kOutput, calls=%fused_computation.10 | convolution fusion | flops 4869586944 | bytes 50331648 | tf_op jit(solution)/shard_map/td,fde->tfe/dot_general | solution.py:52
  204.7 9.7 %fusion.58 = f32[1024,768]{1,0:T(8,128)} fusion(bf16[1024,4,768]{2,0,1:T(8,128)(2,1)} %get-tuple-element.44, bf16[16,768,768]{2,1,0:T(8,128)(2,1)} %all-gather.3.cloned.1.call-done), kind=kOutput, calls=%fused_computation.118 | convolution fusion | flops 4831838208 | bytes 14155776 | tf_op jit(solution)/shard_map/tfe,fed->td/dot_general | solution.py:52
  214.3 12.6 %all-to-all-done = bf16[16,4,24,768]{3,2,1,0:T(8,128)(2,1)} async-done(((bf16[16,4,24,768]{3,2,1,0:T(8,128)(2,1)}), bf16[16,4,24,768]{3,2,1,0:T(8,128)(2,1)}, u32[]{:S(2)}, u32[]{:S(2)}) %all-to-all-start) | async-done | bytes 2359328 | tf_op jit(solution)/shard_map/all_to_all | solution.py:186
  252.4 15.6 %multiply_convert_fusion = (bf16[1024,4,768]{2,0,1:T(8,128)(2,1)}, bf16[1024,4,768]{2,0,1:T(8,128)(2,1)}) fusion(f32[1024,4,768]{2,0,1:T(8,128)} %get-tuple-element.49, f32[1024,4,768]{2,0,1:T(8,128)} %get-tuple-element.48, bf16[16,768,768]{2,1,0:T(8,128)(2,1)} %all-gather.3.cloned.1.call-done, bf16[1024,768]{0,1:T(8,128)(2,1)} %copy-done.27), kind=kOutput, calls=%fused_computation.8 | convolution fusion | flops 4844421120 | bytes 44040192 | tf_op jit(solution)/shard_map/td,fed->tfe/dot_general | solution.py:52
  303.5 13.8 %collective-permute-done.3 = bf16[384,768]{1,0:T(8,128)(2,1)S(1)} collective-permute-done((bf16[384,768]{1,0:T(8,128)(2,1)S(1)}, bf16[384,768]{1,0:T(8,128)(2,1)S(1)}, u32[]{:S(2)}, u32[]{:S(2)}) %collective-permute-start.3) | collective-permute-done | bytes 589856 | tf_op jit(solution)/shard_map/ppermute | solution.py:109
  326.5 10.1 %reshape.246 = bf16[4,2,384,768]{2,1,3,0:T(2,128)(2,1)} reshape(bf16[4,768,768]{1,2,0:T(8,128)(2,1)} %convert_bitcast_fusion.1) | data formatting | bytes 9437184 | tf_op jit(solution)/shard_map/reshape | solution.py:142
  336.7 13.1 %constant_dynamic-slice_fusion.11 = (bf16[4,1,384,768]{2,1,3,0:T(2,128)(2,1)}, bf16[4,1,384,768]{2,1,3,0:T(2,128)(2,1)}) fusion(bf16[4,2,384,768]{2,1,3,0:T(2,128)(2,1)} %reshape.246, s32[]{:T(128)S(6)} %select_n.215, s32[]{:T(128)S(6)} %select_n.217), kind=kLoop, calls=%fused_computation.248 | loop fusion | bytes 9437192 | tf_op jit(solution)/shard_map/jit(dynamic_index_in_dim)/dynamic_slice | solution.py:101
  349.8 11.7 %copy.294 = bf16[4,1,384,768]{3,2,0,1:T(8,128)(2,1)} copy(bf16[4,1,384,768]{2,1,3,0:T(2,128)(2,1)} %get-tuple-element.162) | data formatting | bytes 4718592 | tf_op jit(solution)/shard_map/jit(dynamic_index_in_dim)/dynamic_slice | solution.py:101
  361.5 11.8 %copy.344 = bf16[4,1,384,768]{3,2,0,1:T(8,128)(2,1)} copy(bf16[4,1,384,768]{2,1,3,0:T(2,128)(2,1)} %get-tuple-element.161) | data formatting | bytes 4718592
  373.3 10.1 %reshape.247 = bf16[4,2,384,768]{2,1,3,0:T(2,128)(2,1)} reshape(bf16[4,768,768]{1,2,0:T(8,128)(2,1)} %convert_bitcast_fusion) | data formatting | bytes 9437184 | tf_op jit(solution)/shard_map/reshape | solution.py:142
  383.4 13.3 %constant_dynamic-slice_fusion.9 = (bf16[4,1,384,768]{2,1,3,0:T(2,128)(2,1)}, bf16[4,1,384,768]{2,1,3,0:T(2,128)(2,1)}) fusion(bf16[4,2,384,768]{2,1,3,0:T(2,128)(2,1)} %reshape.247, s32[]{:T(128)S(6)} %select_n.215, s32[]{:T(128)S(6)} %select_n.217), kind=kLoop, calls=%fused_computation.246 | loop fusion | bytes 9437192 | tf_op jit(solution)/shard_map/jit(dynamic_index_in_dim)/dynamic_slice | solution.py:101
  396.6 11.7 %copy.296 = bf16[4,1,384,768]{3,2,0,1:T(8,128)(2,1)} copy(bf16[4,1,384,768]{2,1,3,0:T(2,128)(2,1)} %get-tuple-element.160) | data formatting | bytes 4718592 | tf_op jit(solution)/shard_map/jit(dynamic_index_in_dim)/dynamic_slice | solution.py:101
  408.8 11.7 %copy.345 = bf16[4,1,384,768]{3,2,0,1:T(8,128)(2,1)} copy(bf16[4,1,384,768]{2,1,3,0:T(2,128)(2,1)} %get-tuple-element.159) | data formatting | bytes 4718592
  420.5 10.7 %bitcast_add_fusion = f32[1024,768]{0,1:T(8,128)S(1)} fusion(f32[1024,768,1]{0,1,2:T(8,128)} %fusion.22, bf16[1024,4,768]{2,0,1:T(8,128)(2,1)} %get-tuple-element.55, bf16[16,768,768]{2,1,0:T(8,128)(2,1)} %all-gather.3.cloned.1.call-done, f32[1024]{0:T(1024)S(1)} %get-tuple-element.200, f32[1024,768]{0,1:T(8,128)} %copy-done.1, ...), kind=kOutput, calls=%fused_computation.70 | convolution fusion | flops 4839702528 | bytes 22039552 | tf_op jit(solution)/shard_map/tfe,fde->td/dot_general | solution.py:52
  453.4 13.3 %multiply_convert_fusion.3 = bf16[8,12,128,128]{2,3,1,0:T(8,128)(2,1)} fusion(f32[8,12,128,128]{2,3,1,0:T(8,128)} %fusion.77, f32[8,12,128,128]{2,3,1,0:T(8,128)} %copy-done, f32[8,12,128]{2,1,0:T(8,128)S(1)} %copy-done.43, f32[12,128,128]{1,2,0:T(8,128)S(1)} %copy-done.3), kind=kOutput, calls=%fused_computation.16 | output fusion | flops 15741055 | bytes 16564224 | tf_op jit(solution)/shard_map/sub | solution.py:253
  506.0 10.8 %collective-permute-done.12 = bf16[384,768]{1,0:T(8,128)(2,1)S(1)} collective-permute-done((bf16[384,768]{1,0:T(8,128)(2,1)S(1)}, bf16[384,768]{1,0:T(8,128)(2,1)S(1)}, u32[]{:S(2)}, u32[]{:S(2)}) %collective-permute-start.12) | collective-permute-done | bytes 589856 | tf_op jit(solution)/shard_map/ppermute | solution.py:109
  516.8 13.4 %collective-permute-done.11 = bf16[384,768]{1,0:T(8,128)(2,1)S(1)} collective-permute-done((bf16[384,768]{1,0:T(8,128)(2,1)S(1)}, bf16[384,768]{1,0:T(8,128)(2,1)S(1)}, u32[]{:S(2)}, u32[]{:S(2)}) %collective-permute-start.11) | collective-permute-done | bytes 589856 | tf_op jit(solution)/shard_map/ppermute | solution.py:109
  562.3 12.6 %collective-permute-done.21 = bf16[384,768]{1,0:T(8,128)(2,1)S(1)} collective-permute-done((bf16[384,768]{1,0:T(8,128)(2,1)S(1)}, bf16[384,768]{1,0:T(8,128)(2,1)S(1)}, u32[]{:S(2)}, u32[]{:S(2)}) %collective-permute-start.21) | collective-permute-done | bytes 589856 | tf_op jit(solution)/shard_map/ppermute | solution.py:113
  594.4 12.8 %collective-permute-done.26 = bf16[384,768]{1,0:T(8,128)(2,1)S(1)} collective-permute-done((bf16[384,768]{1,0:T(8,128)(2,1)S(1)}, bf16[384,768]{1,0:T(8,128)(2,1)S(1)}, u32[]{:S(2)}, u32[]{:S(2)}) %collective-permute-start.26) | collective-permute-done | bytes 589856 | tf_op jit(solution)/shard_map/ppermute | solution.py:109
  607.2 14.0 %collective-permute-done.25 = bf16[384,768]{1,0:T(8,128)(2,1)S(1)} collective-permute-done((bf16[384,768]{1,0:T(8,128)(2,1)S(1)}, bf16[384,768]{1,0:T(8,128)(2,1)S(1)}, u32[]{:S(2)}, u32[]{:S(2)}) %collective-permute-start.25) | collective-permute-done | bytes 589856 | tf_op jit(solution)/shard_map/ppermute | solution.py:109
  626.1 41.8 %collective-permute-done.29 = bf16[384,768]{1,0:T(8,128)(2,1)} collective-permute-done((bf16[384,768]{1,0:T(8,128)(2,1)S(1)}, bf16[384,768]{1,0:T(8,128)(2,1)}, u32[]{:S(2)}, u32[]{:S(2)}) %collective-permute-start.29) | collective-permute-done | bytes 589856 | tf_op jit(solution)/shard_map/ppermute | solution.py:113
  693.5 21.1 %all-to-all-done.1 = bf16[16,2,24,768]{3,2,1,0:T(8,128)(2,1)} async-done(((bf16[16,2,24,768]{3,2,1,0:T(8,128)(2,1)}), bf16[16,2,24,768]{3,2,1,0:T(8,128)(2,1)}, u32[]{:S(2)}, u32[]{:S(2)}) %all-to-all-start.1) | async-done | bytes 1179680 | tf_op jit(solution)/shard_map/all_to_all | solution.py:298
  (317 shorter events, 305.4 us)
Async XLA Ops:
  7.2 131.2 %all-gather.3.cloned.1.call-start = ((), (), s32[]{:S(2)}) async-start(), calls=%async_computation.2 | async-start | bytes 19464192 | tf_op jit(solution)/shard_map/all_gather | solution.py:93
  174.7 52.2 %all-to-all-start = ((bf16[16,4,24,768]{3,2,1,0:T(8,128)(2,1)}), bf16[16,4,24,768]{3,2,1,0:T(8,128)(2,1)}, u32[]{:S(2)}, u32[]{:S(2)}) async-start(bf16[16,4,24,768]{3,2,1,0:T(8,128)(2,1)} %fusion.11), calls=%async_computation | async-start | bytes 4718592 | tf_op jit(solution)/shard_map/all_to_all | solution.py:186
  250.3 17.7 %collective-permute-start.1 = (bf16[16,4,24,768]{3,2,0,1:T(8,128)(2,1)}, bf16[16,4,24,768]{3,2,0,1:T(8,128)(2,1)}, u32[]{:S(2)}, u32[]{:S(2)}) collective-permute-start(bf16[16,4,24,768]{3,2,0,1:T(8,128)(2,1)} %copy.284), channel_id=1, source_target_pairs={{0,16},{16,0},{1,17},{17,1},{2,18},{18,2},{3,19},{19,3},{4,20},{20... | collective-permute-start | bytes 7077896 | tf_op jit(solution)/shard_map/ppermute | solution.py:105
  251.9 21.8 %collective-permute-start = (bf16[4,384,768]{2,1,0:T(8,128)(2,1)}, bf16[4,384,768]{2,1,0:T(8,128)(2,1)}, u32[]{:S(2)}, u32[]{:S(2)}) collective-permute-start(bf16[4,384,768]{2,1,0:T(8,128)(2,1)} %dynamic-slice_bitcast_fusion), channel_id=1, source_target_pairs={{0,16},{16,0},{1,17},{17,1},{2,18},{18,2},{3,19},{19,3},{4,20},{20... | collective-permute-start | bytes 7077896 | tf_op jit(solution)/shard_map/ppermute | solution.py:105
  284.3 19.2 %collective-permute-start.4 = (bf16[384,768]{1,0:T(8,128)(2,1)S(1)}, bf16[384,768]{1,0:T(8,128)(2,1)S(1)}, u32[]{:S(2)}, u32[]{:S(2)}) collective-permute-start(bf16[384,768]{1,0:T(8,128)(2,1)S(1)} %get-tuple-element.179), channel_id=1, source_target_pairs={{0,3},{1,0},{2,1},{3,2},{4,7},{5,4},{6,5},{7,6},{8,11},{9,8},{10,9... | collective-permute-start | bytes 1769480 | tf_op jit(solution)/shard_map/ppermute | solution.py:109
  289.7 27.6 %collective-permute-start.3 = (bf16[384,768]{1,0:T(8,128)(2,1)S(1)}, bf16[384,768]{1,0:T(8,128)(2,1)S(1)}, u32[]{:S(2)}, u32[]{:S(2)}) collective-permute-start(bf16[384,768]{1,0:T(8,128)(2,1)S(1)} %get-tuple-element.180), channel_id=1, source_target_pairs={{0,2},{1,3},{2,0},{3,1},{4,6},{5,7},{6,4},{7,5},{8,10},{9,11},{10,... | collective-permute-start | bytes 1769480 | tf_op jit(solution)/shard_map/ppermute | solution.py:109
  289.7 27.6 %collective-permute-start.2 = (bf16[384,768]{1,0:T(8,128)(2,1)S(1)}, bf16[384,768]{1,0:T(8,128)(2,1)S(1)}, u32[]{:S(2)}, u32[]{:S(2)}) collective-permute-start(bf16[384,768]{1,0:T(8,128)(2,1)S(1)} %get-tuple-element.178), channel_id=1, source_target_pairs={{0,1},{1,2},{2,3},{3,0},{4,5},{5,6},{6,7},{7,4},{8,9},{9,10},{10,1... | collective-permute-start | bytes 1769480 | tf_op jit(solution)/shard_map/ppermute | solution.py:109
  361.5 69.7 %collective-permute-start.5 = (bf16[4,384,768]{2,1,0:T(8,128)(2,1)}, bf16[4,384,768]{2,1,0:T(8,128)(2,1)}, u32[]{:S(2)}, u32[]{:S(2)}) collective-permute-start(bf16[4,384,768]{2,1,0:T(8,128)(2,1)} %bitcast.318), channel_id=1, source_target_pairs={{0,16},{16,0},{1,17},{17,1},{2,18},{18,2},{3,19},{19,3},{4,20},{20... | collective-permute-start | bytes 7077896 | tf_op jit(solution)/shard_map/ppermute | solution.py:105
  408.3 26.7 %collective-permute-start.6 = (bf16[4,384,768]{2,1,0:T(8,128)(2,1)}, bf16[4,384,768]{2,1,0:T(8,128)(2,1)}, u32[]{:S(2)}, u32[]{:S(2)}) collective-permute-start(bf16[4,384,768]{2,1,0:T(8,128)(2,1)} %bitcast.319), channel_id=1, source_target_pairs={{0,16},{16,0},{1,17},{17,1},{2,18},{18,2},{3,19},{19,3},{4,20},{20... | collective-permute-start | bytes 7077896 | tf_op jit(solution)/shard_map/ppermute | solution.py:105
  474.7 20.4 %collective-permute-start.9 = (bf16[384,768]{1,0:T(8,128)(2,1)S(1)}, bf16[384,768]{1,0:T(8,128)(2,1)S(1)}, u32[]{:S(2)}, u32[]{:S(2)}) collective-permute-start(bf16[384,768]{1,0:T(8,128)(2,1)S(1)} %get-tuple-element.176), channel_id=1, source_target_pairs={{0,3},{1,0},{2,1},{3,2},{4,7},{5,4},{6,5},{7,6},{8,11},{9,8},{10,9... | collective-permute-start | bytes 1769480 | tf_op jit(solution)/shard_map/ppermute | solution.py:109
  477.6 28.1 %collective-permute-start.8 = (bf16[384,768]{1,0:T(8,128)(2,1)S(1)}, bf16[384,768]{1,0:T(8,128)(2,1)S(1)}, u32[]{:S(2)}, u32[]{:S(2)}) collective-permute-start(bf16[384,768]{1,0:T(8,128)(2,1)S(1)} %get-tuple-element.177), channel_id=1, source_target_pairs={{0,2},{1,3},{2,0},{3,1},{4,6},{5,7},{6,4},{7,5},{8,10},{9,11},{10,... | collective-permute-start | bytes 1769480 | tf_op jit(solution)/shard_map/ppermute | solution.py:109
  478.2 27.5 %collective-permute-start.7 = (bf16[384,768]{1,0:T(8,128)(2,1)S(1)}, bf16[384,768]{1,0:T(8,128)(2,1)S(1)}, u32[]{:S(2)}, u32[]{:S(2)}) collective-permute-start(bf16[384,768]{1,0:T(8,128)(2,1)S(1)} %get-tuple-element.175), channel_id=1, source_target_pairs={{0,1},{1,2},{2,3},{3,0},{4,5},{5,6},{6,7},{7,4},{8,9},{9,10},{10,1... | collective-permute-start | bytes 1769480 | tf_op jit(solution)/shard_map/ppermute | solution.py:109
  491.6 25.2 %collective-permute-start.12 = (bf16[384,768]{1,0:T(8,128)(2,1)S(1)}, bf16[384,768]{1,0:T(8,128)(2,1)S(1)}, u32[]{:S(2)}, u32[]{:S(2)}) collective-permute-start(bf16[384,768]{1,0:T(8,128)(2,1)S(1)} %get-tuple-element.173), channel_id=1, source_target_pairs={{0,3},{1,0},{2,1},{3,2},{4,7},{5,4},{6,5},{7,6},{8,11},{9,8},{10,9... | collective-permute-start | bytes 1769480 | tf_op jit(solution)/shard_map/ppermute | solution.py:109
  494.5 35.7 %collective-permute-start.11 = (bf16[384,768]{1,0:T(8,128)(2,1)S(1)}, bf16[384,768]{1,0:T(8,128)(2,1)S(1)}, u32[]{:S(2)}, u32[]{:S(2)}) collective-permute-start(bf16[384,768]{1,0:T(8,128)(2,1)S(1)} %get-tuple-element.174), channel_id=1, source_target_pairs={{0,2},{1,3},{2,0},{3,1},{4,6},{5,7},{6,4},{7,5},{8,10},{9,11},{10,... | collective-permute-start | bytes 1769480 | tf_op jit(solution)/shard_map/ppermute | solution.py:109
  495.1 35.1 %collective-permute-start.10 = (bf16[384,768]{1,0:T(8,128)(2,1)S(1)}, bf16[384,768]{1,0:T(8,128)(2,1)S(1)}, u32[]{:S(2)}, u32[]{:S(2)}) collective-permute-start(bf16[384,768]{1,0:T(8,128)(2,1)S(1)} %get-tuple-element.172), channel_id=1, source_target_pairs={{0,1},{1,2},{2,3},{3,0},{4,5},{5,6},{6,7},{7,4},{8,9},{9,10},{10,1... | collective-permute-start | bytes 1769480 | tf_op jit(solution)/shard_map/ppermute | solution.py:109
  540.3 22.0 %collective-permute-start.22 = (bf16[384,768]{1,0:T(8,128)(2,1)S(1)}, bf16[384,768]{1,0:T(8,128)(2,1)S(1)}, u32[]{:S(2)}, u32[]{:S(2)}) collective-permute-start(bf16[384,768]{1,0:T(8,128)(2,1)S(1)} %get-tuple-element.182), channel_id=1, source_target_pairs={{0,12},{1,13},{2,14},{3,15},{8,4},{9,5},{10,6},{11,7},{12,8},{13,9... | collective-permute-start | bytes 1769480 | tf_op jit(solution)/shard_map/ppermute | solution.py:113
  548.5 26.4 %collective-permute-start.21 = (bf16[384,768]{1,0:T(8,128)(2,1)S(1)}, bf16[384,768]{1,0:T(8,128)(2,1)S(1)}, u32[]{:S(2)}, u32[]{:S(2)}) collective-permute-start(bf16[384,768]{1,0:T(8,128)(2,1)S(1)} %get-tuple-element.183), channel_id=1, source_target_pairs={{0,8},{1,9},{2,10},{3,11},{4,12},{5,13},{6,14},{7,15},{12,4},{13,5... | collective-permute-start | bytes 1769480 | tf_op jit(solution)/shard_map/ppermute | solution.py:113
  551.8 32.8 %collective-permute-start.20 = (bf16[384,768]{1,0:T(8,128)(2,1)S(1)}, bf16[384,768]{1,0:T(8,128)(2,1)S(1)}, u32[]{:S(2)}, u32[]{:S(2)}) collective-permute-start(bf16[384,768]{1,0:T(8,128)(2,1)S(1)} %get-tuple-element.181), channel_id=1, source_target_pairs={{0,4},{1,5},{2,6},{3,7},{4,8},{5,9},{6,10},{7,11},{8,12},{9,13},{1... | collective-permute-start | bytes 1769480 | tf_op jit(solution)/shard_map/ppermute | solution.py:113
  593.5 27.7 %collective-permute-start.25 = (bf16[384,768]{1,0:T(8,128)(2,1)S(1)}, bf16[384,768]{1,0:T(8,128)(2,1)S(1)}, u32[]{:S(2)}, u32[]{:S(2)}) collective-permute-start(bf16[384,768]{1,0:T(8,128)(2,1)S(1)} %get-tuple-element.171), channel_id=1, source_target_pairs={{0,2},{1,3},{2,0},{3,1},{4,6},{5,7},{6,4},{7,5},{8,10},{9,11},{10,... | collective-permute-start | bytes 1769480 | tf_op jit(solution)/shard_map/ppermute | solution.py:109
  594.0 27.2 %collective-permute-start.24 = (bf16[384,768]{1,0:T(8,128)(2,1)S(1)}, bf16[384,768]{1,0:T(8,128)(2,1)S(1)}, u32[]{:S(2)}, u32[]{:S(2)}) collective-permute-start(bf16[384,768]{1,0:T(8,128)(2,1)S(1)} %get-tuple-element.169), channel_id=1, source_target_pairs={{0,1},{1,2},{2,3},{3,0},{4,5},{5,6},{6,7},{7,4},{8,9},{9,10},{10,1... | collective-permute-start | bytes 1769480 | tf_op jit(solution)/shard_map/ppermute | solution.py:109
  621.5 46.4 %collective-permute-start.29 = (bf16[384,768]{1,0:T(8,128)(2,1)S(1)}, bf16[384,768]{1,0:T(8,128)(2,1)}, u32[]{:S(2)}, u32[]{:S(2)}) collective-permute-start(bf16[384,768]{1,0:T(8,128)(2,1)S(1)} %fusion.95), channel_id=1, source_target_pairs={{4,0},{5,1},{6,2},{7,3},{20,16},{21,17},{22,18},{23,19}} | collective-permute-start | bytes 1769480 | tf_op jit(solution)/shard_map/ppermute | solution.py:113
  622.8 45.1 %collective-permute-start.28 = (bf16[384,768]{1,0:T(8,128)(2,1)S(1)}, bf16[384,768]{1,0:T(8,128)(2,1)}, u32[]{:S(2)}, u32[]{:S(2)}) collective-permute-start(bf16[384,768]{1,0:T(8,128)(2,1)S(1)} %fusion.95), channel_id=1, source_target_pairs={{8,0},{9,1},{10,2},{11,3},{24,16},{25,17},{26,18},{27,19}} | collective-permute-start | bytes 1769480 | tf_op jit(solution)/shard_map/ppermute | solution.py:113
  624.1 43.8 %collective-permute-start.27 = (bf16[384,768]{1,0:T(8,128)(2,1)S(1)}, bf16[384,768]{1,0:T(8,128)(2,1)}, u32[]{:S(2)}, u32[]{:S(2)}) collective-permute-start(bf16[384,768]{1,0:T(8,128)(2,1)S(1)} %fusion.95), channel_id=1, source_target_pairs={{12,0},{13,1},{14,2},{15,3},{28,16},{29,17},{30,18},{31,19}} | collective-permute-start | bytes 1769480 | tf_op jit(solution)/shard_map/ppermute | solution.py:113
  682.5 32.1 %all-to-all-start.1 = ((bf16[16,2,24,768]{3,2,1,0:T(8,128)(2,1)}), bf16[16,2,24,768]{3,2,1,0:T(8,128)(2,1)}, u32[]{:S(2)}, u32[]{:S(2)}) async-start(bf16[16,2,24,768]{3,2,1,0:T(8,128)(2,1)} %fusion.86), calls=%async_computation.1 | async-start | bytes 2359296 | tf_op jit(solution)/shard_map/all_to_all | solution.py:298
  (74 other events, 793.4 us)
Sparse Core Ops, SparseCore 0:
  11.5 126.8 all-gather.2

commit v3 on v2

--- a/solution.py
+++ b/solution.py
@@ -5,6 +5,7 @@
 import numpy as np
 from jax import lax
 from jax.sharding import PartitionSpec as P
+
 
 HEADS = 12
 
@@ -108,9 +109,13 @@
         pairs = [(i, i - i % group + (i + shift) % group) for i in range(owners)]
         return lax.ppermute(values, "zero", pairs)
 
-    def from_lines(values, shift, targets):
+    def from_lines(values, shift):
         pairs = [(i, (i + shift * group) % owners) for i in range(owners)]
-        return lax.ppermute(values, "zero", [(i, k) for i, k in pairs if k // group in targets])
+        return lax.ppermute(values, "zero", pairs)
+
+    def from_line(values, line, shift):
+        pairs = [(i, (i + shift * group) % owners) for i in range(owners) if i // group == line]
+        return lax.ppermute(values, "zero", pairs)
 
     def join_copies(values):
         pieces = [values] + [from_copies(values, shift) for shift in range(1, replicas)]
@@ -135,7 +140,7 @@
             total = total + from_spots(values, shift)
         values = total
         for shift in range(1, lines):
-            total = total + from_lines(values, shift, range(lines))
+            total = total + from_lines(values, shift)
         return total
 
     def sum_copies(tile_list):
@@ -154,24 +159,19 @@
         total = pick(low, my_spot, 0).astype(full_type)
         for shift in range(1, group):
             sent_tile = pick(low, (my_spot + shift) % group, 0)
-            total = total + from_spots(sent_tile, shift).astype(full_type)
+            moved = from_spots(sent_tile, shift)
+            total = total + moved.astype(full_type)
         return total.astype(low_type)
 
-    def sum_lines(group_sums, first_line):
-        last = len(group_sums) - 1
-        stacked = jnp.stack(group_sums)
-        targets = range(first_line, first_line + last + 1)
-
-        def sum_for(line):
-            return pick(stacked, jnp.clip(line - first_line, 0, last), 0)
-
-        total = sum_for(my_line).astype(full_type)
+    def sum_lines(low, target):
+        total = low.astype(full_type)
         for shift in range(1, lines):
-            moved = from_lines(sum_for((my_line + shift) % lines), shift, targets)
+            moved = from_line(low, (target - shift) % lines, shift)
             total = total + moved.astype(full_type)
         return total
 
     def outgoing(values):
+        values = jnp.concatenate([values[tiles - group :], values[: tiles - group]])
         spare = owners - tiles
         return jnp.pad(values, ((0, spare),) + ((0, 0),) * (values.ndim - 1)) if spare else values
 
@@ -220,30 +220,35 @@
         out_grad.astype(full_type), unit_two, rstd_two, gains[2]
     )
     d_branch = d_second.astype(low_type)
-    grad_down = dot32("tfe,td->fed", inner_low, d_branch).astype(low_type)
+    grad_down = [
+        dot32("te,td->ed", inner_low[:, f], d_branch).astype(low_type) for f in range(ff)
+    ]
     d_branch, grad_down = lax.optimization_barrier((d_branch, grad_down))
-    down_low = sum_copies([grad_down])
+    down_low = sum_copies(grad_down)
     packed = join_copies(packed)
     d_inner = dot32("td,fed->tfe", d_branch, whole[4 + 2 * ff :])
     d_gate = (d_inner * up_slope).astype(low_type)
     d_up = (d_inner * act).astype(low_type)
     d_gate, d_up, down_low, packed = lax.optimization_barrier((d_gate, d_up, down_low, packed))
     down_sum = sum_spots(down_low)
-    grad_gate = dot32("td,tfe->fde", hidden_low, d_gate).astype(low_type)
-    grad_up = dot32("td,tfe->fde", hidden_low, d_up).astype(low_type)
+    grad_gate = [dot32("td,te->de", hidden_low, d_gate[:, f]).astype(low_type) for f in range(ff)]
+    grad_up = [dot32("td,te->de", hidden_low, d_up[:, f]).astype(low_type) for f in range(ff)]
     d_gate, d_up, grad_gate, grad_up, down_sum = lax.optimization_barrier(
         (d_gate, d_up, grad_gate, grad_up, down_sum)
     )
-    gate_low = sum_copies([grad_gate])
-    up_low = sum_copies([grad_up])
+    gate_low = sum_copies(grad_gate)
+    up_low = sum_copies(grad_up)
     d_hidden = (
         d_second
         + dot32("tfe,fde->td", d_gate, whole[4 : 4 + ff])
         + dot32("tfe,fde->td", d_up, whole[4 + ff : 4 + 2 * ff])
     )
     d_hidden, gate_low, up_low = lax.optimization_barrier((d_hidden, gate_low, up_low))
+    down_total = sum_lines(down_sum, 0)
     gate_sum = sum_spots(gate_low)
     up_sum = sum_spots(up_low)
+    gate_total = sum_lines(gate_sum, 2)
+    up_total = sum_lines(up_sum, 3)
     d_first, d_gain_one, d_shift_one = norm_back(d_hidden, unit_one, rstd_one, gains[0])
     d_attended = d_first.astype(low_type)
     grad_out = dot32("td,te->de", mixed, d_attended).astype(low_type)
@@ -251,8 +256,6 @@
     d_probs = dot32("bqhd,bkhd->bhqk", d_mixed, values)
     row_delta = jnp.sum(probs * d_probs, axis=-1, keepdims=True)
     d_scores = (probs * (d_probs - row_delta)).astype(low_type)
-    d_scores, gate_sum, up_sum = lax.optimization_barrier((d_scores, gate_sum, up_sum))
-    ff_total = sum_lines([gate_sum, up_sum, down_sum], 1)
     norm_sum = sum_everywhere(jnp.stack([d_gain_one, d_shift_one, d_gain_two, d_shift_two]))
     d_query = dot32("bhqk,bkhd->bqhd", d_scores, key_rows) * scale
     d_keys = dot32("bhqk,bqhd->bkhd", d_scores, queries) * scale
@@ -260,8 +263,10 @@
     d_qkv = [
         grad.astype(low_type).reshape(tok_rows, width) for grad in (d_query, d_keys, d_values)
     ]
-    *d_qkv, norm_sum = lax.optimization_barrier((*d_qkv, norm_sum))
-    grad_qkv = [dot32("td,te->de", inputs, grad).astype(low_type) for grad in d_qkv]
+    grad_values = dot32("td,te->de", inputs, d_qkv[2]).astype(low_type)
+    grad_keys = dot32("td,te->de", inputs, d_qkv[1]).astype(low_type)
+    grad_query = dot32("td,te->de", inputs, d_qkv[0]).astype(low_type)
+    grad_qkv = [grad_query, grad_keys, grad_values]
     d_inputs = d_first
     for k in range(3):
         d_inputs = d_inputs + dot32("te,de->td", d_qkv[k], whole[k])
@@ -269,10 +274,12 @@
 
     columns = norm_params.shape[1]
     norm_sum = lax.dynamic_slice_in_dim(norm_sum, my_rows * columns, columns, 1)
-    *grad_qkv, ff_total = lax.optimization_barrier((*grad_qkv, ff_total))
     attention_low = sum_copies(grad_qkv + [grad_out])
-    attention_total = sum_lines([sum_spots(attention_low)], 0)
-    mine = jnp.where(my_line == 0, attention_total, ff_total).astype(low_type)
+    mine = sum_lines(sum_spots(attention_low), 1)
+    mine, norm_sum = lax.optimization_barrier((mine, norm_sum))
+    mine = jnp.where(my_line == 0, down_total, mine)
+    mine = jnp.where(my_line == 2, gate_total, mine)
+    mine = jnp.where(my_line == 3, up_total, mine).astype(low_type)
     tile_sum = join_copies(mine).reshape(width, width)
     packed = packed.transpose(2, 1, 0, 3, 4).reshape(4, width, width)
     left_low, right_low, moment_one_low, moment_two_low = packed
@@ -295,7 +302,8 @@
     update = dot32("il,ml->im", high, right_low) + dot32("il,ml->im", rest, right_low)
     results = jnp.stack([rotated, update]).reshape(2, owners, replicas, part, width)
     results = pick(results, my_copy, 2).astype(low_type).transpose(1, 0, 2, 3)
-    returned = lax.all_to_all(results, "zero", split_axis=0, concat_axis=0, tiled=True)[:tiles]
+    returned = lax.all_to_all(results, "zero", split_axis=0, concat_axis=0, tiled=True)
+    returned = jnp.concatenate([returned[group:tiles], returned[:group]])
     returned = join_copies(returned).transpose(1, 2, 0, 3, 4)
     returned = returned.reshape(tiles, 2, rows, width).astype(full_type)
     turned_rows = returned[:, 0]

time: 750 us -> 660 us (0.88)
  local copies, waits for them, and re-layouts: 163 us -> 76.6 us
  starting transfers between devices: 57.6 us -> 79.2 us
  waiting for transfers between devices: 253 us -> 234 us
    dynamic_slice x8 -> x16, local copies, waits for them, and re-layouts: 50.1 us -> 9.53 us  [pick(): return lax.dynamic_index_in_dim(values, index, axis, keepdims=False)]
    all_to_all x1, starting transfers between devices: 4.59 us -> 34.8 us  [shards(): lax.all_to_all(results, 'zero', split_axis=0, concat_axis=0, tiled=True)]
    reshape x2 -> x0, local copies, waits for them, and re-layouts: 20.2 us -> none  [sum_copies(): tile.reshape(tile.shape[:-2] + (replicas, -1, width))]
    unnamed x139 -> x172, local copies, waits for them, and re-layouts: 51.3 us -> 31.9 us
    sub x1 -> x0, other arithmetic: 13.3 us -> none  [shards(): d_scores = (probs * (d_probs - row_delta)).astype(low_type)]
    ppermute x9 -> x15, waiting for transfers between devices: 70.3 us -> 60.5 us  [the longest x12 45.2 us: from_line(): return lax.ppermute(values, 'zero', pairs)]
    all_to_all x1, waiting for transfers between devices: 12.6 us -> 4.06 us  [shards(): lax.all_to_all(packed, 'zero', split_axis=0, concat_axis=0, tiled=True)]
    ppermute x9 -> x15, starting transfers between devices: 26 us -> 20.5 us  [the longest x12 20.5 us: from_line(): return lax.ppermute(values, 'zero', pairs)]
  transfers between devices with their start and end apart: 35 -> 41, of which waited for: 16 -> 18; matrix products, arithmetic and copies ran while one was open for 25% -> 19% of each run, Pallas kernels for 0% -> 0%
where the time goes in v3:
time: 660 us; the launch traced here: 651 us
  waiting for transfers between devices  234 us (35%)
  matrix products  146 us (22%)
  starting transfers between devices  79.2 us (12%)
  local copies, waits for them, and re-layouts  76.6 us (12%)
  other arithmetic  55 us (8%)
  blocking collectives  43.9 us (7%)
  between operations  16.9 us (3%)
    dot_general x43, matrix products, dot32(): return jnp.einsum(spec, left, right, preferred_element_type=full_type)  146 us
    ppermute x15, waiting for transfers between devices, from_spots(): return lax.ppermute(values, 'zero', pairs)  86.4 us
    all_gather x1, waiting for transfers between devices, shards(): whole = lax.all_gather(sent, ('zero', 'dp'), axis=1, tiled=True)  60.8 us
    ppermute x12, waiting for transfers between devices, from_line(): return lax.ppermute(values, 'zero', pairs)  45.2 us
    all_gather x1, blocking collectives, shards(): lax.all_gather(norm_params.astype(low_type), 'zero', axis=1, tiled=True)  43.9 us
    all_to_all x1, starting transfers between devices, shards(): lax.all_to_all(results, 'zero', split_axis=0, concat_axis=0, tiled=True)  34.8 us
    unnamed x172, local copies, waits for them, and re-layouts  31.9 us
    all_to_all x1, waiting for transfers between devices, shards(): lax.all_to_all(results, 'zero', split_axis=0, concat_axis=0, tiled=True)  20.7 us
  transfers between devices with their start and end apart: 41, of which 18 were waited for; matrix products, arithmetic and copies ran while one was open for 19% of the time, Pallas kernels for 0%

profile of v3, /device:TPU:0, one launch (start us, length us, event | category | flops | bytes accessed | tf_op | source)
XLA Modules:
  0.0 651.5 jit_solution(7393714248152309481)
XLA Ops:
  17.9 9.2 %gather_fusion = bf16[1024,768]{1,0:T(8,128)(2,1)} fusion(bf16[4096,768]{1,0:T(8,128)(2,1)} %param.19, s32[1024]{0:T(1024)S(1)} %broadcast_clamp_fusion), kind=kCustom, calls=%fused_computation | custom fusion | bytes 3149824 | tf_op jit(solution)/shard_map/jit(_take)/gather | solution.py:182
  29.8 43.9 %all-gather = bf16[16,48,4]{1,2,0:T(4,128)(2,1)S(1)} all-gather(bf16[1,48,4]{1,2,0:T(4,128)(2,1)S(1)} %convert_bitcast_fusion), channel_id=1, replica_groups=mesh['dp'=2,'zero'=16] {'zero'}, dimensions={0}, use_global_device_ids=true | all-gather | bytes 6528 | tf_op jit(solution)/shard_map/all_gather | solution.py:95
  77.0 60.8 %all-gather.3.cloned.1.call-done = bf16[16,768,768]{2,1,0:T(8,128)(2,1)} async-done(((bf16[16,24,768]{2,1,0:T(8,128)(2,1)}), bf16[16,768,768]{2,1,0:T(8,128)(2,1)}) %all-gather.3.cloned.1.call-update) | async-done | bytes 18874384 | tf_op jit(solution)/shard_map/all_gather | solution.py:94
  173.2 4.9 all-to-all-start
  178.6 10.9 %fusion.23 = f32[1024,4,768]{2,0,1:T(8,128)} fusion(bf16[16,768,768]{2,1,0:T(8,128)(2,1)} %all-gather.3.cloned.1.call-done, bf16[1024,768]{0,1:T(8,128)(2,1)S(1)} %fusion.31), kind=kOutput, calls=%fused_computation.48 | convolution fusion | flops 4831838208 | bytes 18874368 | tf_op jit(solution)/shard_map/td,fde->tfe/dot_general | solution.py:53
  189.5 19.9 %multiply_convert_fusion.2 = (bf16[1024,4,768]{2,0,1:T(8,128)(2,1)S(1)}, f32[1024,4,768]{2,0,1:T(8,128)}, f32[1024,4,768]{2,0,1:T(8,128)}) fusion(f32[1024,4,768]{2,0,1:T(8,128)} %fusion.23, bf16[16,768,768]{2,1,0:T(8,128)(2,1)} %all-gather.3.cloned.1.call-done, bf16[1024,768]{0,1:T(8,128)(2,1)S(1)} %fusion.31), kind=kOutput, calls=%fused_computation.9 | convolution fusion | flops 4869586944 | bytes 50331648 | tf_op jit(solution)/shard_map/td,fde->tfe/dot_general | solution.py:53
  212.0 9.6 %fusion.48 = f32[1024,768]{1,0:T(8,128)} fusion(bf16[1024,4,768]{2,0,1:T(8,128)(2,1)S(1)} %get-tuple-element.44, bf16[16,768,768]{2,1,0:T(8,128)(2,1)} %all-gather.3.cloned.1.call-done), kind=kOutput, calls=%fused_computation.110 | convolution fusion | flops 4831838208 | bytes 14155776 | tf_op jit(solution)/shard_map/tfe,fed->td/dot_general | solution.py:53
  253.2 15.9 %multiply_convert_fusion = (bf16[1024,4,768]{2,0,1:T(8,128)(2,1)}, bf16[1024,4,768]{2,0,1:T(8,128)(2,1)}) fusion(f32[1024,4,768]{2,0,1:T(8,128)} %get-tuple-element.49, f32[1024,4,768]{2,0,1:T(8,128)} %get-tuple-element.48, bf16[16,768,768]{2,1,0:T(8,128)(2,1)} %all-gather.3.cloned.1.call-done, bf16[1024,768]{0,1:T(8,128)(2,1)} %copy-done.27), kind=kOutput, calls=%fused_computation.7 | convolution fusion | flops 4844421120 | bytes 44040192 | tf_op jit(solution)/shard_map/td,fed->tfe/dot_general | solution.py:53
  286.1 5.5 collective-permute-start.4
  295.0 10.3 %collective-permute-done.4 = bf16[384,768]{1,0:T(8,128)(2,1)S(1)} collective-permute-done((bf16[384,768]{1,0:T(8,128)(2,1)S(1)}, bf16[384,768]{1,0:T(8,128)(2,1)S(1)}, u32[]{:S(2)}, u32[]{:S(2)}) %collective-permute-start.4) | collective-permute-done | bytes 589856 | tf_op jit(solution)/shard_map/ppermute | solution.py:110
  305.3 13.9 %collective-permute-done.3 = bf16[384,768]{1,0:T(8,128)(2,1)S(1)} collective-permute-done((bf16[384,768]{1,0:T(8,128)(2,1)S(1)}, bf16[384,768]{1,0:T(8,128)(2,1)S(1)}, u32[]{:S(2)}, u32[]{:S(2)}) %collective-permute-start.3) | collective-permute-done | bytes 589856 | tf_op jit(solution)/shard_map/ppermute | solution.py:110
  320.3 8.5 %fusion.17 = f32[1024,768,1]{0,1,2:T(8,128)} fusion(bf16[1024,4,768]{2,0,1:T(8,128)(2,1)S(1)} %bitcast.345, bf16[16,768,768]{2,1,0:T(8,128)(2,1)} %all-gather.3.cloned.1.call-done), kind=kOutput, calls=%fused_computation.42 | convolution fusion | flops 4831838208 | bytes 14155776 | tf_op jit(solution)/shard_map/tfe,fde->td/dot_general | solution.py:53
  339.4 7.9 %bitcast_add_fusion = f32[1024,768]{0,1:T(8,128)S(1)} fusion(f32[1024,768,1]{0,1,2:T(8,128)} %fusion.17, bf16[1024,4,768]{2,0,1:T(8,128)(2,1)S(1)} %bitcast.343, bf16[16,768,768]{2,1,0:T(8,128)(2,1)} %all-gather.3.cloned.1.call-done, f32[1024]{0:T(1024)S(1)} %get-tuple-element.219, f32[1024,768]{0,1:T(8,128)S(1)} %copy-done.2, ...), kind=kOutput, calls=%fused_computation.63 | convolution fusion | flops 4839702528 | bytes 22039552 | tf_op jit(solution)/shard_map/tfe,fde->td/dot_general | solution.py:53
  391.4 40.9 %collective-permute-done.21 = bf16[384,768]{1,0:T(8,128)(2,1)S(1)} collective-permute-done((bf16[384,768]{1,0:T(8,128)(2,1)S(1)}, bf16[384,768]{1,0:T(8,128)(2,1)S(1)}, u32[]{:S(2)}, u32[]{:S(2)}) %collective-permute-start.21) | collective-permute-done | bytes 589856 | tf_op jit(solution)/shard_map/ppermute | solution.py:118
  438.0 11.1 %collective-permute-done.32 = f32[4,768]{1,0:T(4,128)S(1)} collective-permute-done((f32[4,768]{1,0:T(4,128)S(1)}, f32[4,768]{1,0:T(4,128)S(1)}, u32[]{:S(2)}, u32[]{:S(2)}) %collective-permute-start.32) | collective-permute-done | bytes 12320 | tf_op jit(solution)/shard_map/ppermute | solution.py:110
  449.4 11.3 %collective-permute-done.31 = f32[4,768]{1,0:T(4,128)S(1)} collective-permute-done((f32[4,768]{1,0:T(4,128)S(1)}, f32[4,768]{1,0:T(4,128)S(1)}, u32[]{:S(2)}, u32[]{:S(2)}) %collective-permute-start.31) | collective-permute-done | bytes 12320 | tf_op jit(solution)/shard_map/ppermute | solution.py:110
  466.2 10.7 %collective-permute-done.25 = bf16[384,768]{1,0:T(8,128)(2,1)S(1)} collective-permute-done((bf16[384,768]{1,0:T(8,128)(2,1)S(1)}, bf16[384,768]{1,0:T(8,128)(2,1)S(1)}, u32[]{:S(2)}, u32[]{:S(2)}) %collective-permute-start.25) | collective-permute-done | bytes 589856 | tf_op jit(solution)/shard_map/ppermute | solution.py:110
  476.9 12.6 %collective-permute-done.24 = bf16[384,768]{1,0:T(8,128)(2,1)S(1)} collective-permute-done((bf16[384,768]{1,0:T(8,128)(2,1)S(1)}, bf16[384,768]{1,0:T(8,128)(2,1)S(1)}, u32[]{:S(2)}, u32[]{:S(2)}) %collective-permute-start.24) | collective-permute-done | bytes 589856 | tf_op jit(solution)/shard_map/ppermute | solution.py:110
  495.9 6.3 collective-permute-done.9
  502.9 10.2 %collective-permute-done.8 = bf16[384,768]{1,0:T(8,128)(2,1)S(1)} collective-permute-done((bf16[384,768]{1,0:T(8,128)(2,1)S(1)}, bf16[384,768]{1,0:T(8,128)(2,1)S(1)}, u32[]{:S(2)}, u32[]{:S(2)}) %collective-permute-start.8) | collective-permute-done | bytes 589856 | tf_op jit(solution)/shard_map/ppermute | solution.py:110
  515.0 10.7 %collective-permute-done.35 = f32[4,768]{1,0:T(4,128)S(1)} collective-permute-done((f32[4,768]{1,0:T(4,128)S(1)}, f32[4,768]{1,0:T(4,128)S(1)}, u32[]{:S(2)}, u32[]{:S(2)}) %collective-permute-start.35) | collective-permute-done | bytes 12320 | tf_op jit(solution)/shard_map/ppermute | solution.py:114
  529.2 6.5 collective-permute-start.12
  562.6 34.8 %all-to-all-start.1 = ((bf16[16,2,24,768]{3,2,1,0:T(8,128)(2,1)}), bf16[16,2,24,768]{3,2,1,0:T(8,128)(2,1)S(1)}, u32[]{:S(2)}, u32[]{:S(2)}) async-start(bf16[16,2,24,768]{3,2,1,0:T(8,128)(2,1)} %fusion.174), calls=%async_computation.1 | async-start | bytes 2359296 | tf_op jit(solution)/shard_map/all_to_all | solution.py:305
  603.8 20.7 %all-to-all-done.1 = bf16[16,2,24,768]{3,2,1,0:T(8,128)(2,1)S(1)} async-done(((bf16[16,2,24,768]{3,2,1,0:T(8,128)(2,1)}), bf16[16,2,24,768]{3,2,1,0:T(8,128)(2,1)S(1)}, u32[]{:S(2)}, u32[]{:S(2)}) %all-to-all-start.1) | async-done | bytes 1179680 | tf_op jit(solution)/shard_map/all_to_all | solution.py:305
  (385 shorter events, 237.8 us)
Async XLA Ops:
  7.2 130.7 %all-gather.3.cloned.1.call-start = ((), (), s32[]{:S(2)}) async-start(), calls=%async_computation.2 | async-start | bytes 19464192 | tf_op jit(solution)/shard_map/all_gather | solution.py:94
  173.2 52.4 %all-to-all-start = ((bf16[16,4,24,768]{3,2,1,0:T(8,128)(2,1)}), bf16[16,4,24,768]{3,2,1,0:T(8,128)(2,1)}, u32[]{:S(2)}, u32[]{:S(2)}) async-start(bf16[16,4,24,768]{3,2,1,0:T(8,128)(2,1)} %pad_maximum_fusion.1), calls=%async_computation | async-start | bytes 4718592 | tf_op jit(solution)/shard_map/all_to_all | solution.py:186
  252.7 22.1 %collective-permute-start = (bf16[4,384,768]{2,1,0:T(8,128)(2,1)}, bf16[4,384,768]{2,1,0:T(8,128)(2,1)}, u32[]{:S(2)}, u32[]{:S(2)}) collective-permute-start(bf16[4,384,768]{2,1,0:T(8,128)(2,1)} %pad_maximum_fusion.2), channel_id=1, source_target_pairs={{0,16},{16,0},{1,17},{17,1},{2,18},{18,2},{3,19},{19,3},{4,20},{20... | collective-permute-start | bytes 7077896 | tf_op jit(solution)/shard_map/ppermute | solution.py:106
  286.1 19.2 %collective-permute-start.4 = (bf16[384,768]{1,0:T(8,128)(2,1)S(1)}, bf16[384,768]{1,0:T(8,128)(2,1)S(1)}, u32[]{:S(2)}, u32[]{:S(2)}) collective-permute-start(bf16[384,768]{1,0:T(8,128)(2,1)S(1)} %get-tuple-element.175), channel_id=1, source_target_pairs={{0,3},{1,0},{2,1},{3,2},{4,7},{5,4},{6,5},{7,6},{8,11},{9,8},{10,9... | collective-permute-start | bytes 1769480 | tf_op jit(solution)/shard_map/ppermute | solution.py:110
  291.6 27.6 %collective-permute-start.3 = (bf16[384,768]{1,0:T(8,128)(2,1)S(1)}, bf16[384,768]{1,0:T(8,128)(2,1)S(1)}, u32[]{:S(2)}, u32[]{:S(2)}) collective-permute-start(bf16[384,768]{1,0:T(8,128)(2,1)S(1)} %get-tuple-element.176), channel_id=1, source_target_pairs={{0,2},{1,3},{2,0},{3,1},{4,6},{5,7},{6,4},{7,5},{8,10},{9,11},{10,... | collective-permute-start | bytes 1769480 | tf_op jit(solution)/shard_map/ppermute | solution.py:110
  291.6 27.6 %collective-permute-start.2 = (bf16[384,768]{1,0:T(8,128)(2,1)S(1)}, bf16[384,768]{1,0:T(8,128)(2,1)S(1)}, u32[]{:S(2)}, u32[]{:S(2)}) collective-permute-start(bf16[384,768]{1,0:T(8,128)(2,1)S(1)} %get-tuple-element.174), channel_id=1, source_target_pairs={{0,1},{1,2},{2,3},{3,0},{4,5},{5,6},{6,7},{7,4},{8,9},{9,10},{10,1... | collective-permute-start | bytes 1769480 | tf_op jit(solution)/shard_map/ppermute | solution.py:110
  384.9 48.4 %collective-permute-start.22 = (bf16[4,384,768]{2,1,0:T(8,128)(2,1)S(1)}, bf16[4,384,768]{2,1,0:T(8,128)(2,1)S(1)}, u32[]{:S(2)}, u32[]{:S(2)}) collective-permute-start(bf16[4,384,768]{2,1,0:T(8,128)(2,1)S(1)} %pad_maximum_fusion.5), channel_id=1, source_target_pairs={{0,16},{16,0},{1,17},{17,1},{2,18},{18,2},{3,19},{19,3},{4,20},{20... | collective-permute-start | bytes 7077896 | tf_op jit(solution)/shard_map/ppermute | solution.py:106
  385.6 46.6 %collective-permute-start.21 = (bf16[384,768]{1,0:T(8,128)(2,1)S(1)}, bf16[384,768]{1,0:T(8,128)(2,1)S(1)}, u32[]{:S(2)}, u32[]{:S(2)}) collective-permute-start(bf16[384,768]{1,0:T(8,128)(2,1)S(1)} %copy-done.30), channel_id=1, source_target_pairs={{4,0},{5,1},{6,2},{7,3},{20,16},{21,17},{22,18},{23,19}} | collective-permute-start | bytes 1769480 | tf_op jit(solution)/shard_map/ppermute | solution.py:118
  386.9 45.7 %collective-permute-start.20 = (bf16[384,768]{1,0:T(8,128)(2,1)S(1)}, bf16[384,768]{1,0:T(8,128)(2,1)S(1)}, u32[]{:S(2)}, u32[]{:S(2)}) collective-permute-start(bf16[384,768]{1,0:T(8,128)(2,1)S(1)} %copy-done.30), channel_id=1, source_target_pairs={{8,0},{9,1},{10,2},{11,3},{24,16},{25,17},{26,18},{27,19}} | collective-permute-start | bytes 1769480 | tf_op jit(solution)/shard_map/ppermute | solution.py:118
  388.2 48.0 %collective-permute-start.19 = (bf16[384,768]{1,0:T(8,128)(2,1)S(1)}, bf16[384,768]{1,0:T(8,128)(2,1)S(1)}, u32[]{:S(2)}, u32[]{:S(2)}) collective-permute-start(bf16[384,768]{1,0:T(8,128)(2,1)S(1)} %copy-done.30), channel_id=1, source_target_pairs={{12,0},{13,1},{14,2},{15,3},{28,16},{29,17},{30,18},{31,19}} | collective-permute-start | bytes 1769480 | tf_op jit(solution)/shard_map/ppermute | solution.py:118
  391.0 70.0 %collective-permute-start.15 = (bf16[384,768]{1,0:T(8,128)(2,1)S(1)}, bf16[384,768]{1,0:T(8,128)(2,1)S(1)}, u32[]{:S(2)}, u32[]{:S(2)}) collective-permute-start(bf16[384,768]{1,0:T(8,128)(2,1)S(1)} %get-tuple-element.169), channel_id=1, source_target_pairs={{0,3},{1,0},{2,1},{3,2},{4,7},{5,4},{6,5},{7,6},{8,11},{9,8},{10,9... | collective-permute-start | bytes 1769480 | tf_op jit(solution)/shard_map/ppermute | solution.py:110
  432.2 31.0 %collective-permute-start.14 = (bf16[384,768]{1,0:T(8,128)(2,1)S(1)}, bf16[384,768]{1,0:T(8,128)(2,1)S(1)}, u32[]{:S(2)}, u32[]{:S(2)}) collective-permute-start(bf16[384,768]{1,0:T(8,128)(2,1)S(1)} %get-tuple-element.170), channel_id=1, source_target_pairs={{0,2},{1,3},{2,0},{3,1},{4,6},{5,7},{6,4},{7,5},{8,10},{9,11},{10,... | collective-permute-start | bytes 1769480 | tf_op jit(solution)/shard_map/ppermute | solution.py:110
  432.6 31.8 %collective-permute-start.13 = (bf16[384,768]{1,0:T(8,128)(2,1)S(1)}, bf16[384,768]{1,0:T(8,128)(2,1)S(1)}, u32[]{:S(2)}, u32[]{:S(2)}) collective-permute-start(bf16[384,768]{1,0:T(8,128)(2,1)S(1)} %get-tuple-element.168), channel_id=1, source_target_pairs={{0,1},{1,2},{2,3},{3,0},{4,5},{5,6},{6,7},{7,4},{8,9},{9,10},{10,1... | collective-permute-start | bytes 1769480 | tf_op jit(solution)/shard_map/ppermute | solution.py:110
  436.3 24.4 %collective-permute-start.31 = (f32[4,768]{1,0:T(4,128)S(1)}, f32[4,768]{1,0:T(4,128)S(1)}, u32[]{:S(2)}, u32[]{:S(2)}) collective-permute-start(f32[4,768]{1,0:T(4,128)S(1)} %fusion.217), channel_id=1, source_target_pairs={{0,2},{1,3},{2,0},{3,1},{4,6},{5,7},{6,4},{7,5},{8,10},{9,11},{10,... | collective-permute-start | bytes 36872 | tf_op jit(solution)/shard_map/ppermute | solution.py:110
  460.7 28.8 %collective-permute-start.24 = (bf16[384,768]{1,0:T(8,128)(2,1)S(1)}, bf16[384,768]{1,0:T(8,128)(2,1)S(1)}, u32[]{:S(2)}, u32[]{:S(2)}) collective-permute-start(bf16[384,768]{1,0:T(8,128)(2,1)S(1)} %get-tuple-element.173), channel_id=1, source_target_pairs={{0,2},{1,3},{2,0},{3,1},{4,6},{5,7},{6,4},{7,5},{8,10},{9,11},{10,... | collective-permute-start | bytes 1769480 | tf_op jit(solution)/shard_map/ppermute | solution.py:110
  461.0 28.6 %collective-permute-start.23 = (bf16[384,768]{1,0:T(8,128)(2,1)S(1)}, bf16[384,768]{1,0:T(8,128)(2,1)S(1)}, u32[]{:S(2)}, u32[]{:S(2)}) collective-permute-start(bf16[384,768]{1,0:T(8,128)(2,1)S(1)} %get-tuple-element.171), channel_id=1, source_target_pairs={{0,1},{1,2},{2,3},{3,0},{4,5},{5,6},{6,7},{7,4},{8,9},{9,10},{10,1... | collective-permute-start | bytes 1769480 | tf_op jit(solution)/shard_map/ppermute | solution.py:110
  463.2 39.1 %collective-permute-start.9 = (bf16[384,768]{1,0:T(8,128)(2,1)S(1)}, bf16[384,768]{1,0:T(8,128)(2,1)S(1)}, u32[]{:S(2)}, u32[]{:S(2)}) collective-permute-start(bf16[384,768]{1,0:T(8,128)(2,1)S(1)} %get-tuple-element.166), channel_id=1, source_target_pairs={{0,3},{1,0},{2,1},{3,2},{4,7},{5,4},{6,5},{7,6},{8,11},{9,8},{10,9... | collective-permute-start | bytes 1769480 | tf_op jit(solution)/shard_map/ppermute | solution.py:110
  464.4 48.7 %collective-permute-start.8 = (bf16[384,768]{1,0:T(8,128)(2,1)S(1)}, bf16[384,768]{1,0:T(8,128)(2,1)S(1)}, u32[]{:S(2)}, u32[]{:S(2)}) collective-permute-start(bf16[384,768]{1,0:T(8,128)(2,1)S(1)} %get-tuple-element.167), channel_id=1, source_target_pairs={{0,2},{1,3},{2,0},{3,1},{4,6},{5,7},{6,4},{7,5},{8,10},{9,11},{10,... | collective-permute-start | bytes 1769480 | tf_op jit(solution)/shard_map/ppermute | solution.py:110
  476.9 37.7 %collective-permute-start.7 = (bf16[384,768]{1,0:T(8,128)(2,1)S(1)}, bf16[384,768]{1,0:T(8,128)(2,1)S(1)}, u32[]{:S(2)}, u32[]{:S(2)}) collective-permute-start(bf16[384,768]{1,0:T(8,128)(2,1)S(1)} %get-tuple-element.165), channel_id=1, source_target_pairs={{0,1},{1,2},{2,3},{3,0},{4,5},{5,6},{6,7},{7,4},{8,9},{9,10},{10,1... | collective-permute-start | bytes 1769480 | tf_op jit(solution)/shard_map/ppermute | solution.py:110
  494.3 33.5 %collective-permute-start.18 = (bf16[384,768]{1,0:T(8,128)(2,1)S(1)}, bf16[384,768]{1,0:T(8,128)(2,1)S(1)}, u32[]{:S(2)}, u32[]{:S(2)}) collective-permute-start(bf16[384,768]{1,0:T(8,128)(2,1)S(1)} %fusion.186), channel_id=1, source_target_pairs={{12,8},{13,9},{14,10},{15,11},{28,24},{29,25},{30,26},{31,27}} | collective-permute-start | bytes 1769480 | tf_op jit(solution)/shard_map/ppermute | solution.py:118
  495.2 34.0 %collective-permute-start.28 = (bf16[384,768]{1,0:T(8,128)(2,1)S(1)}, bf16[384,768]{1,0:T(8,128)(2,1)S(1)}, u32[]{:S(2)}, u32[]{:S(2)}) collective-permute-start(bf16[384,768]{1,0:T(8,128)(2,1)S(1)} %fusion.183), channel_id=1, source_target_pairs={{8,4},{9,5},{10,6},{11,7},{24,20},{25,21},{26,22},{27,23}} | collective-permute-start | bytes 1769480 | tf_op jit(solution)/shard_map/ppermute | solution.py:118
  502.2 33.5 %collective-permute-start.27 = (bf16[384,768]{1,0:T(8,128)(2,1)S(1)}, bf16[384,768]{1,0:T(8,128)(2,1)S(1)}, u32[]{:S(2)}, u32[]{:S(2)}) collective-permute-start(bf16[384,768]{1,0:T(8,128)(2,1)S(1)} %fusion.183), channel_id=1, source_target_pairs={{12,4},{13,5},{14,6},{15,7},{28,20},{29,21},{30,22},{31,23}} | collective-permute-start | bytes 1769480 | tf_op jit(solution)/shard_map/ppermute | solution.py:118
  513.1 24.1 %collective-permute-start.26 = (bf16[384,768]{1,0:T(8,128)(2,1)S(1)}, bf16[384,768]{1,0:T(8,128)(2,1)S(1)}, u32[]{:S(2)}, u32[]{:S(2)}) collective-permute-start(bf16[384,768]{1,0:T(8,128)(2,1)S(1)} %fusion.183), channel_id=1, source_target_pairs={{0,4},{1,5},{2,6},{3,7},{16,20},{17,21},{18,22},{19,23}} | collective-permute-start | bytes 1769480 | tf_op jit(solution)/shard_map/ppermute | solution.py:118
  562.6 61.9 %all-to-all-start.1 = ((bf16[16,2,24,768]{3,2,1,0:T(8,128)(2,1)}), bf16[16,2,24,768]{3,2,1,0:T(8,128)(2,1)S(1)}, u32[]{:S(2)}, u32[]{:S(2)}) async-start(bf16[16,2,24,768]{3,2,1,0:T(8,128)(2,1)} %fusion.174), calls=%async_computation.1 | async-start | bytes 2359296 | tf_op jit(solution)/shard_map/all_to_all | solution.py:305
  (101 other events, 898.7 us)
Sparse Core Ops, SparseCore 0:
  10.9 126.8 all-gather.2

commit v4 on v3

--- a/solution.py
+++ b/solution.py
@@ -91,8 +91,6 @@
     part = rows // replicas
     shard_low = masters.astype(low_type)
     sent = lax.dynamic_slice_in_dim(shard_low, my_copy * part, part, 1)
-    whole = lax.all_gather(sent, ("zero", "dp"), axis=1, tiled=True)
-    norm_whole = lax.all_gather(norm_params.astype(low_type), "zero", axis=1, tiled=True)
 
     group = ff
     lines = owners // group
@@ -131,6 +129,41 @@
             )
         return joined
 
+    def place(pieces, me, axis):
+        count = len(pieces)
+        shape = list(pieces[0].shape)
+        shape.insert(axis, count)
+        placed = jnp.zeros(shape, pieces[0].dtype)
+        for shift, piece in enumerate(pieces):
+            index = (me + count - shift) % count
+            placed = lax.dynamic_update_index_in_dim(placed, piece, index, axis)
+        return placed
+
+    def gather_rows(values):
+        pieces = [values]
+        for shift in range(1, lines):
+            pieces.append(from_lines(values, shift))
+        values = place(pieces, my_line, 1)
+        pieces = [values]
+        for shift in range(1, group):
+            pieces.append(from_spots(values, shift))
+        return place(pieces, my_spot, 2)
+
+    def gather_tiles(values):
+        half = gather_rows(values)
+        pieces = [half]
+        for shift in range(1, replicas):
+            pieces.append(from_copies(half, shift))
+        if replicas == 2:
+            first = my_copy == 0
+            joined = jnp.stack(
+                [jnp.where(first, pieces[0], pieces[1]), jnp.where(first, pieces[1], pieces[0])],
+                axis=3,
+            )
+        else:
+            joined = place(pieces, my_copy, 3)
+        return joined.reshape(values.shape[0], width, width)
+
     def sum_everywhere(values):
         total = values
         for shift in range(1, replicas):
@@ -180,18 +213,21 @@
     masked = jnp.any(mask_hits, axis=1).reshape(-1, 1)
     row_ids = jnp.sum(jnp.where(mask_hits, repl_id[:, :, None], 0), axis=1).reshape(-1)
     inputs = jnp.where(masked, jnp.take(replace_embed, row_ids, axis=0), tokens)
-    packed = jnp.stack([left_basis, right_basis, first_moment, second_moment], axis=1)
-    packed = lax.dynamic_slice_in_dim(packed, my_copy * part, part, 2).astype(low_type)
-    whole, inputs, packed = lax.optimization_barrier((whole, inputs, outgoing(packed)))
-    packed = lax.all_to_all(packed, "zero", split_axis=0, concat_axis=0, tiled=True)
-    gains = norm_whole.astype(full_type)
+    attention_w = gather_tiles(sent[:4])
+    gate_w = gather_tiles(sent[4 : 4 + ff])
+    up_w = gather_tiles(sent[4 + ff : 4 + 2 * ff])
+    down_w = gather_tiles(sent[4 + 2 * ff :])
+    norm_low = norm_params.astype(low_type)[:, None, :]
+    gains = gather_rows(norm_low).reshape(norm_params.shape[0], width)
+    attention_w, inputs, gains = lax.optimization_barrier((attention_w, inputs, gains))
+    gains = gains.astype(full_type)
 
     slopes = jnp.asarray(alibi_slopes(heads))
     distance = jnp.abs(positions[:, None] - positions[None, :]).astype(full_type)
     alibi_bias = -slopes[:, None, None] * distance[None]
     head_shape = (seq_count, length, heads, head_size)
 
-    qkv = [dot32("td,de->te", inputs, whole[k]).astype(low_type) for k in range(3)]
+    qkv = [dot32("td,de->te", inputs, attention_w[k]).astype(low_type) for k in range(3)]
     queries, key_rows, values = [part_k.reshape(head_shape) for part_k in qkv]
     scores = dot32("bqhd,bkhd->bhqk", queries, key_rows) * scale + alibi_bias[None]
     row_max = jnp.max(scores, axis=-1, keepdims=True)
@@ -199,20 +235,23 @@
     probs = jnp.exp(scores - log_total)
     soft_low = probs.astype(low_type)
     mixed = dot32("bhqk,bkhd->bqhd", soft_low, values).reshape(tok_rows, width).astype(low_type)
-    attended = dot32("td,de->te", mixed, whole[3])
+    attended = dot32("td,de->te", mixed, attention_w[3])
     unit_one, rstd_one = norm_stats(inputs.astype(full_type) + attended)
     hidden = unit_one * gains[0] + gains[1]
     hidden_low = hidden.astype(low_type)
 
-    gate = dot32("td,fde->tfe", hidden_low, whole[4 : 4 + ff])
-    up = dot32("td,fde->tfe", hidden_low, whole[4 + ff : 4 + 2 * ff])
+    gate = dot32("td,fde->tfe", hidden_low, gate_w)
+    up = dot32("td,fde->tfe", hidden_low, up_w)
     half_erf = 0.5 + 0.5 * lax.erf(gate * math.sqrt(0.5))
     act = gate * half_erf
     slope = half_erf + gate * (jnp.exp(-0.5 * gate * gate) * (1.0 / math.sqrt(2.0 * math.pi)))
     inner_low = (act * up).astype(low_type)
     inner_low, act, up_slope = lax.optimization_barrier((inner_low, act, up * slope))
-    branch = dot32("tfe,fed->td", inner_low, whole[4 + 2 * ff :])
-    branch, packed = lax.optimization_barrier((branch, packed))
+    branch = dot32("tfe,fed->td", inner_low, down_w)
+    packed = jnp.stack([left_basis, right_basis, first_moment, second_moment], axis=1)
+    packed = lax.dynamic_slice_in_dim(packed, my_copy * part, part, 2).astype(low_type)
+    branch, packed = lax.optimization_barrier((branch, outgoing(packed)))
+    packed = lax.all_to_all(packed, "zero", split_axis=0, concat_axis=0, tiled=True)
     unit_two, rstd_two = norm_stats(hidden + branch)
     layer_out = (unit_two * gains[2] + gains[3]).astype(low_type)
 
@@ -225,11 +264,11 @@
     ]
     d_branch, grad_down = lax.optimization_barrier((d_branch, grad_down))
     down_low = sum_copies(grad_down)
-    packed = join_copies(packed)
-    d_inner = dot32("td,fed->tfe", d_branch, whole[4 + 2 * ff :])
+    d_inner = dot32("td,fed->tfe", d_branch, down_w)
     d_gate = (d_inner * up_slope).astype(low_type)
     d_up = (d_inner * act).astype(low_type)
     d_gate, d_up, down_low, packed = lax.optimization_barrier((d_gate, d_up, down_low, packed))
+    packed = join_copies(packed)
     down_sum = sum_spots(down_low)
     grad_gate = [dot32("td,te->de", hidden_low, d_gate[:, f]).astype(low_type) for f in range(ff)]
     grad_up = [dot32("td,te->de", hidden_low, d_up[:, f]).astype(low_type) for f in range(ff)]
@@ -240,10 +279,12 @@
     up_low = sum_copies(grad_up)
     d_hidden = (
         d_second
-        + dot32("tfe,fde->td", d_gate, whole[4 : 4 + ff])
-        + dot32("tfe,fde->td", d_up, whole[4 + ff : 4 + 2 * ff])
-    )
-    d_hidden, gate_low, up_low = lax.optimization_barrier((d_hidden, gate_low, up_low))
+        + dot32("tfe,fde->td", d_gate, gate_w)
+        + dot32("tfe,fde->td", d_up, up_w)
+    )
+    d_hidden, gate_low, up_low, packed = lax.optimization_barrier(
+        (d_hidden, gate_low, up_low, packed)
+    )
     down_total = sum_lines(down_sum, 0)
     gate_sum = sum_spots(gate_low)
     up_sum = sum_spots(up_low)
@@ -252,7 +293,7 @@
     d_first, d_gain_one, d_shift_one = norm_back(d_hidden, unit_one, rstd_one, gains[0])
     d_attended = d_first.astype(low_type)
     grad_out = dot32("td,te->de", mixed, d_attended).astype(low_type)
-    d_mixed = dot32("te,de->td", d_attended, whole[3]).astype(low_type).reshape(head_shape)
+    d_mixed = dot32("te,de->td", d_attended, attention_w[3]).astype(low_type).reshape(head_shape)
     d_probs = dot32("bqhd,bkhd->bhqk", d_mixed, values)
     row_delta = jnp.sum(probs * d_probs, axis=-1, keepdims=True)
     d_scores = (probs * (d_probs - row_delta)).astype(low_type)
@@ -269,7 +310,7 @@
     grad_qkv = [grad_query, grad_keys, grad_values]
     d_inputs = d_first
     for k in range(3):
-        d_inputs = d_inputs + dot32("te,de->td", d_qkv[k], whole[k])
+        d_inputs = d_inputs + dot32("te,de->td", d_qkv[k], attention_w[k])
     in_grad = jnp.where(masked, 0.0, d_inputs)
 
     columns = norm_params.shape[1]

time: 660 us -> 705 us (1.068)
  starting transfers between devices: 79.2 us -> 132 us
  blocking collectives: 43.9 us -> 0 us
  local copies, waits for them, and re-layouts: 76.6 us -> 101 us
  waiting for transfers between devices: 234 us -> 253 us
  between operations: 16.9 us -> 3.95 us
  other arithmetic: 55 us -> 65.4 us
    ppermute x15 -> x30, waiting for transfers between devices: 86.4 us -> 156 us  [from_spots(): return lax.ppermute(values, 'zero', pairs)]
    all_gather x1 -> x0, waiting for transfers between devices: 60.8 us -> none  [shards(): whole = lax.all_gather(sent, ('zero', 'dp'), axis=1, tiled=True)]
    all_gather x1 -> x0, blocking collectives: 43.9 us -> none  [shards(): lax.all_gather(norm_params.astype(low_type), 'zero', axis=1, tiled=True)]
    ppermute x3 -> x18, starting transfers between devices: 0.06 us -> 30.5 us  [from_lines(): return lax.ppermute(values, 'zero', pairs)]
    ppermute x15 -> x30, starting transfers between devices: 16.7 us -> 33.6 us  [from_spots(): return lax.ppermute(values, 'zero', pairs)]
    dynamic_update_slice x0 -> x40, local copies, waits for them, and re-layouts: none -> 10.2 us  [place(): placed = lax.dynamic_update_index_in_dim(placed, piece, index, axis)]
    all_to_all x1, waiting for transfers between devices: 4.06 us -> 13.3 us  [shards(): lax.all_to_all(packed, 'zero', split_axis=0, concat_axis=0, tiled=True)]
    another operation x0 -> x11, local copies, waits for them, and re-layouts: none -> 8.8 us  [the longest x3 5.45 us: gather_tiles(): jnp.stack([jnp.where(first, pieces[0], pieces[1]), jnp.where(first, piece...]
  transfers between devices with their start and end apart: 41 -> 74, of which waited for: 18 -> 32; matrix products, arithmetic and copies ran while one was open for 19% -> 24% of each run, Pallas kernels for 0% -> 0%
where the time goes in v4:
time: 705 us; the launch traced here: 696 us
  waiting for transfers between devices  253 us (36%)
  matrix products  142 us (20%)
  starting transfers between devices  132 us (19%)
  local copies, waits for them, and re-layouts  101 us (14%)
  other arithmetic  65.4 us (9%)
    ppermute x30, waiting for transfers between devices, from_spots(): return lax.ppermute(values, 'zero', pairs)  156 us
    dot_general x43, matrix products, dot32(): return jnp.einsum(spec, left, right, preferred_element_type=full_type)  142 us
    ppermute x12, waiting for transfers between devices, from_line(): return lax.ppermute(values, 'zero', pairs)  42 us
    unnamed x194, local copies, waits for them, and re-layouts  34.6 us
    ppermute x30, starting transfers between devices, from_spots(): return lax.ppermute(values, 'zero', pairs)  33.6 us
    all_to_all x1, starting transfers between devices, shards(): lax.all_to_all(results, 'zero', split_axis=0, concat_axis=0, tiled=True)  31.4 us
    ppermute x18, starting transfers between devices, from_lines(): return lax.ppermute(values, 'zero', pairs)  30.5 us
    ppermute x12, starting transfers between devices, from_line(): return lax.ppermute(values, 'zero', pairs)  27.2 us
  transfers between devices with their start and end apart: 74, of which 32 were waited for; matrix products, arithmetic and copies ran while one was open for 24% of the time, Pallas kernels for 0%

profile of v4, /device:TPU:0, one launch (start us, length us, event | category | flops | bytes accessed | tf_op | source)
XLA Modules:
  0.0 696.3 jit_solution(10309135418737831469)
XLA Ops:
  20.0 9.2 %gather_fusion = bf16[1024,768]{1,0:T(8,128)(2,1)} fusion(bf16[4096,768]{1,0:T(8,128)(2,1)} %param.19, s32[1024]{0:T(1024)S(1)} %broadcast_clamp_fusion), kind=kCustom, calls=%fused_computation | custom fusion | bytes 3149824 | tf_op jit(solution)/shard_map/jit(_take)/gather | solution.py:215
  89.4 10.3 %collective-permute-done.30 = bf16[4,4,24,768]{3,2,1,0:T(8,128)(2,1)S(1)} collective-permute-done((bf16[4,4,24,768]{3,2,1,0:T(8,128)(2,1)}, bf16[4,4,24,768]{3,2,1,0:T(8,128)(2,1)S(1)}, u32[]{:S(2)}, u32[]{:S(2)}) %collective-permute-start.30) | collective-permute-done | bytes 589856 | tf_op jit(solution)/shard_map/ppermute | solution.py:108
  99.8 24.6 %collective-permute-done.31 = bf16[4,4,24,768]{3,2,1,0:T(8,128)(2,1)S(1)} collective-permute-done((bf16[4,4,24,768]{3,2,1,0:T(8,128)(2,1)}, bf16[4,4,24,768]{3,2,1,0:T(8,128)(2,1)S(1)}, u32[]{:S(2)}, u32[]{:S(2)}) %collective-permute-start.31) | collective-permute-done | bytes 589856 | tf_op jit(solution)/shard_map/ppermute | solution.py:108
  125.1 10.6 %collective-permute-done.3 = bf16[4,4,24,768]{3,2,1,0:T(8,128)(2,1)S(1)} collective-permute-done((bf16[4,4,24,768]{3,2,1,0:T(8,128)(2,1)S(1)}, bf16[4,4,24,768]{3,2,1,0:T(8,128)(2,1)S(1)}, u32[]{:S(2)}, u32[]{:S(2)}) %collective-permute-start.3) | collective-permute-done | bytes 589856 | tf_op jit(solution)/shard_map/ppermute | solution.py:108
  135.8 18.3 %collective-permute-done.4 = bf16[4,4,24,768]{3,2,1,0:T(8,128)(2,1)S(1)} collective-permute-done((bf16[4,4,24,768]{3,2,1,0:T(8,128)(2,1)S(1)}, bf16[4,4,24,768]{3,2,1,0:T(8,128)(2,1)S(1)}, u32[]{:S(2)}, u32[]{:S(2)}) %collective-permute-start.4) | collective-permute-done | bytes 589856 | tf_op jit(solution)/shard_map/ppermute | solution.py:108
  159.5 10.7 %collective-permute-done.25 = bf16[4,4,24,768]{3,2,1,0:T(8,128)(2,1)S(1)} collective-permute-done((bf16[4,4,24,768]{3,2,1,0:T(8,128)(2,1)S(1)}, bf16[4,4,24,768]{3,2,1,0:T(8,128)(2,1)S(1)}, u32[]{:S(2)}, u32[]{:S(2)}) %collective-permute-start.25) | collective-permute-done | bytes 589856 | tf_op jit(solution)/shard_map/ppermute | solution.py:108
  171.4 11.5 %collective-permute-done.16 = bf16[4,4,24,768]{3,2,1,0:T(8,128)(2,1)S(1)} collective-permute-done((bf16[4,4,24,768]{3,2,1,0:T(8,128)(2,1)S(1)}, bf16[4,4,24,768]{3,2,1,0:T(8,128)(2,1)S(1)}, u32[]{:S(2)}, u32[]{:S(2)}) %collective-permute-start.16) | collective-permute-done | bytes 589856 | tf_op jit(solution)/shard_map/ppermute | solution.py:108
  239.7 8.7 %fusion.76 = f32[1024,4,768]{2,0,1:T(8,128)} fusion(bf16[4,768,768]{2,1,0:T(8,128)(2,1)S(1)} %bitcast.532, bf16[1024,768]{0,1:T(8,128)(2,1)S(1)} %fusion.19), kind=kOutput, calls=%fused_computation.162 | convolution fusion | flops 4831838208 | bytes 18874368 | tf_op jit(solution)/shard_map/td,fde->tfe/dot_general | solution.py:53
  248.4 17.8 %multiply_convert_fusion.2 = (bf16[1024,4,768]{2,0,1:T(8,128)(2,1)}, f32[1024,4,768]{2,0,1:T(8,128)}, f32[1024,4,768]{2,0,1:T(8,128)}) fusion(f32[1024,4,768]{2,0,1:T(8,128)} %fusion.76, bf16[4,768,768]{2,1,0:T(8,128)(2,1)S(1)} %bitcast.528, bf16[1024,768]{0,1:T(8,128)(2,1)S(1)} %fusion.19), kind=kOutput, calls=%fused_computation.9 | convolution fusion | flops 4869586944 | bytes 50331648 | tf_op jit(solution)/shard_map/td,fde->tfe/dot_general | solution.py:53
  266.2 8.3 %convolution_bitcast_fusion = f32[1024,768]{1,0:T(8,128)} fusion(bf16[1024,4,768]{2,0,1:T(8,128)(2,1)} %get-tuple-element.46, bf16[4,768,768]{2,1,0:T(8,128)(2,1)S(1)} %bitcast.494), kind=kOutput, calls=%fused_computation.110 | convolution fusion | flops 4831838208 | bytes 14155776 | tf_op jit(solution)/shard_map/tfe,fed->td/dot_general | solution.py:53
  292.0 7.7 %all-to-all-start = ((bf16[16,4,24,768]{3,2,1,0:T(8,128)(2,1)}), bf16[16,4,24,768]{3,2,1,0:T(8,128)(2,1)}, u32[]{:S(2)}, u32[]{:S(2)}) async-start(bf16[16,4,24,768]{3,2,1,0:T(8,128)(2,1)} %pad_maximum_fusion.5), calls=%async_computation | async-start | bytes 4718592 | tf_op jit(solution)/shard_map/all_to_all | solution.py:254
  314.4 15.8 %multiply_convert_fusion = (bf16[1024,4,768]{2,0,1:T(8,128)(2,1)}, bf16[1024,4,768]{2,0,1:T(8,128)(2,1)}) fusion(f32[1024,4,768]{2,0,1:T(8,128)} %get-tuple-element.50, f32[1024,4,768]{2,0,1:T(8,128)} %get-tuple-element.49, bf16[4,768,768]{2,1,0:T(8,128)(2,1)} %bitcast.491, bf16[1024,768]{0,1:T(8,128)(2,1)} %copy-done.29), kind=kOutput, calls=%fused_computation.7 | convolution fusion | flops 4844421120 | bytes 44040192 | tf_op jit(solution)/shard_map/td,fed->tfe/dot_general | solution.py:53
  334.1 13.3 %all-to-all-done = bf16[16,4,24,768]{3,2,1,0:T(8,128)(2,1)} async-done(((bf16[16,4,24,768]{3,2,1,0:T(8,128)(2,1)}), bf16[16,4,24,768]{3,2,1,0:T(8,128)(2,1)}, u32[]{:S(2)}, u32[]{:S(2)}) %all-to-all-start) | async-done | bytes 2359328 | tf_op jit(solution)/shard_map/all_to_all | solution.py:254
  372.2 9.8 %collective-permute-done.35 = bf16[384,768]{1,0:T(8,128)(2,1)S(1)} collective-permute-done((bf16[384,768]{1,0:T(8,128)(2,1)S(1)}, bf16[384,768]{1,0:T(8,128)(2,1)S(1)}, u32[]{:S(2)}, u32[]{:S(2)}) %collective-permute-start.35) | collective-permute-done | bytes 589856 | tf_op jit(solution)/shard_map/ppermute | solution.py:108
  382.0 12.4 %collective-permute-done.36 = bf16[384,768]{1,0:T(8,128)(2,1)S(1)} collective-permute-done((bf16[384,768]{1,0:T(8,128)(2,1)S(1)}, bf16[384,768]{1,0:T(8,128)(2,1)S(1)}, u32[]{:S(2)}, u32[]{:S(2)}) %collective-permute-start.36) | collective-permute-done | bytes 589856 | tf_op jit(solution)/shard_map/ppermute | solution.py:108
  471.2 15.3 %collective-permute-done.53 = bf16[384,768]{1,0:T(8,128)(2,1)S(1)} collective-permute-done((bf16[384,768]{1,0:T(8,128)(2,1)S(1)}, bf16[384,768]{1,0:T(8,128)(2,1)S(1)}, u32[]{:S(2)}, u32[]{:S(2)}) %collective-permute-start.53) | collective-permute-done | bytes 589856 | tf_op jit(solution)/shard_map/ppermute | solution.py:116
  487.6 11.0 %collective-permute-done.54 = bf16[384,768]{1,0:T(8,128)(2,1)S(1)} collective-permute-done((bf16[384,768]{1,0:T(8,128)(2,1)S(1)}, bf16[384,768]{1,0:T(8,128)(2,1)S(1)}, u32[]{:S(2)}, u32[]{:S(2)}) %collective-permute-start.54) | collective-permute-done | bytes 589856 | tf_op jit(solution)/shard_map/ppermute | solution.py:116
  501.3 9.8 %collective-permute-done.55 = bf16[384,768]{1,0:T(8,128)(2,1)S(1)} collective-permute-done((bf16[384,768]{1,0:T(8,128)(2,1)S(1)}, bf16[384,768]{1,0:T(8,128)(2,1)S(1)}, u32[]{:S(2)}, u32[]{:S(2)}) %collective-permute-start.55) | collective-permute-done | bytes 589856 | tf_op jit(solution)/shard_map/ppermute | solution.py:116
  523.3 9.7 %collective-permute-done.57 = bf16[384,768]{1,0:T(8,128)(2,1)S(1)} collective-permute-done((bf16[384,768]{1,0:T(8,128)(2,1)S(1)}, bf16[384,768]{1,0:T(8,128)(2,1)S(1)}, u32[]{:S(2)}, u32[]{:S(2)}) %collective-permute-start.57) | collective-permute-done | bytes 589856 | tf_op jit(solution)/shard_map/ppermute | solution.py:108
  533.3 12.4 %collective-permute-done.58 = bf16[384,768]{1,0:T(8,128)(2,1)S(1)} collective-permute-done((bf16[384,768]{1,0:T(8,128)(2,1)S(1)}, bf16[384,768]{1,0:T(8,128)(2,1)S(1)}, u32[]{:S(2)}, u32[]{:S(2)}) %collective-permute-start.58) | collective-permute-done | bytes 589856 | tf_op jit(solution)/shard_map/ppermute | solution.py:108
  559.1 9.3 %collective-permute-done.48 = bf16[384,768]{1,0:T(8,128)(2,1)S(1)} collective-permute-done((bf16[384,768]{1,0:T(8,128)(2,1)S(1)}, bf16[384,768]{1,0:T(8,128)(2,1)S(1)}, u32[]{:S(2)}, u32[]{:S(2)}) %collective-permute-start.48) | collective-permute-done | bytes 589856 | tf_op jit(solution)/shard_map/ppermute | solution.py:108
  580.2 10.5 %collective-permute-start.51 = (bf16[384,768]{1,0:T(8,128)(2,1)S(1)}, bf16[384,768]{1,0:T(8,128)(2,1)}, u32[]{:S(2)}, u32[]{:S(2)}) collective-permute-start(bf16[384,768]{1,0:T(8,128)(2,1)S(1)} %fusion.172), channel_id=1, source_target_pairs={{0,8},{1,9},{2,10},{3,11},{16,24},{17,25},{18,26},{19,27}} | collective-permute-start | bytes 1769480 | tf_op jit(solution)/shard_map/ppermute | solution.py:116
  617.6 31.4 %all-to-all-start.1 = ((bf16[16,2,24,768]{3,2,1,0:T(8,128)(2,1)}), bf16[16,2,24,768]{3,2,1,0:T(8,128)(2,1)S(1)}, u32[]{:S(2)}, u32[]{:S(2)}) async-start(bf16[16,2,24,768]{3,2,1,0:T(8,128)(2,1)} %fusion.160), calls=%async_computation.1 | async-start | bytes 2359296 | tf_op jit(solution)/shard_map/all_to_all | solution.py:346
  655.5 20.6 %all-to-all-done.1 = bf16[16,2,24,768]{3,2,1,0:T(8,128)(2,1)S(1)} async-done(((bf16[16,2,24,768]{3,2,1,0:T(8,128)(2,1)}), bf16[16,2,24,768]{3,2,1,0:T(8,128)(2,1)S(1)}, u32[]{:S(2)}, u32[]{:S(2)}) %all-to-all-start.1) | async-done | bytes 1179680 | tf_op jit(solution)/shard_map/all_to_all | solution.py:346
  (543 shorter events, 373.1 us)
Async XLA Ops:
  2.8 48.7 %collective-permute-start.27 = (bf16[4,24,768]{2,1,0:T(8,128)(2,1)}, bf16[4,24,768]{2,1,0:T(8,128)(2,1)}, u32[]{:S(2)}, u32[]{:S(2)}) collective-permute-start(bf16[4,24,768]{2,1,0:T(8,128)(2,1)} %get-tuple-element.248), channel_id=1, source_target_pairs={{0,4},{1,5},{2,6},{3,7},{4,8},{5,9},{6,10},{7,11},{8,12},{9,13},{1... | collective-permute-start | bytes 442376 | tf_op jit(solution)/shard_map/ppermute | solution.py:112
  5.9 48.2 %collective-permute-start.28 = (bf16[4,24,768]{2,1,0:T(8,128)(2,1)}, bf16[4,24,768]{2,1,0:T(8,128)(2,1)}, u32[]{:S(2)}, u32[]{:S(2)}) collective-permute-start(bf16[4,24,768]{2,1,0:T(8,128)(2,1)} %get-tuple-element.248), channel_id=1, source_target_pairs={{0,8},{1,9},{2,10},{3,11},{4,12},{5,13},{6,14},{7,15},{8,0},{9,1},... | collective-permute-start | bytes 442376 | tf_op jit(solution)/shard_map/ppermute | solution.py:112
  9.0 29.7 %collective-permute-start.7 = (bf16[4,1,48]{2,0,1:T(4,128)(2,1)}, bf16[4,1,48]{2,0,1:T(4,128)(2,1)}, u32[]{:S(2)}, u32[]{:S(2)}) collective-permute-start(bf16[4,1,48]{2,0,1:T(4,128)(2,1)} %get-tuple-element.252), channel_id=1, source_target_pairs={{0,4},{1,5},{2,6},{3,7},{4,8},{5,9},{6,10},{7,11},{8,12},{9,13},{1... | collective-permute-start | bytes 1160 | tf_op jit(solution)/shard_map/ppermute | solution.py:112
  9.0 30.4 %collective-permute-start.8 = (bf16[4,1,48]{2,0,1:T(4,128)(2,1)}, bf16[4,1,48]{2,0,1:T(4,128)(2,1)}, u32[]{:S(2)}, u32[]{:S(2)}) collective-permute-start(bf16[4,1,48]{2,0,1:T(4,128)(2,1)} %get-tuple-element.252), channel_id=1, source_target_pairs={{0,8},{1,9},{2,10},{3,11},{4,12},{5,13},{6,14},{7,15},{8,0},{9,1},... | collective-permute-start | bytes 1160 | tf_op jit(solution)/shard_map/ppermute | solution.py:112
  82.9 41.5 %collective-permute-start.31 = (bf16[4,4,24,768]{3,2,1,0:T(8,128)(2,1)}, bf16[4,4,24,768]{3,2,1,0:T(8,128)(2,1)S(1)}, u32[]{:S(2)}, u32[]{:S(2)}) collective-permute-start(bf16[4,4,24,768]{3,2,1,0:T(8,128)(2,1)} %bitcast_dynamic-update-slice_fusion.31), channel_id=1, source_target_pairs={{0,2},{1,3},{2,0},{3,1},{4,6},{5,7},{6,4},{7,5},{8,10},{9,11},{10,... | collective-permute-start | bytes 1769480 | tf_op jit(solution)/shard_map/ppermute | solution.py:108
  83.8 41.2 %collective-permute-start.32 = (bf16[4,4,24,768]{3,2,1,0:T(8,128)(2,1)}, bf16[4,4,24,768]{3,2,1,0:T(8,128)(2,1)S(1)}, u32[]{:S(2)}, u32[]{:S(2)}) collective-permute-start(bf16[4,4,24,768]{3,2,1,0:T(8,128)(2,1)} %bitcast_dynamic-update-slice_fusion.31), channel_id=1, source_target_pairs={{0,3},{1,0},{2,1},{3,2},{4,7},{5,4},{6,5},{7,6},{8,11},{9,8},{10,9... | collective-permute-start | bytes 1769480 | tf_op jit(solution)/shard_map/ppermute | solution.py:108
  88.2 68.6 %collective-permute-start.23 = (bf16[4,4,24,768]{3,2,1,0:T(8,128)(2,1)S(1)}, bf16[4,4,24,768]{3,2,1,0:T(8,128)(2,1)S(1)}, u32[]{:S(2)}, u32[]{:S(2)}) collective-permute-start(bf16[4,4,24,768]{3,2,1,0:T(8,128)(2,1)S(1)} %bitcast_dynamic-update-slice_fusion.19), channel_id=1, source_target_pairs={{0,1},{1,2},{2,3},{3,0},{4,5},{5,6},{6,7},{7,4},{8,9},{9,10},{10,1... | collective-permute-start | bytes 1769480 | tf_op jit(solution)/shard_map/ppermute | solution.py:108
  88.8 70.1 %collective-permute-start.24 = (bf16[4,4,24,768]{3,2,1,0:T(8,128)(2,1)S(1)}, bf16[4,4,24,768]{3,2,1,0:T(8,128)(2,1)S(1)}, u32[]{:S(2)}, u32[]{:S(2)}) collective-permute-start(bf16[4,4,24,768]{3,2,1,0:T(8,128)(2,1)S(1)} %bitcast_dynamic-update-slice_fusion.19), channel_id=1, source_target_pairs={{0,2},{1,3},{2,0},{3,1},{4,6},{5,7},{6,4},{7,5},{8,10},{9,11},{10,... | collective-permute-start | bytes 1769480 | tf_op jit(solution)/shard_map/ppermute | solution.py:108
  99.7 36.0 %collective-permute-start.3 = (bf16[4,4,24,768]{3,2,1,0:T(8,128)(2,1)S(1)}, bf16[4,4,24,768]{3,2,1,0:T(8,128)(2,1)S(1)}, u32[]{:S(2)}, u32[]{:S(2)}) collective-permute-start(bf16[4,4,24,768]{3,2,1,0:T(8,128)(2,1)S(1)} %bitcast_dynamic-update-slice_fusion.27), channel_id=1, source_target_pairs={{0,1},{1,2},{2,3},{3,0},{4,5},{5,6},{6,7},{7,4},{8,9},{9,10},{10,1... | collective-permute-start | bytes 1769480 | tf_op jit(solution)/shard_map/ppermute | solution.py:108
  135.7 57.7 %collective-permute-start.33 = (bf16[4,4,4,24,768]{4,3,2,1,0:T(8,128)(2,1)S(1)}, bf16[4,4,4,24,768]{4,3,2,1,0:T(8,128)(2,1)S(1)}, u32[]{:S(2)}, u32[]{:S(2)}) collective-permute-start(bf16[4,4,4,24,768]{4,3,2,1,0:T(8,128)(2,1)S(1)} %bitcast_dynamic-update-slice_fusion.15), channel_id=1, source_target_pairs={{0,16},{16,0},{1,17},{17,1},{2,18},{18,2},{3,19},{19,3},{4,20},{20... | collective-permute-start | bytes 7077896 | tf_op jit(solution)/shard_map/ppermute | solution.py:104
  154.2 42.5 %collective-permute-start.6 = (bf16[4,4,4,24,768]{4,3,2,1,0:T(8,128)(2,1)S(1)}, bf16[4,4,4,24,768]{4,3,2,1,0:T(8,128)(2,1)S(1)}, u32[]{:S(2)}, u32[]{:S(2)}) collective-permute-start(bf16[4,4,4,24,768]{4,3,2,1,0:T(8,128)(2,1)S(1)} %bitcast_dynamic-update-slice_fusion.11), channel_id=1, source_target_pairs={{0,16},{16,0},{1,17},{17,1},{2,18},{18,2},{3,19},{19,3},{4,20},{20... | collective-permute-start | bytes 7077896 | tf_op jit(solution)/shard_map/ppermute | solution.py:104
  193.4 40.4 %collective-permute-start.19 = (bf16[4,4,4,24,768]{4,3,2,1,0:T(8,128)(2,1)}, bf16[4,4,4,24,768]{4,3,2,1,0:T(8,128)(2,1)}, u32[]{:S(2)}, u32[]{:S(2)}) collective-permute-start(bf16[4,4,4,24,768]{4,3,2,1,0:T(8,128)(2,1)} %bitcast_dynamic-update-slice_fusion.7), channel_id=1, source_target_pairs={{0,16},{16,0},{1,17},{17,1},{2,18},{18,2},{3,19},{19,3},{4,20},{20... | collective-permute-start | bytes 7077896 | tf_op jit(solution)/shard_map/ppermute | solution.py:104
  292.0 55.3 %all-to-all-start = ((bf16[16,4,24,768]{3,2,1,0:T(8,128)(2,1)}), bf16[16,4,24,768]{3,2,1,0:T(8,128)(2,1)}, u32[]{:S(2)}, u32[]{:S(2)}) async-start(bf16[16,4,24,768]{3,2,1,0:T(8,128)(2,1)} %pad_maximum_fusion.5), calls=%async_computation | async-start | bytes 4718592 | tf_op jit(solution)/shard_map/all_to_all | solution.py:254
  362.3 57.9 %collective-permute-start.40 = (bf16[16,4,24,768]{3,2,0,1:T(8,128)(2,1)}, bf16[16,4,24,768]{3,2,0,1:T(8,128)(2,1)}, u32[]{:S(2)}, u32[]{:S(2)}) collective-permute-start(bf16[16,4,24,768]{3,2,0,1:T(8,128)(2,1)} %copy.698), channel_id=1, source_target_pairs={{0,16},{16,0},{1,17},{17,1},{2,18},{18,2},{3,19},{19,3},{4,20},{20... | collective-permute-start | bytes 7077896 | tf_op jit(solution)/shard_map/ppermute | solution.py:104
  364.7 29.7 %collective-permute-start.36 = (bf16[384,768]{1,0:T(8,128)(2,1)S(1)}, bf16[384,768]{1,0:T(8,128)(2,1)S(1)}, u32[]{:S(2)}, u32[]{:S(2)}) collective-permute-start(bf16[384,768]{1,0:T(8,128)(2,1)S(1)} %get-tuple-element.213), channel_id=1, source_target_pairs={{0,2},{1,3},{2,0},{3,1},{4,6},{5,7},{6,4},{7,5},{8,10},{9,11},{10,... | collective-permute-start | bytes 1769480 | tf_op jit(solution)/shard_map/ppermute | solution.py:108
  463.5 37.0 %collective-permute-start.56 = (bf16[4,384,768]{2,1,0:T(8,128)(2,1)S(1)}, bf16[4,384,768]{2,1,0:T(8,128)(2,1)S(1)}, u32[]{:S(2)}, u32[]{:S(2)}) collective-permute-start(bf16[4,384,768]{2,1,0:T(8,128)(2,1)S(1)} %pad_maximum_fusion.9), channel_id=1, source_target_pairs={{0,16},{16,0},{1,17},{17,1},{2,18},{18,2},{3,19},{19,3},{4,20},{20... | collective-permute-start | bytes 7077896 | tf_op jit(solution)/shard_map/ppermute | solution.py:104
  465.6 33.0 %collective-permute-start.54 = (bf16[384,768]{1,0:T(8,128)(2,1)S(1)}, bf16[384,768]{1,0:T(8,128)(2,1)S(1)}, u32[]{:S(2)}, u32[]{:S(2)}) collective-permute-start(bf16[384,768]{1,0:T(8,128)(2,1)S(1)} %copy-done.34), channel_id=1, source_target_pairs={{8,0},{9,1},{10,2},{11,3},{24,16},{25,17},{26,18},{27,19}} | collective-permute-start | bytes 1769480 | tf_op jit(solution)/shard_map/ppermute | solution.py:116
  466.9 44.2 %collective-permute-start.55 = (bf16[384,768]{1,0:T(8,128)(2,1)S(1)}, bf16[384,768]{1,0:T(8,128)(2,1)S(1)}, u32[]{:S(2)}, u32[]{:S(2)}) collective-permute-start(bf16[384,768]{1,0:T(8,128)(2,1)S(1)} %copy-done.34), channel_id=1, source_target_pairs={{4,0},{5,1},{6,2},{7,3},{20,16},{21,17},{22,18},{23,19}} | collective-permute-start | bytes 1769480 | tf_op jit(solution)/shard_map/ppermute | solution.py:116
  469.5 49.5 %collective-permute-start.41 = (bf16[384,768]{1,0:T(8,128)(2,1)S(1)}, bf16[384,768]{1,0:T(8,128)(2,1)S(1)}, u32[]{:S(2)}, u32[]{:S(2)}) collective-permute-start(bf16[384,768]{1,0:T(8,128)(2,1)S(1)} %get-tuple-element.202), channel_id=1, source_target_pairs={{0,1},{1,2},{2,3},{3,0},{4,5},{5,6},{6,7},{7,4},{8,9},{9,10},{10,1... | collective-permute-start | bytes 1769480 | tf_op jit(solution)/shard_map/ppermute | solution.py:108
  486.5 35.8 %collective-permute-start.42 = (bf16[384,768]{1,0:T(8,128)(2,1)S(1)}, bf16[384,768]{1,0:T(8,128)(2,1)S(1)}, u32[]{:S(2)}, u32[]{:S(2)}) collective-permute-start(bf16[384,768]{1,0:T(8,128)(2,1)S(1)} %get-tuple-element.204), channel_id=1, source_target_pairs={{0,2},{1,3},{2,0},{3,1},{4,6},{5,7},{6,4},{7,5},{8,10},{9,11},{10,... | collective-permute-start | bytes 1769480 | tf_op jit(solution)/shard_map/ppermute | solution.py:108
  522.3 36.1 %collective-permute-start.47 = (bf16[384,768]{1,0:T(8,128)(2,1)S(1)}, bf16[384,768]{1,0:T(8,128)(2,1)S(1)}, u32[]{:S(2)}, u32[]{:S(2)}) collective-permute-start(bf16[384,768]{1,0:T(8,128)(2,1)S(1)} %get-tuple-element.205), channel_id=1, source_target_pairs={{0,1},{1,2},{2,3},{3,0},{4,5},{5,6},{6,7},{7,4},{8,9},{9,10},{10,1... | collective-permute-start | bytes 1769480 | tf_op jit(solution)/shard_map/ppermute | solution.py:108
  522.4 46.0 %collective-permute-start.48 = (bf16[384,768]{1,0:T(8,128)(2,1)S(1)}, bf16[384,768]{1,0:T(8,128)(2,1)S(1)}, u32[]{:S(2)}, u32[]{:S(2)}) collective-permute-start(bf16[384,768]{1,0:T(8,128)(2,1)S(1)} %get-tuple-element.207), channel_id=1, source_target_pairs={{0,2},{1,3},{2,0},{3,1},{4,6},{5,7},{6,4},{7,5},{8,10},{9,11},{10,... | collective-permute-start | bytes 1769480 | tf_op jit(solution)/shard_map/ppermute | solution.py:108
  533.1 36.1 %collective-permute-start.49 = (bf16[384,768]{1,0:T(8,128)(2,1)S(1)}, bf16[384,768]{1,0:T(8,128)(2,1)S(1)}, u32[]{:S(2)}, u32[]{:S(2)}) collective-permute-start(bf16[384,768]{1,0:T(8,128)(2,1)S(1)} %get-tuple-element.206), channel_id=1, source_target_pairs={{0,3},{1,0},{2,1},{3,2},{4,7},{5,4},{6,5},{7,6},{8,11},{9,8},{10,9... | collective-permute-start | bytes 1769480 | tf_op jit(solution)/shard_map/ppermute | solution.py:108
  617.6 58.5 %all-to-all-start.1 = ((bf16[16,2,24,768]{3,2,1,0:T(8,128)(2,1)}), bf16[16,2,24,768]{3,2,1,0:T(8,128)(2,1)S(1)}, u32[]{:S(2)}, u32[]{:S(2)}) async-start(bf16[16,2,24,768]{3,2,1,0:T(8,128)(2,1)} %fusion.160), calls=%async_computation.1 | async-start | bytes 2359296 | tf_op jit(solution)/shard_map/all_to_all | solution.py:346
  (145 other events, 1696.6 us)

commit v5 on v3

--- a/solution.py
+++ b/solution.py
@@ -233,17 +233,14 @@
     down_sum = sum_spots(down_low)
     grad_gate = [dot32("td,te->de", hidden_low, d_gate[:, f]).astype(low_type) for f in range(ff)]
     grad_up = [dot32("td,te->de", hidden_low, d_up[:, f]).astype(low_type) for f in range(ff)]
-    d_gate, d_up, grad_gate, grad_up, down_sum = lax.optimization_barrier(
-        (d_gate, d_up, grad_gate, grad_up, down_sum)
-    )
+    d_gate, d_up, grad_gate, grad_up = lax.optimization_barrier((d_gate, d_up, grad_gate, grad_up))
     gate_low = sum_copies(grad_gate)
     up_low = sum_copies(grad_up)
-    d_hidden = (
-        d_second
-        + dot32("tfe,fde->td", d_gate, whole[4 : 4 + ff])
-        + dot32("tfe,fde->td", d_up, whole[4 + ff : 4 + 2 * ff])
-    )
-    d_hidden, gate_low, up_low = lax.optimization_barrier((d_hidden, gate_low, up_low))
+    gate_back = dot32("tfe,fde->td", d_gate, whole[4 : 4 + ff])
+    d_hidden = d_second + gate_back + dot32("tfe,fde->td", d_up, whole[4 + ff : 4 + 2 * ff])
+    d_hidden, gate_low, up_low, down_sum = lax.optimization_barrier(
+        (d_hidden, gate_low, up_low, down_sum)
+    )
     down_total = sum_lines(down_sum, 0)
     gate_sum = sum_spots(gate_low)
     up_sum = sum_spots(up_low)
@@ -276,7 +273,7 @@
     norm_sum = lax.dynamic_slice_in_dim(norm_sum, my_rows * columns, columns, 1)
     attention_low = sum_copies(grad_qkv + [grad_out])
     mine = sum_lines(sum_spots(attention_low), 1)
-    mine, norm_sum = lax.optimization_barrier((mine, norm_sum))
+    mine, norm_sum, in_grad = lax.optimization_barrier((mine, norm_sum, in_grad))
     mine = jnp.where(my_line == 0, down_total, mine)
     mine = jnp.where(my_line == 2, gate_total, mine)
     mine = jnp.where(my_line == 3, up_total, mine).astype(low_type)

time: 660 us -> 619 us (0.938)
  waiting for transfers between devices: 234 us -> 152 us
  blocking collectives: 43.9 us -> 103 us
  starting transfers between devices: 79.2 us -> 57.6 us
    all_to_all x0 -> x1, blocking collectives: none -> 59.2 us  [shards(): lax.all_to_all(results, 'zero', split_axis=0, concat_axis=0, tiled=True)]
    all_to_all x1 -> x0, starting transfers between devices: 34.8 us -> none  [shards(): lax.all_to_all(results, 'zero', split_axis=0, concat_axis=0, tiled=True)]
    ppermute x12, waiting for transfers between devices: 45.2 us -> 17.3 us  [from_line(): return lax.ppermute(values, 'zero', pairs)]
    ppermute x15, waiting for transfers between devices: 86.4 us -> 64.9 us  [from_spots(): return lax.ppermute(values, 'zero', pairs)]
    all_to_all x1 -> x0, waiting for transfers between devices: 20.7 us -> none  [shards(): lax.all_to_all(results, 'zero', split_axis=0, concat_axis=0, tiled=True)]
    ppermute x3, waiting for transfers between devices: 15.3 us -> 0.01 us  [from_lines(): return lax.ppermute(values, 'zero', pairs)]
    ppermute x3, starting transfers between devices: 0.06 us -> 10.4 us  [from_lines(): return lax.ppermute(values, 'zero', pairs)]
    unnamed x172 -> x162, local copies, waits for them, and re-layouts: 31.9 us -> 31.8 us
  transfers between devices with their start and end apart: 41 -> 40, of which waited for: 18 -> 15; matrix products, arithmetic and copies ran while one was open for 19% -> 21% of each run, Pallas kernels for 0% -> 0%
where the time goes in v5:
time: 619 us; the launch traced here: 612 us
  waiting for transfers between devices  152 us (25%)
  matrix products  144 us (23%)
  blocking collectives  103 us (17%)
  local copies, waits for them, and re-layouts  82 us (13%)
  starting transfers between devices  57.6 us (9%)
  other arithmetic  55.8 us (9%)
  between operations  16.7 us (3%)
    dot_general x43, matrix products, dot32(): return jnp.einsum(spec, left, right, preferred_element_type=full_type)  144 us
    ppermute x15, waiting for transfers between devices, from_spots(): return lax.ppermute(values, 'zero', pairs)  64.9 us
    all_gather x1, waiting for transfers between devices, shards(): whole = lax.all_gather(sent, ('zero', 'dp'), axis=1, tiled=True)  60.8 us
    all_to_all x1, blocking collectives, shards(): lax.all_to_all(results, 'zero', split_axis=0, concat_axis=0, tiled=True)  59.2 us
    all_gather x1, blocking collectives, shards(): lax.all_gather(norm_params.astype(low_type), 'zero', axis=1, tiled=True)  43.9 us
    unnamed x162, local copies, waits for them, and re-layouts  31.8 us
    ppermute x12, starting transfers between devices, from_line(): return lax.ppermute(values, 'zero', pairs)  23.3 us
    ppermute x15, starting transfers between devices, from_spots(): return lax.ppermute(values, 'zero', pairs)  17.5 us
  transfers between devices with their start and end apart: 40, of which 15 were waited for; matrix products, arithmetic and copies ran while one was open for 21% of the time, Pallas kernels for 0%

profile of v5, /device:TPU:0, one launch (start us, length us, event | category | flops | bytes accessed | tf_op | source)
XLA Modules:
  0.0 612.0 jit_solution(10967003837967581725)
XLA Ops:
  17.9 9.2 %gather_fusion = bf16[1024,768]{1,0:T(8,128)(2,1)} fusion(bf16[4096,768]{1,0:T(8,128)(2,1)} %param.19, s32[1024]{0:T(1024)S(1)} %broadcast_clamp_fusion), kind=kCustom, calls=%fused_computation | custom fusion | bytes 3149824 | tf_op jit(solution)/shard_map/jit(_take)/gather | solution.py:182
  29.8 43.9 %all-gather = bf16[16,48,4]{1,2,0:T(4,128)(2,1)S(1)} all-gather(bf16[1,48,4]{1,2,0:T(4,128)(2,1)S(1)} %convert_bitcast_fusion), channel_id=1, replica_groups=mesh['dp'=2,'zero'=16] {'zero'}, dimensions={0}, use_global_device_ids=true | all-gather | bytes 6528 | tf_op jit(solution)/shard_map/all_gather | solution.py:95
  77.0 60.8 %all-gather.3.cloned.1.call-done = bf16[16,768,768]{2,1,0:T(8,128)(2,1)} async-done(((bf16[16,24,768]{2,1,0:T(8,128)(2,1)}), bf16[16,768,768]{2,1,0:T(8,128)(2,1)}) %all-gather.3.cloned.1.call-update) | async-done | bytes 18874384 | tf_op jit(solution)/shard_map/all_gather | solution.py:94
  173.3 4.7 all-to-all-start
  178.5 10.9 %fusion.23 = f32[1024,4,768]{2,0,1:T(8,128)} fusion(bf16[16,768,768]{2,1,0:T(8,128)(2,1)} %all-gather.3.cloned.1.call-done, bf16[1024,768]{0,1:T(8,128)(2,1)S(1)} %fusion.31), kind=kOutput, calls=%fused_computation.48 | convolution fusion | flops 4831838208 | bytes 18874368 | tf_op jit(solution)/shard_map/td,fde->tfe/dot_general | solution.py:53
  189.4 19.8 %multiply_convert_fusion.2 = (bf16[1024,4,768]{2,0,1:T(8,128)(2,1)S(1)}, f32[1024,4,768]{2,0,1:T(8,128)}, f32[1024,4,768]{2,0,1:T(8,128)}) fusion(f32[1024,4,768]{2,0,1:T(8,128)} %fusion.23, bf16[16,768,768]{2,1,0:T(8,128)(2,1)} %all-gather.3.cloned.1.call-done, bf16[1024,768]{0,1:T(8,128)(2,1)S(1)} %fusion.31), kind=kOutput, calls=%fused_computation.9 | convolution fusion | flops 4869586944 | bytes 50331648 | tf_op jit(solution)/shard_map/td,fde->tfe/dot_general | solution.py:53
  211.7 9.6 %fusion.48 = f32[1024,768]{1,0:T(8,128)} fusion(bf16[1024,4,768]{2,0,1:T(8,128)(2,1)S(1)} %get-tuple-element.45, bf16[16,768,768]{2,1,0:T(8,128)(2,1)} %all-gather.3.cloned.1.call-done), kind=kOutput, calls=%fused_computation.110 | convolution fusion | flops 4831838208 | bytes 14155776 | tf_op jit(solution)/shard_map/tfe,fed->td/dot_general | solution.py:53
  253.3 15.6 %multiply_convert_fusion = (bf16[1024,4,768]{2,0,1:T(8,128)(2,1)}, bf16[1024,4,768]{2,0,1:T(8,128)(2,1)}) fusion(f32[1024,4,768]{2,0,1:T(8,128)} %get-tuple-element.50, f32[1024,4,768]{2,0,1:T(8,128)} %get-tuple-element.49, bf16[16,768,768]{2,1,0:T(8,128)(2,1)} %all-gather.3.cloned.1.call-done, bf16[1024,768]{0,1:T(8,128)(2,1)} %copy-done.26), kind=kOutput, calls=%fused_computation.7 | convolution fusion | flops 4844421120 | bytes 44040192 | tf_op jit(solution)/shard_map/td,fed->tfe/dot_general | solution.py:53
  288.7 8.1 %fusion.17 = f32[1024,768,1]{0,1,2:T(8,128)} fusion(bf16[1024,4,768]{2,0,1:T(8,128)(2,1)S(1)} %bitcast.345, bf16[16,768,768]{2,1,0:T(8,128)(2,1)} %all-gather.3.cloned.1.call-done), kind=kOutput, calls=%fused_computation.42 | convolution fusion | flops 4831838208 | bytes 14155776 | tf_op jit(solution)/shard_map/tfe,fde->td/dot_general | solution.py:53
  307.6 5.6 collective-permute-start.6
  313.8 7.9 %bitcast_add_fusion = f32[1024,768]{0,1:T(8,128)S(1)} fusion(f32[1024,768,1]{0,1,2:T(8,128)} %fusion.17, bf16[1024,4,768]{2,0,1:T(8,128)(2,1)S(1)} %bitcast.343, bf16[16,768,768]{2,1,0:T(8,128)(2,1)} %all-gather.3.cloned.1.call-done, f32[1024]{0:T(1024)S(1)} %get-tuple-element.221, f32[1024,768]{0,1:T(8,128)S(1)} %copy-done.2, ...), kind=kOutput, calls=%fused_computation.63 | convolution fusion | flops 4839702528 | bytes 22039552 | tf_op jit(solution)/shard_map/tfe,fde->td/dot_general | solution.py:53
  321.7 5.5 collective-permute-done.6
  327.2 13.8 %collective-permute-done.5 = bf16[384,768]{1,0:T(8,128)(2,1)} collective-permute-done((bf16[384,768]{1,0:T(8,128)(2,1)}, bf16[384,768]{1,0:T(8,128)(2,1)}, u32[]{:S(2)}, u32[]{:S(2)}) %collective-permute-start.5) | collective-permute-done | bytes 589856 | tf_op jit(solution)/shard_map/ppermute | solution.py:110
  362.2 5.3 fusion.153
  396.1 6.6 %collective-permute-start.19 = (f32[4,768]{1,0:T(4,128)S(1)}, f32[4,768]{1,0:T(4,128)S(1)}, u32[]{:S(2)}, u32[]{:S(2)}) collective-permute-start(f32[4,768]{1,0:T(4,128)S(1)} %add_add_fusion), channel_id=1, source_target_pairs={{0,8},{1,9},{2,10},{3,11},{4,12},{5,13},{6,14},{7,15},{8,0},{9,1},... | collective-permute-start | bytes 36872 | tf_op jit(solution)/shard_map/ppermute | solution.py:114
  416.1 11.4 %collective-permute-done.27 = bf16[384,768]{1,0:T(8,128)(2,1)} collective-permute-done((bf16[384,768]{1,0:T(8,128)(2,1)}, bf16[384,768]{1,0:T(8,128)(2,1)}, u32[]{:S(2)}, u32[]{:S(2)}) %collective-permute-start.27) | collective-permute-done | bytes 589856 | tf_op jit(solution)/shard_map/ppermute | solution.py:110
  428.9 10.5 %collective-permute-done.10 = bf16[384,768]{1,0:T(8,128)(2,1)} collective-permute-done((bf16[384,768]{1,0:T(8,128)(2,1)}, bf16[384,768]{1,0:T(8,128)(2,1)}, u32[]{:S(2)}, u32[]{:S(2)}) %collective-permute-start.10) | collective-permute-done | bytes 589856 | tf_op jit(solution)/shard_map/ppermute | solution.py:110
  441.6 11.3 %collective-permute-done.8 = bf16[384,768]{1,0:T(8,128)(2,1)} collective-permute-done((bf16[384,768]{1,0:T(8,128)(2,1)}, bf16[384,768]{1,0:T(8,128)(2,1)}, u32[]{:S(2)}, u32[]{:S(2)}) %collective-permute-start.8) | collective-permute-done | bytes 589856 | tf_op jit(solution)/shard_map/ppermute | solution.py:110
  466.0 9.0 %collective-permute-done.21 = bf16[384,768]{1,0:T(8,128)(2,1)S(1)} collective-permute-done((bf16[384,768]{1,0:T(8,128)(2,1)S(1)}, bf16[384,768]{1,0:T(8,128)(2,1)S(1)}, u32[]{:S(2)}, u32[]{:S(2)}) %collective-permute-start.21) | collective-permute-done | bytes 589856 | tf_op jit(solution)/shard_map/ppermute | solution.py:110
  475.0 7.5 %collective-permute-start.11 = (bf16[384,768]{1,0:T(8,128)(2,1)S(1)}, bf16[384,768]{1,0:T(8,128)(2,1)S(1)}, u32[]{:S(2)}, u32[]{:S(2)}) collective-permute-start(bf16[384,768]{1,0:T(8,128)(2,1)S(1)} %fusion.189), channel_id=1, source_target_pairs={{0,4},{1,5},{2,6},{3,7},{16,20},{17,21},{18,22},{19,23}} | collective-permute-start | bytes 1769480 | tf_op jit(solution)/shard_map/ppermute | solution.py:118
  487.9 6.2 %collective-permute-start.26 = (bf16[384,768]{1,0:T(8,128)(2,1)S(1)}, bf16[384,768]{1,0:T(8,128)(2,1)S(1)}, u32[]{:S(2)}, u32[]{:S(2)}) collective-permute-start(bf16[384,768]{1,0:T(8,128)(2,1)S(1)} %fusion.186), channel_id=1, source_target_pairs={{0,12},{1,13},{2,14},{3,15},{16,28},{17,29},{18,30},{19,31}} | collective-permute-start | bytes 1769480 | tf_op jit(solution)/shard_map/ppermute | solution.py:118
  500.9 8.0 %collective-permute-done.31 = bf16[384,768]{1,0:T(8,128)(2,1)S(1)} collective-permute-done((bf16[384,768]{1,0:T(8,128)(2,1)S(1)}, bf16[384,768]{1,0:T(8,128)(2,1)S(1)}, u32[]{:S(2)}, u32[]{:S(2)}) %collective-permute-start.31) | collective-permute-done | bytes 589856 | tf_op jit(solution)/shard_map/ppermute | solution.py:118
  508.9 7.8 %collective-permute-done.26 = bf16[384,768]{1,0:T(8,128)(2,1)S(1)} collective-permute-done((bf16[384,768]{1,0:T(8,128)(2,1)S(1)}, bf16[384,768]{1,0:T(8,128)(2,1)S(1)}, u32[]{:S(2)}, u32[]{:S(2)}) %collective-permute-start.26) | collective-permute-done | bytes 589856 | tf_op jit(solution)/shard_map/ppermute | solution.py:118
  529.1 59.2 %all_to_all.10 = bf16[16,2,24,768]{3,2,1,0:T(8,128)(2,1)S(1)} all-to-all(bf16[16,2,24,768]{3,2,1,0:T(8,128)(2,1)S(1)} %fusion.174), channel_id=1, replica_groups=mesh['dp'=2,'zero'=16] {'zero'}, dimensions={0} | all-to-all | bytes 2359296 | tf_op jit(solution)/shard_map/all_to_all | solution.py:302
  (374 shorter events, 237.0 us)
Async XLA Ops:
  7.2 130.7 %all-gather.3.cloned.1.call-start = ((), (), s32[]{:S(2)}) async-start(), calls=%async_computation.2 | async-start | bytes 19464192 | tf_op jit(solution)/shard_map/all_gather | solution.py:94
  173.3 52.3 %all-to-all-start = ((bf16[16,4,24,768]{3,2,1,0:T(8,128)(2,1)}), bf16[16,4,24,768]{3,2,1,0:T(8,128)(2,1)}, u32[]{:S(2)}, u32[]{:S(2)}) async-start(bf16[16,4,24,768]{3,2,1,0:T(8,128)(2,1)} %pad_maximum_fusion.1), calls=%async_computation | async-start | bytes 4718592 | tf_op jit(solution)/shard_map/all_to_all | solution.py:186
  252.8 21.8 %collective-permute-start = (bf16[4,384,768]{2,1,0:T(8,128)(2,1)}, bf16[4,384,768]{2,1,0:T(8,128)(2,1)}, u32[]{:S(2)}, u32[]{:S(2)}) collective-permute-start(bf16[4,384,768]{2,1,0:T(8,128)(2,1)} %pad_maximum_fusion.2), channel_id=1, source_target_pairs={{0,16},{16,0},{1,17},{17,1},{2,18},{18,2},{3,19},{19,3},{4,20},{20... | collective-permute-start | bytes 7077896 | tf_op jit(solution)/shard_map/ppermute | solution.py:106
  300.5 43.1 %collective-permute-start.2 = (bf16[4,384,768]{2,1,0:T(8,128)(2,1)}, bf16[4,384,768]{2,1,0:T(8,128)(2,1)S(1)}, u32[]{:S(2)}, u32[]{:S(2)}) collective-permute-start(bf16[4,384,768]{2,1,0:T(8,128)(2,1)} %pad_maximum_fusion.3), channel_id=1, source_target_pairs={{0,16},{16,0},{1,17},{17,1},{2,18},{18,2},{3,19},{19,3},{4,20},{20... | collective-permute-start | bytes 7077896 | tf_op jit(solution)/shard_map/ppermute | solution.py:106
  305.8 39.6 %collective-permute-start.3 = (bf16[4,384,768]{2,1,0:T(8,128)(2,1)}, bf16[4,384,768]{2,1,0:T(8,128)(2,1)}, u32[]{:S(2)}, u32[]{:S(2)}) collective-permute-start(bf16[4,384,768]{2,1,0:T(8,128)(2,1)} %pad_maximum_fusion.4), channel_id=1, source_target_pairs={{0,16},{16,0},{1,17},{17,1},{2,18},{18,2},{3,19},{19,3},{4,20},{20... | collective-permute-start | bytes 7077896 | tf_op jit(solution)/shard_map/ppermute | solution.py:106
  313.2 27.9 %collective-permute-start.5 = (bf16[384,768]{1,0:T(8,128)(2,1)}, bf16[384,768]{1,0:T(8,128)(2,1)}, u32[]{:S(2)}, u32[]{:S(2)}) collective-permute-start(bf16[384,768]{1,0:T(8,128)(2,1)} %get-tuple-element.178), channel_id=1, source_target_pairs={{0,2},{1,3},{2,0},{3,1},{4,6},{5,7},{6,4},{7,5},{8,10},{9,11},{10,... | collective-permute-start | bytes 1769480 | tf_op jit(solution)/shard_map/ppermute | solution.py:110
  313.2 27.9 %collective-permute-start.4 = (bf16[384,768]{1,0:T(8,128)(2,1)}, bf16[384,768]{1,0:T(8,128)(2,1)}, u32[]{:S(2)}, u32[]{:S(2)}) collective-permute-start(bf16[384,768]{1,0:T(8,128)(2,1)} %get-tuple-element.176), channel_id=1, source_target_pairs={{0,1},{1,2},{2,3},{3,0},{4,5},{5,6},{6,7},{7,4},{8,9},{9,10},{10,1... | collective-permute-start | bytes 1769480 | tf_op jit(solution)/shard_map/ppermute | solution.py:110
  410.2 29.2 %collective-permute-start.10 = (bf16[384,768]{1,0:T(8,128)(2,1)}, bf16[384,768]{1,0:T(8,128)(2,1)}, u32[]{:S(2)}, u32[]{:S(2)}) collective-permute-start(bf16[384,768]{1,0:T(8,128)(2,1)} %get-tuple-element.174), channel_id=1, source_target_pairs={{0,3},{1,0},{2,1},{3,2},{4,7},{5,4},{6,5},{7,6},{8,11},{9,8},{10,9... | collective-permute-start | bytes 1769480 | tf_op jit(solution)/shard_map/ppermute | solution.py:110
  413.1 27.2 %collective-permute-start.9 = (bf16[384,768]{1,0:T(8,128)(2,1)}, bf16[384,768]{1,0:T(8,128)(2,1)}, u32[]{:S(2)}, u32[]{:S(2)}) collective-permute-start(bf16[384,768]{1,0:T(8,128)(2,1)} %get-tuple-element.175), channel_id=1, source_target_pairs={{0,2},{1,3},{2,0},{3,1},{4,6},{5,7},{6,4},{7,5},{8,10},{9,11},{10,... | collective-permute-start | bytes 1769480 | tf_op jit(solution)/shard_map/ppermute | solution.py:110
  413.7 39.2 %collective-permute-start.8 = (bf16[384,768]{1,0:T(8,128)(2,1)}, bf16[384,768]{1,0:T(8,128)(2,1)}, u32[]{:S(2)}, u32[]{:S(2)}) collective-permute-start(bf16[384,768]{1,0:T(8,128)(2,1)} %get-tuple-element.173), channel_id=1, source_target_pairs={{0,1},{1,2},{2,3},{3,0},{4,5},{5,6},{6,7},{7,4},{8,9},{9,10},{10,1... | collective-permute-start | bytes 1769480 | tf_op jit(solution)/shard_map/ppermute | solution.py:110
  414.7 44.6 %collective-permute-start.35 = (bf16[384,768]{1,0:T(8,128)(2,1)S(1)}, bf16[384,768]{1,0:T(8,128)(2,1)S(1)}, u32[]{:S(2)}, u32[]{:S(2)}) collective-permute-start(bf16[384,768]{1,0:T(8,128)(2,1)S(1)} %copy-done.28), channel_id=1, source_target_pairs={{4,0},{5,1},{6,2},{7,3},{20,16},{21,17},{22,18},{23,19}} | collective-permute-start | bytes 1769480 | tf_op jit(solution)/shard_map/ppermute | solution.py:118
  427.6 33.0 %collective-permute-start.34 = (bf16[384,768]{1,0:T(8,128)(2,1)S(1)}, bf16[384,768]{1,0:T(8,128)(2,1)S(1)}, u32[]{:S(2)}, u32[]{:S(2)}) collective-permute-start(bf16[384,768]{1,0:T(8,128)(2,1)S(1)} %copy-done.28), channel_id=1, source_target_pairs={{8,0},{9,1},{10,2},{11,3},{24,16},{25,17},{26,18},{27,19}} | collective-permute-start | bytes 1769480 | tf_op jit(solution)/shard_map/ppermute | solution.py:118
  439.3 25.2 %collective-permute-start.23 = (bf16[384,768]{1,0:T(8,128)(2,1)S(1)}, bf16[384,768]{1,0:T(8,128)(2,1)S(1)}, u32[]{:S(2)}, u32[]{:S(2)}) collective-permute-start(bf16[384,768]{1,0:T(8,128)(2,1)S(1)} %get-tuple-element.168), channel_id=1, source_target_pairs={{0,3},{1,0},{2,1},{3,2},{4,7},{5,4},{6,5},{7,6},{8,11},{9,8},{10,9... | collective-permute-start | bytes 1769480 | tf_op jit(solution)/shard_map/ppermute | solution.py:110
  440.2 25.1 %collective-permute-start.22 = (bf16[384,768]{1,0:T(8,128)(2,1)S(1)}, bf16[384,768]{1,0:T(8,128)(2,1)S(1)}, u32[]{:S(2)}, u32[]{:S(2)}) collective-permute-start(bf16[384,768]{1,0:T(8,128)(2,1)S(1)} %get-tuple-element.169), channel_id=1, source_target_pairs={{0,2},{1,3},{2,0},{3,1},{4,6},{5,7},{6,4},{7,5},{8,10},{9,11},{10,... | collective-permute-start | bytes 1769480 | tf_op jit(solution)/shard_map/ppermute | solution.py:110
  452.9 22.1 %collective-permute-start.21 = (bf16[384,768]{1,0:T(8,128)(2,1)S(1)}, bf16[384,768]{1,0:T(8,128)(2,1)S(1)}, u32[]{:S(2)}, u32[]{:S(2)}) collective-permute-start(bf16[384,768]{1,0:T(8,128)(2,1)S(1)} %get-tuple-element.167), channel_id=1, source_target_pairs={{0,1},{1,2},{2,3},{3,0},{4,5},{5,6},{6,7},{7,4},{8,9},{9,10},{10,1... | collective-permute-start | bytes 1769480 | tf_op jit(solution)/shard_map/ppermute | solution.py:110
  459.3 26.4 %collective-permute-start.33 = (bf16[384,768]{1,0:T(8,128)(2,1)S(1)}, bf16[384,768]{1,0:T(8,128)(2,1)S(1)}, u32[]{:S(2)}, u32[]{:S(2)}) collective-permute-start(bf16[384,768]{1,0:T(8,128)(2,1)S(1)} %copy-done.28), channel_id=1, source_target_pairs={{12,0},{13,1},{14,2},{15,3},{28,16},{29,17},{30,18},{31,19}} | collective-permute-start | bytes 1769480 | tf_op jit(solution)/shard_map/ppermute | solution.py:118
  460.6 26.6 %collective-permute-start.32 = (bf16[384,768]{1,0:T(8,128)(2,1)S(1)}, bf16[384,768]{1,0:T(8,128)(2,1)S(1)}, u32[]{:S(2)}, u32[]{:S(2)}) collective-permute-start(bf16[384,768]{1,0:T(8,128)(2,1)S(1)} %fusion.183), channel_id=1, source_target_pairs={{12,8},{13,9},{14,10},{15,11},{28,24},{29,25},{30,26},{31,27}} | collective-permute-start | bytes 1769480 | tf_op jit(solution)/shard_map/ppermute | solution.py:118
  464.6 23.3 %collective-permute-start.13 = (bf16[384,768]{1,0:T(8,128)(2,1)S(1)}, bf16[384,768]{1,0:T(8,128)(2,1)S(1)}, u32[]{:S(2)}, u32[]{:S(2)}) collective-permute-start(bf16[384,768]{1,0:T(8,128)(2,1)S(1)} %fusion.189), channel_id=1, source_target_pairs={{8,4},{9,5},{10,6},{11,7},{24,20},{25,21},{26,22},{27,23}} | collective-permute-start | bytes 1769480 | tf_op jit(solution)/shard_map/ppermute | solution.py:118
  465.3 28.7 %collective-permute-start.12 = (bf16[384,768]{1,0:T(8,128)(2,1)S(1)}, bf16[384,768]{1,0:T(8,128)(2,1)S(1)}, u32[]{:S(2)}, u32[]{:S(2)}) collective-permute-start(bf16[384,768]{1,0:T(8,128)(2,1)S(1)} %fusion.189), channel_id=1, source_target_pairs={{12,4},{13,5},{14,6},{15,7},{28,20},{29,21},{30,22},{31,23}} | collective-permute-start | bytes 1769480 | tf_op jit(solution)/shard_map/ppermute | solution.py:118
  475.0 21.2 %collective-permute-start.11 = (bf16[384,768]{1,0:T(8,128)(2,1)S(1)}, bf16[384,768]{1,0:T(8,128)(2,1)S(1)}, u32[]{:S(2)}, u32[]{:S(2)}) collective-permute-start(bf16[384,768]{1,0:T(8,128)(2,1)S(1)} %fusion.189), channel_id=1, source_target_pairs={{0,4},{1,5},{2,6},{3,7},{16,20},{17,21},{18,22},{19,23}} | collective-permute-start | bytes 1769480 | tf_op jit(solution)/shard_map/ppermute | solution.py:118
  485.7 23.2 %collective-permute-start.31 = (bf16[384,768]{1,0:T(8,128)(2,1)S(1)}, bf16[384,768]{1,0:T(8,128)(2,1)S(1)}, u32[]{:S(2)}, u32[]{:S(2)}) collective-permute-start(bf16[384,768]{1,0:T(8,128)(2,1)S(1)} %fusion.183), channel_id=1, source_target_pairs={{0,8},{1,9},{2,10},{3,11},{16,24},{17,25},{18,26},{19,27}} | collective-permute-start | bytes 1769480 | tf_op jit(solution)/shard_map/ppermute | solution.py:118
  487.2 21.7 %collective-permute-start.30 = (bf16[384,768]{1,0:T(8,128)(2,1)S(1)}, bf16[384,768]{1,0:T(8,128)(2,1)S(1)}, u32[]{:S(2)}, u32[]{:S(2)}) collective-permute-start(bf16[384,768]{1,0:T(8,128)(2,1)S(1)} %fusion.183), channel_id=1, source_target_pairs={{4,8},{5,9},{6,10},{7,11},{20,24},{21,25},{22,26},{23,27}} | collective-permute-start | bytes 1769480 | tf_op jit(solution)/shard_map/ppermute | solution.py:118
  487.9 28.8 %collective-permute-start.26 = (bf16[384,768]{1,0:T(8,128)(2,1)S(1)}, bf16[384,768]{1,0:T(8,128)(2,1)S(1)}, u32[]{:S(2)}, u32[]{:S(2)}) collective-permute-start(bf16[384,768]{1,0:T(8,128)(2,1)S(1)} %fusion.186), channel_id=1, source_target_pairs={{0,12},{1,13},{2,14},{3,15},{16,28},{17,29},{18,30},{19,31}} | collective-permute-start | bytes 1769480 | tf_op jit(solution)/shard_map/ppermute | solution.py:118
  494.1 22.6 %collective-permute-start.25 = (bf16[384,768]{1,0:T(8,128)(2,1)S(1)}, bf16[384,768]{1,0:T(8,128)(2,1)S(1)}, u32[]{:S(2)}, u32[]{:S(2)}) collective-permute-start(bf16[384,768]{1,0:T(8,128)(2,1)S(1)} %fusion.186), channel_id=1, source_target_pairs={{4,12},{5,13},{6,14},{7,15},{20,28},{21,29},{22,30},{23,31}} | collective-permute-start | bytes 1769480 | tf_op jit(solution)/shard_map/ppermute | solution.py:118
  (95 other events, 849.7 us)
Sparse Core Ops, SparseCore 0:
  10.9 126.8 all-gather.2

commit v6 on v5

--- a/solution.py
+++ b/solution.py
@@ -51,11 +51,6 @@
 
 def dot32(spec, left, right):
     return jnp.einsum(spec, left, right, preferred_element_type=full_type)
-
-
-def two_parts(values):
-    high = lax.reduce_precision(values, 8, 7)
-    return high.astype(low_type), (values - high).astype(low_type)
 
 
 def shards(
@@ -288,15 +283,12 @@
     fix_one = 1.0 - jnp.power(beta_one, step_value)
     fix_two = 1.0 - jnp.power(beta_two, step_value)
     turned = dot32("ji,jl->il", left_low, tile_sum)
-    high, rest = two_parts(turned)
-    rotated = dot32("il,lm->im", high, right_low) + dot32("il,lm->im", rest, right_low)
+    rotated = dot32("il,lm->im", turned.astype(low_type), right_low)
     mean_one = beta_one * moment_one_low.astype(full_type) + (1.0 - beta_one) * rotated
     mean_two = beta_two * moment_two_low.astype(full_type) + (1.0 - beta_two) * rotated * rotated
     direction = mean_one / fix_one / (jnp.sqrt(mean_two / fix_two) + adam_eps)
-    high, rest = two_parts(direction)
-    turned = dot32("ij,jl->il", left_low, high) + dot32("ij,jl->il", left_low, rest)
-    high, rest = two_parts(turned)
-    update = dot32("il,ml->im", high, right_low) + dot32("il,ml->im", rest, right_low)
+    turned = dot32("ij,jl->il", left_low, direction.astype(low_type))
+    update = dot32("il,ml->im", turned.astype(low_type), right_low)
     results = jnp.stack([rotated, update]).reshape(2, owners, replicas, part, width)
     results = pick(results, my_copy, 2).astype(low_type).transpose(1, 0, 2, 3)
     returned = lax.all_to_all(results, "zero", split_axis=0, concat_axis=0, tiled=True)

time: 619 us -> 626 us (1.011)
    dot_general x43 -> x39, matrix products: 144 us -> 147 us  [dot32(): return jnp.einsum(spec, left, right, preferred_element_type=full_type)]
    unnamed x162 -> x166, local copies, waits for them, and re-layouts: 31.8 us -> 31.9 us
  transfers between devices with their start and end apart: 40 -> 40, of which waited for: 15 -> 14; matrix products, arithmetic and copies ran while one was open for 21% -> 21% of each run, Pallas kernels for 0% -> 0%
where the time goes in v6:
time: 626 us; the launch traced here: 619 us
  waiting for transfers between devices  151 us (24%)
  matrix products  147 us (23%)
  blocking collectives  103 us (16%)
  local copies, waits for them, and re-layouts  83.7 us (13%)
  other arithmetic  59.3 us (9%)
  starting transfers between devices  57.5 us (9%)
  between operations  16.6 us (3%)
    dot_general x39, matrix products, dot32(): return jnp.einsum(spec, left, right, preferred_element_type=full_type)  147 us
    ppermute x15, waiting for transfers between devices, from_spots(): return lax.ppermute(values, 'zero', pairs)  64.9 us
    all_gather x1, waiting for transfers between devices, shards(): whole = lax.all_gather(sent, ('zero', 'dp'), axis=1, tiled=True)  60.8 us
    all_to_all x1, blocking collectives, shards(): lax.all_to_all(results, 'zero', split_axis=0, concat_axis=0, tiled=True)  59.4 us
    all_gather x1, blocking collectives, shards(): lax.all_gather(norm_params.astype(low_type), 'zero', axis=1, tiled=True)  43.9 us
    unnamed x166, local copies, waits for them, and re-layouts  31.9 us
    ppermute x12, starting transfers between devices, from_line(): return lax.ppermute(values, 'zero', pairs)  23.3 us
    ppermute x15, starting transfers between devices, from_spots(): return lax.ppermute(values, 'zero', pairs)  17.4 us
  transfers between devices with their start and end apart: 40, of which 14 were waited for; matrix products, arithmetic and copies ran while one was open for 21% of the time, Pallas kernels for 0%

profile of v6, /device:TPU:0, one launch (start us, length us, event | category | flops | bytes accessed | tf_op | source)
XLA Modules:
  0.0 618.9 jit_solution(17233177422721220098)
XLA Ops:
  17.9 9.2 %gather_fusion = bf16[1024,768]{1,0:T(8,128)(2,1)} fusion(bf16[4096,768]{1,0:T(8,128)(2,1)} %param.19, s32[1024]{0:T(1024)S(1)} %broadcast_clamp_fusion), kind=kCustom, calls=%fused_computation | custom fusion | bytes 3149824 | tf_op jit(solution)/shard_map/jit(_take)/gather | solution.py:177
  29.8 43.9 %all-gather = bf16[16,48,4]{1,2,0:T(4,128)(2,1)S(1)} all-gather(bf16[1,48,4]{1,2,0:T(4,128)(2,1)S(1)} %convert_bitcast_fusion), channel_id=1, replica_groups=mesh['dp'=2,'zero'=16] {'zero'}, dimensions={0}, use_global_device_ids=true | all-gather | bytes 6528 | tf_op jit(solution)/shard_map/all_gather | solution.py:90
  77.0 60.8 %all-gather.3.cloned.1.call-done = bf16[16,768,768]{2,1,0:T(8,128)(2,1)} async-done(((bf16[16,24,768]{2,1,0:T(8,128)(2,1)}), bf16[16,768,768]{2,1,0:T(8,128)(2,1)}) %all-gather.3.cloned.1.call-update) | async-done | bytes 18874384 | tf_op jit(solution)/shard_map/all_gather | solution.py:89
  178.7 10.9 %fusion.23 = f32[1024,4,768]{2,0,1:T(8,128)} fusion(bf16[16,768,768]{2,1,0:T(8,128)(2,1)} %all-gather.3.cloned.1.call-done, bf16[1024,768]{0,1:T(8,128)(2,1)S(1)} %fusion.31), kind=kOutput, calls=%fused_computation.48 | convolution fusion | flops 4831838208 | bytes 18874368 | tf_op jit(solution)/shard_map/td,fde->tfe/dot_general | solution.py:53
  189.6 19.8 %multiply_convert_fusion.2 = (bf16[1024,4,768]{2,0,1:T(8,128)(2,1)S(1)}, f32[1024,4,768]{2,0,1:T(8,128)}, f32[1024,4,768]{2,0,1:T(8,128)}) fusion(f32[1024,4,768]{2,0,1:T(8,128)} %fusion.23, bf16[16,768,768]{2,1,0:T(8,128)(2,1)} %all-gather.3.cloned.1.call-done, bf16[1024,768]{0,1:T(8,128)(2,1)S(1)} %fusion.31), kind=kOutput, calls=%fused_computation.9 | convolution fusion | flops 4869586944 | bytes 50331648 | tf_op jit(solution)/shard_map/td,fde->tfe/dot_general | solution.py:53
  212.0 9.6 %fusion.47 = f32[1024,768]{1,0:T(8,128)} fusion(bf16[1024,4,768]{2,0,1:T(8,128)(2,1)S(1)} %get-tuple-element.45, bf16[16,768,768]{2,1,0:T(8,128)(2,1)} %all-gather.3.cloned.1.call-done), kind=kOutput, calls=%fused_computation.102 | convolution fusion | flops 4831838208 | bytes 14155776 | tf_op jit(solution)/shard_map/tfe,fed->td/dot_general | solution.py:53
  253.3 15.7 %multiply_convert_fusion = (bf16[1024,4,768]{2,0,1:T(8,128)(2,1)}, bf16[1024,4,768]{2,0,1:T(8,128)(2,1)}) fusion(f32[1024,4,768]{2,0,1:T(8,128)} %get-tuple-element.50, f32[1024,4,768]{2,0,1:T(8,128)} %get-tuple-element.49, bf16[16,768,768]{2,1,0:T(8,128)(2,1)} %all-gather.3.cloned.1.call-done, bf16[1024,768]{0,1:T(8,128)(2,1)} %copy-done.26), kind=kOutput, calls=%fused_computation.7 | convolution fusion | flops 4844421120 | bytes 44040192 | tf_op jit(solution)/shard_map/td,fed->tfe/dot_general | solution.py:53
  289.0 8.1 %fusion.17 = f32[1024,768,1]{0,1,2:T(8,128)} fusion(bf16[1024,4,768]{2,0,1:T(8,128)(2,1)S(1)} %bitcast.354, bf16[16,768,768]{2,1,0:T(8,128)(2,1)} %all-gather.3.cloned.1.call-done), kind=kOutput, calls=%fused_computation.42 | convolution fusion | flops 4831838208 | bytes 14155776 | tf_op jit(solution)/shard_map/tfe,fde->td/dot_general | solution.py:53
  308.0 5.5 collective-permute-start.6
  314.1 7.9 %bitcast_add_fusion = f32[1024,768]{0,1:T(8,128)S(1)} fusion(f32[1024,768,1]{0,1,2:T(8,128)} %fusion.17, bf16[1024,4,768]{2,0,1:T(8,128)(2,1)S(1)} %bitcast.352, bf16[16,768,768]{2,1,0:T(8,128)(2,1)} %all-gather.3.cloned.1.call-done, f32[1024]{0:T(1024)S(1)} %get-tuple-element.212, f32[1024,768]{0,1:T(8,128)S(1)} %copy-done.2, ...), kind=kOutput, calls=%fused_computation.57 | convolution fusion | flops 4839702528 | bytes 22039552 | tf_op jit(solution)/shard_map/tfe,fde->td/dot_general | solution.py:53
  322.1 5.5 collective-permute-done.6
  327.6 13.8 %collective-permute-done.5 = bf16[384,768]{1,0:T(8,128)(2,1)} collective-permute-done((bf16[384,768]{1,0:T(8,128)(2,1)}, bf16[384,768]{1,0:T(8,128)(2,1)}, u32[]{:S(2)}, u32[]{:S(2)}) %collective-permute-start.5) | collective-permute-done | bytes 589856 | tf_op jit(solution)/shard_map/ppermute | solution.py:105
  362.5 5.3 fusion.152
  396.4 6.6 %collective-permute-start.19 = (f32[4,768]{1,0:T(4,128)S(1)}, f32[4,768]{1,0:T(4,128)S(1)}, u32[]{:S(2)}, u32[]{:S(2)}) collective-permute-start(f32[4,768]{1,0:T(4,128)S(1)} %add_add_fusion), channel_id=1, source_target_pairs={{0,8},{1,9},{2,10},{3,11},{4,12},{5,13},{6,14},{7,15},{8,0},{9,1},... | collective-permute-start | bytes 36872 | tf_op jit(solution)/shard_map/ppermute | solution.py:109
  416.4 11.4 %collective-permute-done.27 = bf16[384,768]{1,0:T(8,128)(2,1)} collective-permute-done((bf16[384,768]{1,0:T(8,128)(2,1)}, bf16[384,768]{1,0:T(8,128)(2,1)}, u32[]{:S(2)}, u32[]{:S(2)}) %collective-permute-start.27) | collective-permute-done | bytes 589856 | tf_op jit(solution)/shard_map/ppermute | solution.py:105
  429.2 10.5 %collective-permute-done.10 = bf16[384,768]{1,0:T(8,128)(2,1)} collective-permute-done((bf16[384,768]{1,0:T(8,128)(2,1)}, bf16[384,768]{1,0:T(8,128)(2,1)}, u32[]{:S(2)}, u32[]{:S(2)}) %collective-permute-start.10) | collective-permute-done | bytes 589856 | tf_op jit(solution)/shard_map/ppermute | solution.py:105
  441.9 11.3 %collective-permute-done.8 = bf16[384,768]{1,0:T(8,128)(2,1)} collective-permute-done((bf16[384,768]{1,0:T(8,128)(2,1)}, bf16[384,768]{1,0:T(8,128)(2,1)}, u32[]{:S(2)}, u32[]{:S(2)}) %collective-permute-start.8) | collective-permute-done | bytes 589856 | tf_op jit(solution)/shard_map/ppermute | solution.py:105
  466.3 9.0 %collective-permute-done.21 = bf16[384,768]{1,0:T(8,128)(2,1)S(1)} collective-permute-done((bf16[384,768]{1,0:T(8,128)(2,1)S(1)}, bf16[384,768]{1,0:T(8,128)(2,1)S(1)}, u32[]{:S(2)}, u32[]{:S(2)}) %collective-permute-start.21) | collective-permute-done | bytes 589856 | tf_op jit(solution)/shard_map/ppermute | solution.py:105
  475.3 7.5 %collective-permute-start.11 = (bf16[384,768]{1,0:T(8,128)(2,1)S(1)}, bf16[384,768]{1,0:T(8,128)(2,1)S(1)}, u32[]{:S(2)}, u32[]{:S(2)}) collective-permute-start(bf16[384,768]{1,0:T(8,128)(2,1)S(1)} %fusion.182), channel_id=1, source_target_pairs={{0,4},{1,5},{2,6},{3,7},{16,20},{17,21},{18,22},{19,23}} | collective-permute-start | bytes 1769480 | tf_op jit(solution)/shard_map/ppermute | solution.py:113
  488.2 6.2 collective-permute-start.26
  501.1 8.0 %collective-permute-done.31 = bf16[384,768]{1,0:T(8,128)(2,1)S(1)} collective-permute-done((bf16[384,768]{1,0:T(8,128)(2,1)S(1)}, bf16[384,768]{1,0:T(8,128)(2,1)S(1)}, u32[]{:S(2)}, u32[]{:S(2)}) %collective-permute-start.31) | collective-permute-done | bytes 589856 | tf_op jit(solution)/shard_map/ppermute | solution.py:113
  509.2 7.8 %collective-permute-done.26 = bf16[384,768]{1,0:T(8,128)(2,1)S(1)} collective-permute-done((bf16[384,768]{1,0:T(8,128)(2,1)S(1)}, bf16[384,768]{1,0:T(8,128)(2,1)S(1)}, u32[]{:S(2)}, u32[]{:S(2)}) %collective-permute-start.26) | collective-permute-done | bytes 589856 | tf_op jit(solution)/shard_map/ppermute | solution.py:113
  523.8 7.8 %fusion.44 = (bf16[768,768]{1,0:T(8,128)(2,1)}, bf16[768,768]{1,0:T(8,128)(2,1)}) fusion(f32[1,16,2,24,768]{4,3,2,1,0:T(8,128)} %get-tuple-element.149, f32[1,16,2,24,768]{4,3,2,1,0:T(8,128)} %get-tuple-element.148, f32[]{:T(128)} %bitcast.82, f32[]{:T(128)} %bitcast.80, bf16[768,768]{1,0:T(8,128)(2,1)} %bitcast.392, bf16[768,768]{1,0:T(8,128)(2,1)} %bitcast.394, ...), kind=kOutput, calls=%fused_computation.101 | convolution fusion | flops 1819017216 | bytes 10616840 | tf_op jit(solution)/shard_map/il,lm->im/dot_general | solution.py:53
  535.9 59.4 %all_to_all.10 = bf16[16,2,24,768]{3,2,1,0:T(8,128)(2,1)S(1)} all-to-all(bf16[16,2,24,768]{3,2,1,0:T(8,128)(2,1)S(1)} %copy.209), channel_id=1, replica_groups=mesh['dp'=2,'zero'=16] {'zero'}, dimensions={0} | all-to-all | bytes 2359296 | tf_op jit(solution)/shard_map/all_to_all | solution.py:294
  (375 shorter events, 240.7 us)
Async XLA Ops:
  7.2 130.7 %all-gather.3.cloned.1.call-start = ((), (), s32[]{:S(2)}) async-start(), calls=%async_computation.2 | async-start | bytes 19464192 | tf_op jit(solution)/shard_map/all_gather | solution.py:89
  173.6 52.2 %all-to-all-start = ((bf16[16,4,24,768]{3,2,1,0:T(8,128)(2,1)}), bf16[16,4,24,768]{3,2,1,0:T(8,128)(2,1)}, u32[]{:S(2)}, u32[]{:S(2)}) async-start(bf16[16,4,24,768]{3,2,1,0:T(8,128)(2,1)} %pad_maximum_fusion.1), calls=%async_computation | async-start | bytes 4718592 | tf_op jit(solution)/shard_map/all_to_all | solution.py:181
  252.8 21.9 %collective-permute-start = (bf16[4,384,768]{2,1,0:T(8,128)(2,1)}, bf16[4,384,768]{2,1,0:T(8,128)(2,1)}, u32[]{:S(2)}, u32[]{:S(2)}) collective-permute-start(bf16[4,384,768]{2,1,0:T(8,128)(2,1)} %pad_maximum_fusion.2), channel_id=1, source_target_pairs={{0,16},{16,0},{1,17},{17,1},{2,18},{18,2},{3,19},{19,3},{4,20},{20... | collective-permute-start | bytes 7077896 | tf_op jit(solution)/shard_map/ppermute | solution.py:101
  300.9 43.1 %collective-permute-start.2 = (bf16[4,384,768]{2,1,0:T(8,128)(2,1)}, bf16[4,384,768]{2,1,0:T(8,128)(2,1)S(1)}, u32[]{:S(2)}, u32[]{:S(2)}) collective-permute-start(bf16[4,384,768]{2,1,0:T(8,128)(2,1)} %pad_maximum_fusion.3), channel_id=1, source_target_pairs={{0,16},{16,0},{1,17},{17,1},{2,18},{18,2},{3,19},{19,3},{4,20},{20... | collective-permute-start | bytes 7077896 | tf_op jit(solution)/shard_map/ppermute | solution.py:101
  306.2 39.5 %collective-permute-start.3 = (bf16[4,384,768]{2,1,0:T(8,128)(2,1)}, bf16[4,384,768]{2,1,0:T(8,128)(2,1)}, u32[]{:S(2)}, u32[]{:S(2)}) collective-permute-start(bf16[4,384,768]{2,1,0:T(8,128)(2,1)} %pad_maximum_fusion.4), channel_id=1, source_target_pairs={{0,16},{16,0},{1,17},{17,1},{2,18},{18,2},{3,19},{19,3},{4,20},{20... | collective-permute-start | bytes 7077896 | tf_op jit(solution)/shard_map/ppermute | solution.py:101
  313.5 27.9 %collective-permute-start.5 = (bf16[384,768]{1,0:T(8,128)(2,1)}, bf16[384,768]{1,0:T(8,128)(2,1)}, u32[]{:S(2)}, u32[]{:S(2)}) collective-permute-start(bf16[384,768]{1,0:T(8,128)(2,1)} %get-tuple-element.169), channel_id=1, source_target_pairs={{0,2},{1,3},{2,0},{3,1},{4,6},{5,7},{6,4},{7,5},{8,10},{9,11},{10,... | collective-permute-start | bytes 1769480 | tf_op jit(solution)/shard_map/ppermute | solution.py:105
  313.5 27.9 %collective-permute-start.4 = (bf16[384,768]{1,0:T(8,128)(2,1)}, bf16[384,768]{1,0:T(8,128)(2,1)}, u32[]{:S(2)}, u32[]{:S(2)}) collective-permute-start(bf16[384,768]{1,0:T(8,128)(2,1)} %get-tuple-element.167), channel_id=1, source_target_pairs={{0,1},{1,2},{2,3},{3,0},{4,5},{5,6},{6,7},{7,4},{8,9},{9,10},{10,1... | collective-permute-start | bytes 1769480 | tf_op jit(solution)/shard_map/ppermute | solution.py:105
  410.5 29.2 %collective-permute-start.10 = (bf16[384,768]{1,0:T(8,128)(2,1)}, bf16[384,768]{1,0:T(8,128)(2,1)}, u32[]{:S(2)}, u32[]{:S(2)}) collective-permute-start(bf16[384,768]{1,0:T(8,128)(2,1)} %get-tuple-element.165), channel_id=1, source_target_pairs={{0,3},{1,0},{2,1},{3,2},{4,7},{5,4},{6,5},{7,6},{8,11},{9,8},{10,9... | collective-permute-start | bytes 1769480 | tf_op jit(solution)/shard_map/ppermute | solution.py:105
  413.4 27.2 %collective-permute-start.9 = (bf16[384,768]{1,0:T(8,128)(2,1)}, bf16[384,768]{1,0:T(8,128)(2,1)}, u32[]{:S(2)}, u32[]{:S(2)}) collective-permute-start(bf16[384,768]{1,0:T(8,128)(2,1)} %get-tuple-element.166), channel_id=1, source_target_pairs={{0,2},{1,3},{2,0},{3,1},{4,6},{5,7},{6,4},{7,5},{8,10},{9,11},{10,... | collective-permute-start | bytes 1769480 | tf_op jit(solution)/shard_map/ppermute | solution.py:105
  414.0 39.2 %collective-permute-start.8 = (bf16[384,768]{1,0:T(8,128)(2,1)}, bf16[384,768]{1,0:T(8,128)(2,1)}, u32[]{:S(2)}, u32[]{:S(2)}) collective-permute-start(bf16[384,768]{1,0:T(8,128)(2,1)} %get-tuple-element.164), channel_id=1, source_target_pairs={{0,1},{1,2},{2,3},{3,0},{4,5},{5,6},{6,7},{7,4},{8,9},{9,10},{10,1... | collective-permute-start | bytes 1769480 | tf_op jit(solution)/shard_map/ppermute | solution.py:105
  415.0 44.6 %collective-permute-start.35 = (bf16[384,768]{1,0:T(8,128)(2,1)S(1)}, bf16[384,768]{1,0:T(8,128)(2,1)S(1)}, u32[]{:S(2)}, u32[]{:S(2)}) collective-permute-start(bf16[384,768]{1,0:T(8,128)(2,1)S(1)} %copy-done.28), channel_id=1, source_target_pairs={{4,0},{5,1},{6,2},{7,3},{20,16},{21,17},{22,18},{23,19}} | collective-permute-start | bytes 1769480 | tf_op jit(solution)/shard_map/ppermute | solution.py:113
  427.9 33.0 %collective-permute-start.34 = (bf16[384,768]{1,0:T(8,128)(2,1)S(1)}, bf16[384,768]{1,0:T(8,128)(2,1)S(1)}, u32[]{:S(2)}, u32[]{:S(2)}) collective-permute-start(bf16[384,768]{1,0:T(8,128)(2,1)S(1)} %copy-done.28), channel_id=1, source_target_pairs={{8,0},{9,1},{10,2},{11,3},{24,16},{25,17},{26,18},{27,19}} | collective-permute-start | bytes 1769480 | tf_op jit(solution)/shard_map/ppermute | solution.py:113
  439.6 25.2 %collective-permute-start.23 = (bf16[384,768]{1,0:T(8,128)(2,1)S(1)}, bf16[384,768]{1,0:T(8,128)(2,1)S(1)}, u32[]{:S(2)}, u32[]{:S(2)}) collective-permute-start(bf16[384,768]{1,0:T(8,128)(2,1)S(1)} %get-tuple-element.159), channel_id=1, source_target_pairs={{0,3},{1,0},{2,1},{3,2},{4,7},{5,4},{6,5},{7,6},{8,11},{9,8},{10,9... | collective-permute-start | bytes 1769480 | tf_op jit(solution)/shard_map/ppermute | solution.py:105
  440.5 25.1 %collective-permute-start.22 = (bf16[384,768]{1,0:T(8,128)(2,1)S(1)}, bf16[384,768]{1,0:T(8,128)(2,1)S(1)}, u32[]{:S(2)}, u32[]{:S(2)}) collective-permute-start(bf16[384,768]{1,0:T(8,128)(2,1)S(1)} %get-tuple-element.160), channel_id=1, source_target_pairs={{0,2},{1,3},{2,0},{3,1},{4,6},{5,7},{6,4},{7,5},{8,10},{9,11},{10,... | collective-permute-start | bytes 1769480 | tf_op jit(solution)/shard_map/ppermute | solution.py:105
  453.2 22.1 %collective-permute-start.21 = (bf16[384,768]{1,0:T(8,128)(2,1)S(1)}, bf16[384,768]{1,0:T(8,128)(2,1)S(1)}, u32[]{:S(2)}, u32[]{:S(2)}) collective-permute-start(bf16[384,768]{1,0:T(8,128)(2,1)S(1)} %get-tuple-element.158), channel_id=1, source_target_pairs={{0,1},{1,2},{2,3},{3,0},{4,5},{5,6},{6,7},{7,4},{8,9},{9,10},{10,1... | collective-permute-start | bytes 1769480 | tf_op jit(solution)/shard_map/ppermute | solution.py:105
  459.6 26.4 %collective-permute-start.33 = (bf16[384,768]{1,0:T(8,128)(2,1)S(1)}, bf16[384,768]{1,0:T(8,128)(2,1)S(1)}, u32[]{:S(2)}, u32[]{:S(2)}) collective-permute-start(bf16[384,768]{1,0:T(8,128)(2,1)S(1)} %copy-done.28), channel_id=1, source_target_pairs={{12,0},{13,1},{14,2},{15,3},{28,16},{29,17},{30,18},{31,19}} | collective-permute-start | bytes 1769480 | tf_op jit(solution)/shard_map/ppermute | solution.py:113
  460.9 26.6 %collective-permute-start.32 = (bf16[384,768]{1,0:T(8,128)(2,1)S(1)}, bf16[384,768]{1,0:T(8,128)(2,1)S(1)}, u32[]{:S(2)}, u32[]{:S(2)}) collective-permute-start(bf16[384,768]{1,0:T(8,128)(2,1)S(1)} %fusion.176), channel_id=1, source_target_pairs={{12,8},{13,9},{14,10},{15,11},{28,24},{29,25},{30,26},{31,27}} | collective-permute-start | bytes 1769480 | tf_op jit(solution)/shard_map/ppermute | solution.py:113
  464.9 23.3 %collective-permute-start.13 = (bf16[384,768]{1,0:T(8,128)(2,1)S(1)}, bf16[384,768]{1,0:T(8,128)(2,1)S(1)}, u32[]{:S(2)}, u32[]{:S(2)}) collective-permute-start(bf16[384,768]{1,0:T(8,128)(2,1)S(1)} %fusion.182), channel_id=1, source_target_pairs={{8,4},{9,5},{10,6},{11,7},{24,20},{25,21},{26,22},{27,23}} | collective-permute-start | bytes 1769480 | tf_op jit(solution)/shard_map/ppermute | solution.py:113
  465.6 28.7 %collective-permute-start.12 = (bf16[384,768]{1,0:T(8,128)(2,1)S(1)}, bf16[384,768]{1,0:T(8,128)(2,1)S(1)}, u32[]{:S(2)}, u32[]{:S(2)}) collective-permute-start(bf16[384,768]{1,0:T(8,128)(2,1)S(1)} %fusion.182), channel_id=1, source_target_pairs={{12,4},{13,5},{14,6},{15,7},{28,20},{29,21},{30,22},{31,23}} | collective-permute-start | bytes 1769480 | tf_op jit(solution)/shard_map/ppermute | solution.py:113
  475.3 21.2 %collective-permute-start.11 = (bf16[384,768]{1,0:T(8,128)(2,1)S(1)}, bf16[384,768]{1,0:T(8,128)(2,1)S(1)}, u32[]{:S(2)}, u32[]{:S(2)}) collective-permute-start(bf16[384,768]{1,0:T(8,128)(2,1)S(1)} %fusion.182), channel_id=1, source_target_pairs={{0,4},{1,5},{2,6},{3,7},{16,20},{17,21},{18,22},{19,23}} | collective-permute-start | bytes 1769480 | tf_op jit(solution)/shard_map/ppermute | solution.py:113
  486.0 23.2 %collective-permute-start.31 = (bf16[384,768]{1,0:T(8,128)(2,1)S(1)}, bf16[384,768]{1,0:T(8,128)(2,1)S(1)}, u32[]{:S(2)}, u32[]{:S(2)}) collective-permute-start(bf16[384,768]{1,0:T(8,128)(2,1)S(1)} %fusion.176), channel_id=1, source_target_pairs={{0,8},{1,9},{2,10},{3,11},{16,24},{17,25},{18,26},{19,27}} | collective-permute-start | bytes 1769480 | tf_op jit(solution)/shard_map/ppermute | solution.py:113
  487.5 21.7 %collective-permute-start.30 = (bf16[384,768]{1,0:T(8,128)(2,1)S(1)}, bf16[384,768]{1,0:T(8,128)(2,1)S(1)}, u32[]{:S(2)}, u32[]{:S(2)}) collective-permute-start(bf16[384,768]{1,0:T(8,128)(2,1)S(1)} %fusion.176), channel_id=1, source_target_pairs={{4,8},{5,9},{6,10},{7,11},{20,24},{21,25},{22,26},{23,27}} | collective-permute-start | bytes 1769480 | tf_op jit(solution)/shard_map/ppermute | solution.py:113
  488.2 28.8 %collective-permute-start.26 = (bf16[384,768]{1,0:T(8,128)(2,1)S(1)}, bf16[384,768]{1,0:T(8,128)(2,1)S(1)}, u32[]{:S(2)}, u32[]{:S(2)}) collective-permute-start(bf16[384,768]{1,0:T(8,128)(2,1)S(1)} %fusion.179), channel_id=1, source_target_pairs={{0,12},{1,13},{2,14},{3,15},{16,28},{17,29},{18,30},{19,31}} | collective-permute-start | bytes 1769480 | tf_op jit(solution)/shard_map/ppermute | solution.py:113
  494.4 22.6 %collective-permute-start.25 = (bf16[384,768]{1,0:T(8,128)(2,1)S(1)}, bf16[384,768]{1,0:T(8,128)(2,1)S(1)}, u32[]{:S(2)}, u32[]{:S(2)}) collective-permute-start(bf16[384,768]{1,0:T(8,128)(2,1)S(1)} %fusion.179), channel_id=1, source_target_pairs={{4,12},{5,13},{6,14},{7,15},{20,28},{21,29},{22,30},{23,31}} | collective-permute-start | bytes 1769480 | tf_op jit(solution)/shard_map/ppermute | solution.py:113
  (97 other events, 857.3 us)
Sparse Core Ops, SparseCore 0:
  10.9 126.8 all-gather.2
